TPU v7x, 256 devices: a whole 4x4x8 slice. The times are simulated.
256 devices in a mesh: layer: 8 (over z), row: 16 (over y, x), col: 2 (over core).
Axes of the slice: x: 4, y: 4, z: 8, core: 2. Of those that a mesh axis runs over, the one named last changes fastest.
Arguments:
- leaf_rhs: float32 [8, 3, 4096, 256], P('layer', None, 'row'), may hold values from -6 to 6
- anc_rhs: float32 [2, 4096, 256], P(None, 'row'), may hold values from -6 to 6
- leaf_tiles: bfloat16 [8, 3, 4096, 4096], P('layer', None, 'row', 'col'), may hold values from -0.09375 to 0.09375
- cross_tiles: bfloat16 [8, 2, 3, 4096, 4096], P('layer', None, None, 'row', 'col'), may hold values from -0.03125 to 0.03125
- top_tiles: bfloat16 [1, 4096, 4096], P(None, 'row', 'col'), may hold values from -0.09375 to 0.09375
- leaf_pattern: int32 [8, 3, 32, 32], P('layer', None, 'row', 'col'), may hold values 0 or 1
- cross_pattern: int32 [8, 2, 3, 32, 32], P('layer', None, None, 'row', 'col'), may hold values 0 or 1
- top_pattern: int32 [1, 32, 32], P(None, 'row', 'col'), may hold values 0 or 1
- leaf_inverse: bfloat16 [8, 3, 32, 128, 128], P('layer'), may hold values from -0.5 to 0.5
- anc_inverse: bfloat16 [2, 32, 128, 128], replicated, may hold values from -0.5 to 0.5
Outputs:
- leaf_solution: bfloat16 [8, 3, 4096, 256], P('layer', None, 'row')
- anc_solution: bfloat16 [2, 4096, 256], P(None, 'row')
All inputs are finite; a program needn't handle non-finite values. No bound on the sum of `leaf_pattern` or of `cross_pattern` or of `top_pattern` on one device may be relied on, other than what follows from the above.
Results may differ from a plain program's by a relative error of at most 0.023.
Values may be sent and summed in bfloat16 or wider, within the bound.
No kernel may reach another device: no remote copies, remote signals or barrier semaphores. Data moves between devices by JAX's collectives and lax.ppermute only.
A program may use at most 128 MiB of HBM per device.

v0:
```python
import jax
import jax.numpy as jnp
from jax import lax
from jax.sharding import PartitionSpec as P


def copy_for_each(x, axis):
    copies = jnp.broadcast_to(x, (lax.axis_size(axis), *x.shape))
    return lax.all_to_all(copies, axis, split_axis=0, concat_axis=0, tiled=True)


def of_everyone(x, axis):
    everything = copy_for_each(x, axis)
    return jnp.sum(everything.astype(jnp.float32), axis=0)


def laid_out(pieces, dim):
    shape = list(pieces.shape[1:])
    shape[dim] *= pieces.shape[0]
    return jnp.moveaxis(pieces, 0, dim).reshape(shape)


def gathered_copies(x, axis, dim):
    return laid_out(copy_for_each(x, axis), dim)


def padded_to(lines, peers):
    spare = -lines.shape[0] % peers
    if not spare:
        return lines
    return jnp.concatenate([lines, jnp.zeros((spare, *lines.shape[1:]), lines.dtype)])


def whole_of(x, axes, dim):
    far, near = axes
    pieces = copy_for_each(copy_for_each(x, far), near)
    return laid_out(pieces.swapaxes(0, 1).reshape(-1, *x.shape), dim)


def in_blocks(x, dim, peers):
    before, after = (x.shape[:dim], x.shape[dim + 1 :])
    return jnp.moveaxis(x.reshape(*before, peers, -1, *after), dim, 0)


def sent_and_summed(x, axis, dim):
    peers = lax.axis_size(axis)
    pieces = lax.all_to_all(in_blocks(x, dim, peers), axis, 0, 0, tiled=True)
    return jnp.sum(pieces.astype(jnp.float32), axis=0)


def sum_by_axis(x, axes, dim):
    far, near = axes
    own = sent_and_summed(in_blocks(x, dim, lax.axis_size(far)), near, dim + 1)
    return jnp.sum(
        lax.all_to_all(own.astype(jnp.bfloat16), far, 0, 0, tiled=True).astype(jnp.float32), axis=0
    )


def sum_by_parts(x, axes):
    lines = x.reshape(-1, x.shape[-1])
    padded = padded_to(lines, lax.axis_size(axes[0]) * lax.axis_size(axes[1]))
    whole = whole_of(sum_by_axis(padded, axes, 0).astype(jnp.bfloat16), axes, 0)
    return lax.slice_in_dim(whole, 0, len(lines)).reshape(x.shape).astype(jnp.float32)


def total_of(x, axes):
    lines = x.reshape(-1, x.shape[-1])
    own = sent_and_summed(padded_to(lines, lax.axis_size(axes)), axes, 0)
    whole = gathered_copies(own.astype(jnp.bfloat16), axes, 0)
    return whole[: len(lines)].reshape(x.shape).astype(jnp.float32)


def pair_index(target, source):
    return target * (target - 1) // 2 + source


def expand_mask(pattern, tiles, tile_width):
    grown = jnp.repeat(jnp.repeat(pattern, tile_width, axis=-2), tile_width, axis=-1)
    return tiles * grown.astype(tiles.dtype)


def forward_product(masked, vector):
    return jnp.dot(masked, vector, preferred_element_type=jnp.float32)


def backward_product(masked, vector):
    return lax.dot_general(
        masked, vector, (((0,), (0,)), ((), ())), preferred_element_type=jnp.float32
    )


def solve_blocks(inverse, first_block, residual, flipped):
    tile_width = inverse.shape[-1]
    number = residual.shape[0] // tile_width
    blocks = lax.dynamic_slice_in_dim(inverse, first_block, number, 0)
    pieces = residual.astype(jnp.bfloat16).reshape(number, tile_width, residual.shape[1])
    text_form = "sji,sjk->sik" if flipped else "sij,sjk->sik"
    solved = jnp.einsum(text_form, blocks, pieces, preferred_element_type=jnp.float32)
    return solved.reshape(residual.shape).astype(jnp.bfloat16)


def local(
    leaf_rhs,
    anc_rhs,
    leaf_tiles,
    cross_tiles,
    top_tiles,
    leaf_pattern,
    cross_pattern,
    top_pattern,
    leaf_inverse,
    anc_inverse,
):
    tile_width = leaf_inverse.shape[-1]
    row_count = leaf_rhs.shape[2]
    col_count = leaf_tiles.shape[3]
    leaf_levels = leaf_rhs.shape[1]
    anc_levels = anc_rhs.shape[0]
    row_index = lax.axis_index("row")
    col_index = lax.axis_index("col")
    row_first = row_index * (row_count // tile_width)
    col_first = col_index * (col_count // tile_width)
    leaf_masked = expand_mask(leaf_pattern[0], leaf_tiles[0], tile_width)
    cross_masked = expand_mask(cross_pattern[0], cross_tiles[0], tile_width)
    top_masked = expand_mask(top_pattern, top_tiles, tile_width)
    leaf_blocks = leaf_inverse[0]
    leaf_columns = []
    for target in range(leaf_levels):
        rhs_rows = leaf_rhs[0, target]
        partial_value = None
        for source in range(target):
            term_now = forward_product(
                leaf_masked[pair_index(target, source)], leaf_columns[source]
            )
            partial_value = term_now if partial_value is None else partial_value + term_now
        if partial_value is None:
            residual = rhs_rows
        else:
            residual = rhs_rows - of_everyone(partial_value.astype(jnp.bfloat16), "col").astype(
                jnp.float32
            )
        row_block = solve_blocks(leaf_blocks[target], row_first, residual, False)
        whole = gathered_copies(row_block, "row", 0)
        column_part = lax.dynamic_slice_in_dim(whole, col_index * col_count, col_count, 0)
        leaf_columns.append(column_part)
    leaf_terms = []
    for target in range(anc_levels):
        term_sum = forward_product(cross_masked[target, 0], leaf_columns[0])
        for source in range(1, leaf_levels):
            term_sum = term_sum + forward_product(
                cross_masked[target, source], leaf_columns[source]
            )
        leaf_terms.append(term_sum)
    lower_sums = sum_by_parts(jnp.stack(leaf_terms).astype(jnp.bfloat16), ("layer", "col"))
    anc_rows = []
    anc_columns = []
    for target in range(anc_levels):
        upper_part = None
        for source in range(target):
            term_now = forward_product(top_masked[pair_index(target, source)], anc_columns[source])
            upper_part = term_now
        summed = lower_sums[target]
        if upper_part is not None:
            summed = summed + of_everyone(upper_part.astype(jnp.bfloat16), "col").astype(
                jnp.float32
            )
        solved = solve_blocks(anc_inverse[target], row_first, anc_rhs[target] - summed, False)
        anc_rows.append(solved)
        whole = gathered_copies(solved, "row", 0)
        anc_columns.append(lax.dynamic_slice_in_dim(whole, col_index * col_count, col_count, 0))

    def finish(partial_value, column_values, inverse):
        summed = total_of(partial_value.astype(jnp.bfloat16), "row")
        residual = column_values.astype(jnp.float32) - summed
        solved = solve_blocks(inverse, col_first, residual, True)
        whole = gathered_copies(solved, "col", 0)
        return lax.dynamic_slice_in_dim(whole, row_index * row_count, row_count, 0)

    anc_out = [None] * anc_levels
    anc_out[anc_levels - 1] = solve_blocks(
        anc_inverse[anc_levels - 1], row_first, anc_rows[anc_levels - 1], True
    )
    target = 0
    partial_value = backward_product(
        top_masked[pair_index(target + 1, target)], anc_out[target + 1]
    )
    anc_out[target] = finish(partial_value, anc_columns[target], anc_inverse[target])
    leaf_out = [None] * leaf_levels
    for target in range(leaf_levels - 1, -1, -1):
        partial_value = backward_product(cross_masked[0, target], anc_out[0])
        partial_value = partial_value + backward_product(cross_masked[1, target], anc_out[1])
        for source in range(target + 1, leaf_levels):
            partial_value = partial_value + backward_product(
                leaf_masked[pair_index(source, target)], leaf_out[source]
            )
        leaf_out[target] = finish(partial_value, leaf_columns[target], leaf_blocks[target])
    return (jnp.stack(leaf_out)[None], jnp.stack(anc_out))


def solution(mesh):
    in_specs = (
        P("layer", None, "row", None),
        P(None, "row", None),
        P("layer", None, "row", "col"),
        P("layer", None, None, "row", "col"),
        P(None, "row", "col"),
        P("layer", None, "row", "col"),
        P("layer", None, None, "row", "col"),
        P(None, "row", "col"),
        P("layer", None, None, None, None),
        P(),
    )
    out_specs = (P("layer", None, "row", None), P(None, "row", None))
    return jax.shard_map(local, mesh=mesh, in_specs=in_specs, out_specs=out_specs, check_vma=False)
```

profile of v0, /device:TPU:1, one launch (start us, length us, event | category | flops | bytes accessed | tf_op | source)
XLA Modules:
  0.0 445.2 jit_solution(12982953590023085866)
XLA Ops:
  6.9 7.8 %all-to-all-start = ((bf16[16,256,256]{2,1,0:T(8,128)(2,1)}), bf16[16,256,256]{2,1,0:T(8,128)(2,1)}, u32[]{:S(2)}, u32[]{:S(2)}) async-start(bf16[16,256,256]{2,1,0:T(8,128)(2,1)} %broadcast_in_dim.72), calls=%async_computation | async-start | bytes 4194304 | tf_op jit(solution)/shard_map/all_to_all | solution.py:9
  25.0 20.7 %all-to-all-done = bf16[16,256,256]{2,1,0:T(8,128)(2,1)} async-done(((bf16[16,256,256]{2,1,0:T(8,128)(2,1)}), bf16[16,256,256]{2,1,0:T(8,128)(2,1)}, u32[]{:S(2)}, u32[]{:S(2)}) %all-to-all-start) | async-done | bytes 2097184 | tf_op jit(solution)/shard_map/all_to_all | solution.py:9
  47.5 5.4 %all_to_all.115 = bf16[2,256,256]{2,1,0:T(8,128)(2,1)S(1)} all-to-all(bf16[2,256,256]{2,1,0:T(8,128)(2,1)S(1)} %broadcast_in_dim.77), channel_id=1, replica_groups=mesh['layer'=8,'row'=16,'col'=2] {'col'}, dimensions={0} | all-to-all | bytes 524288 | tf_op jit(solution)/shard_map/all_to_all | solution.py:9
  60.1 5.5 %broadcast_in_dim.74 = bf16[2,3,256,16,128]{4,3,2,1,0:T(8,128)(2,1)} broadcast(bf16[2,3,256,16]{3,2,1,0:T(8,128)(2,1)S(1)} %bitcast.197), dimensions={0,1,2,3} | broadcast | bytes 6340608 | tf_op jit(solution)/shard_map/broadcast_in_dim | solution.py:78
  65.6 10.3 %convert_element_type.254 = bf16[2,3,256,2048]{3,2,1,0:T(8,128)(2,1)} reshape(bf16[2,3,256,16,128]{4,3,2,1,0:T(8,128)(2,1)} %broadcast_in_dim.74) | data formatting | bytes 12582912 | tf_op jit(solution)/shard_map/convert_element_type | solution.py:79
  78.3 14.8 %all-to-all-done.2 = bf16[16,256,256]{2,1,0:T(8,128)(2,1)} async-done(((bf16[16,256,256]{2,1,0:T(8,128)(2,1)}), bf16[16,256,256]{2,1,0:T(8,128)(2,1)}, u32[]{:S(2)}, u32[]{:S(2)}) %all-to-all-start.2) | async-done | bytes 2097184 | tf_op jit(solution)/shard_map/all_to_all | solution.py:9
  106.7 5.2 %bitcast_multiply_fusion = bf16[2,3,256,2048]{3,2,1,0:T(8,128)(2,1)S(1)} fusion(bf16[2,3,256,2048]{3,2,1,0:T(8,128)(2,1)} %convert_element_type.254, bf16[1,2,3,256,2048]{4,3,2,1,0:T(8,128)(2,1)} %param.13), kind=kLoop, calls=%fused_computation | loop fusion | flops 3145728 | bytes 18874368 | tf_op jit(solution)/shard_map/mul | solution.py:79
  120.2 19.5 %all-to-all-done.4 = bf16[16,256,256]{2,1,0:T(8,128)(2,1)} async-done(((bf16[16,256,256]{2,1,0:T(8,128)(2,1)}), bf16[16,256,256]{2,1,0:T(8,128)(2,1)}, u32[]{:S(2)}, u32[]{:S(2)}) %all-to-all-start.4) | async-done | bytes 2097184 | tf_op jit(solution)/shard_map/all_to_all | solution.py:9
  148.8 15.9 %all_to_all.118 = bf16[8,32,256]{2,1,0:T(8,128)(2,1)S(1)} all-to-all(bf16[8,32,256]{2,1,0:T(8,128)(2,1)S(1)} %reduce_sum.109), channel_id=1, replica_groups=mesh['layer'=8,'row'=16,'col'=2] {'layer'}, dimensions={0} | all-to-all | bytes 262144 | tf_op jit(solution)/shard_map/all_to_all | solution.py:55
  170.0 6.7 %all-to-all-done.7 = bf16[8,32,256]{2,1,0:T(8,128)(2,1)S(1)} async-done(((bf16[8,32,256]{2,1,0:T(8,128)(2,1)}), bf16[8,32,256]{2,1,0:T(8,128)(2,1)S(1)}, u32[]{:S(2)}, u32[]{:S(2)}) %all-to-all-start.7) | async-done | bytes 131104 | tf_op jit(solution)/shard_map/all_to_all | solution.py:9
  176.8 6.8 %all_to_all.119 = bf16[2,8,32,256]{3,2,1,0:T(8,128)(2,1)S(1)} all-to-all(bf16[2,8,32,256]{3,2,1,0:T(8,128)(2,1)S(1)} %broadcast_in_dim.82), channel_id=1, replica_groups=mesh['layer'=8,'row'=16,'col'=2] {'col'}, dimensions={0} | all-to-all | bytes 524288 | tf_op jit(solution)/shard_map/all_to_all | solution.py:9
  193.9 29.8 %all-to-all-done.9 = bf16[16,256,256]{2,1,0:T(8,128)(2,1)S(1)} async-done(((bf16[16,256,256]{2,1,0:T(8,128)(2,1)}), bf16[16,256,256]{2,1,0:T(8,128)(2,1)S(1)}, u32[]{:S(2)}, u32[]{:S(2)}) %all-to-all-start.9) | async-done | bytes 2097184 | tf_op jit(solution)/shard_map/all_to_all | solution.py:9
  233.4 19.5 %all_to_all.121 = bf16[16,128,256]{2,1,0:T(8,128)(2,1)S(1)} all-to-all(bf16[16,128,256]{2,1,0:T(8,128)(2,1)S(1)} %bitcast.180), channel_id=1, replica_groups=mesh['layer'=8,'row'=16,'col'=2] {'row'}, dimensions={0} | all-to-all | bytes 2097152 | tf_op jit(solution)/shard_map/all_to_all | solution.py:47
  258.1 15.2 %all-to-all-done.12 = bf16[16,128,256]{2,1,0:T(8,128)(2,1)S(1)} async-done(((bf16[16,128,256]{2,1,0:T(8,128)(2,1)}), bf16[16,128,256]{2,1,0:T(8,128)(2,1)S(1)}, u32[]{:S(2)}, u32[]{:S(2)}) %all-to-all-start.12) | async-done | bytes 1048608 | tf_op jit(solution)/shard_map/all_to_all | solution.py:9
  275.1 8.2 %all_to_all.122 = bf16[2,2048,256]{2,1,0:T(8,128)(2,1)S(1)} all-to-all(bf16[2,2048,256]{2,1,0:T(8,128)(2,1)S(1)} %broadcast_in_dim.88), channel_id=1, replica_groups=mesh['layer'=8,'row'=16,'col'=2] {'col'}, dimensions={0} | all-to-all | bytes 4194304 | tf_op jit(solution)/shard_map/all_to_all | solution.py:9
  287.5 19.1 %all_to_all.123 = bf16[16,128,256]{2,1,0:T(8,128)(2,1)S(1)} all-to-all(bf16[16,128,256]{2,1,0:T(8,128)(2,1)S(1)} %bitcast.186), channel_id=1, replica_groups=mesh['layer'=8,'row'=16,'col'=2] {'row'}, dimensions={0} | all-to-all | bytes 2097152 | tf_op jit(solution)/shard_map/all_to_all | solution.py:47
  316.3 10.5 %all-to-all-done.15 = bf16[16,128,256]{2,1,0:T(8,128)(2,1)S(1)} async-done(((bf16[16,128,256]{2,1,0:T(8,128)(2,1)}), bf16[16,128,256]{2,1,0:T(8,128)(2,1)S(1)}, u32[]{:S(2)}, u32[]{:S(2)}) %all-to-all-start.15) | async-done | bytes 1048608 | tf_op jit(solution)/shard_map/all_to_all | solution.py:9
  329.1 8.4 %all_to_all.124 = bf16[2,2048,256]{2,1,0:T(8,128)(2,1)S(1)} all-to-all(bf16[2,2048,256]{2,1,0:T(8,128)(2,1)S(1)} %broadcast_in_dim.90), channel_id=1, replica_groups=mesh['layer'=8,'row'=16,'col'=2] {'col'}, dimensions={0} | all-to-all | bytes 4194304 | tf_op jit(solution)/shard_map/all_to_all | solution.py:9
  338.9 19.9 %all_to_all.125 = bf16[16,128,256]{2,1,0:T(8,128)(2,1)} all-to-all(bf16[16,128,256]{2,1,0:T(8,128)(2,1)S(1)} %bitcast.181), channel_id=1, replica_groups=mesh['layer'=8,'row'=16,'col'=2] {'row'}, dimensions={0} | all-to-all | bytes 2097152 | tf_op jit(solution)/shard_map/all_to_all | solution.py:47
  370.4 10.7 %all-to-all-done.18 = bf16[16,128,256]{2,1,0:T(8,128)(2,1)} async-done(((bf16[16,128,256]{2,1,0:T(8,128)(2,1)}), bf16[16,128,256]{2,1,0:T(8,128)(2,1)}, u32[]{:S(2)}, u32[]{:S(2)}) %all-to-all-start.18) | async-done | bytes 1048608 | tf_op jit(solution)/shard_map/all_to_all | solution.py:9
  383.6 8.2 %all_to_all.126 = bf16[2,2048,256]{2,1,0:T(8,128)(2,1)S(1)} all-to-all(bf16[2,2048,256]{2,1,0:T(8,128)(2,1)S(1)} %broadcast_in_dim.92), channel_id=1, replica_groups=mesh['layer'=8,'row'=16,'col'=2] {'col'}, dimensions={0} | all-to-all | bytes 4194304 | tf_op jit(solution)/shard_map/all_to_all | solution.py:9
  394.6 19.2 %all_to_all.127 = bf16[16,128,256]{2,1,0:T(8,128)(2,1)S(1)} all-to-all(bf16[16,128,256]{2,1,0:T(8,128)(2,1)S(1)} %bitcast.179), channel_id=1, replica_groups=mesh['layer'=8,'row'=16,'col'=2] {'row'}, dimensions={0} | all-to-all | bytes 2097152 | tf_op jit(solution)/shard_map/all_to_all | solution.py:47
  422.2 11.9 %all-to-all-done.21 = bf16[16,128,256]{2,1,0:T(8,128)(2,1)S(1)} async-done(((bf16[16,128,256]{2,1,0:T(8,128)(2,1)}), bf16[16,128,256]{2,1,0:T(8,128)(2,1)S(1)}, u32[]{:S(2)}, u32[]{:S(2)}) %all-to-all-start.21) | async-done | bytes 1048608 | tf_op jit(solution)/shard_map/all_to_all | solution.py:9
  436.4 8.1 %all_to_all.128 = bf16[2,2048,256]{2,1,0:T(8,128)(2,1)S(1)} all-to-all(bf16[2,2048,256]{2,1,0:T(8,128)(2,1)S(1)} %broadcast_in_dim.94), channel_id=1, replica_groups=mesh['layer'=8,'row'=16,'col'=2] {'col'}, dimensions={0} | all-to-all | bytes 4194304 | tf_op jit(solution)/shard_map/all_to_all | solution.py:9
  (138 shorter events, 136.7 us)
Async XLA Ops:
  6.9 7.8 %copy-start.18 = (s32[1,3,2,16]{3,2,1,0:T(2,128)S(1)}, s32[1,3,2,16]{3,2,1,0:T(2,128)}, u32[]{:S(2)}) copy-start(s32[1,3,2,16]{3,2,1,0:T(2,128)} %param.15) | copy-start | bytes 1156
  6.9 38.8 %all-to-all-start = ((bf16[16,256,256]{2,1,0:T(8,128)(2,1)}), bf16[16,256,256]{2,1,0:T(8,128)(2,1)}, u32[]{:S(2)}, u32[]{:S(2)}) async-start(bf16[16,256,256]{2,1,0:T(8,128)(2,1)} %broadcast_in_dim.72), calls=%async_computation | async-start | bytes 4194304 | tf_op jit(solution)/shard_map/all_to_all | solution.py:9
  25.0 68.1 %copy-start.1 = (bf16[3,256,2048]{2,1,0:T(8,128)(2,1)}, bf16[3,256,2048]{2,1,0:T(8,128)(2,1)S(1)}, u32[]{:S(2)}) copy-start(bf16[3,256,2048]{2,1,0:T(8,128)(2,1)S(1)} %bitcast_multiply_fusion.1) | copy-start | bytes 9437188
  45.7 7.1 %copy-start.15 = (f32[1,1,256,256]{3,2,1,0:T(8,128)S(1)}, f32[1,1,256,256]{3,2,1,0:T(8,128)}, u32[]{:S(2)}) copy-start(f32[1,1,256,256]{3,2,1,0:T(8,128)} %get-tuple-element.8) | copy-start | bytes 786436
  55.5 4.6 %copy-start.17 = (s32[1,2,3,2,16]{4,3,2,1,0:T(2,128)S(1)}, s32[1,2,3,2,16]{4,3,2,1,0:T(2,128)}, u32[]{:S(2)}) copy-start(s32[1,2,3,2,16]{4,3,2,1,0:T(2,128)} %param.16) | copy-start | bytes 2308
  55.5 37.6 %all-to-all-start.2 = ((bf16[16,256,256]{2,1,0:T(8,128)(2,1)}), bf16[16,256,256]{2,1,0:T(8,128)(2,1)}, u32[]{:S(2)}, u32[]{:S(2)}) async-start(bf16[16,256,256]{2,1,0:T(8,128)(2,1)} %broadcast_in_dim.78), calls=%async_computation.2 | async-start | bytes 4194304 | tf_op jit(solution)/shard_map/all_to_all | solution.py:9
  102.3 37.5 %all-to-all-start.4 = ((bf16[16,256,256]{2,1,0:T(8,128)(2,1)}), bf16[16,256,256]{2,1,0:T(8,128)(2,1)}, u32[]{:S(2)}, u32[]{:S(2)}) async-start(bf16[16,256,256]{2,1,0:T(8,128)(2,1)} %broadcast_in_dim.80), calls=%async_computation.4 | async-start | bytes 4194304 | tf_op jit(solution)/shard_map/all_to_all | solution.py:9
  112.0 5.9 %copy-start = (bf16[2,3,256,2048]{3,2,1,0:T(8,128)(2,1)}, bf16[2,3,256,2048]{3,2,1,0:T(8,128)(2,1)S(1)}, u32[]{:S(2)}) copy-start(bf16[2,3,256,2048]{3,2,1,0:T(8,128)(2,1)S(1)} %bitcast_multiply_fusion) | copy-start | bytes 18874372
  120.2 21.5 %copy-start.20 = (f32[256,256]{1,0:T(8,128)S(1)}, f32[256,256]{1,0:T(8,128)}, u32[]{:S(2)}) copy-start(f32[256,256]{1,0:T(8,128)} %convolution_add_fusion.10) | copy-start | bytes 786436
  141.8 27.0 %copy-start.14 = (bf16[2,32,128,128]{3,2,1,0:T(8,128)(2,1)S(1)}, bf16[2,32,128,128]{3,2,1,0:T(8,128)(2,1)}, u32[]{:S(2)}) copy-start(bf16[2,32,128,128]{3,2,1,0:T(8,128)(2,1)} %param.19) | copy-start | bytes 6291460
  165.4 11.3 %all-to-all-start.7 = ((bf16[8,32,256]{2,1,0:T(8,128)(2,1)}), bf16[8,32,256]{2,1,0:T(8,128)(2,1)S(1)}, u32[]{:S(2)}, u32[]{:S(2)}) async-start(bf16[8,32,256]{2,1,0:T(8,128)(2,1)} %broadcast_in_dim.81), calls=%async_computation.7 | async-start | bytes 262144 | tf_op jit(solution)/shard_map/all_to_all | solution.py:9
  170.0 15.2 %copy-start.12 = (bf16[1,32,128,128]{3,2,1,0:T(8,128)(2,1)}, bf16[1,32,128,128]{3,2,1,0:T(8,128)(2,1)S(1)}, u32[]{:S(2)}) copy-start(bf16[1,32,128,128]{3,2,1,0:T(8,128)(2,1)S(1)} %get-tuple-element.6) | copy-start | bytes 3145732
  170.0 14.3 %copy-start.16 = (f32[2,256,256]{2,1,0:T(8,128)S(1)}, f32[2,256,256]{2,1,0:T(8,128)}, u32[]{:S(2)}) copy-start(f32[2,256,256]{2,1,0:T(8,128)} %param.11) | copy-start | bytes 1572868
  186.8 36.8 %all-to-all-start.9 = ((bf16[16,256,256]{2,1,0:T(8,128)(2,1)}), bf16[16,256,256]{2,1,0:T(8,128)(2,1)S(1)}, u32[]{:S(2)}, u32[]{:S(2)}) async-start(bf16[16,256,256]{2,1,0:T(8,128)(2,1)} %broadcast_in_dim.83), calls=%async_computation.9 | async-start | bytes 4194304 | tf_op jit(solution)/shard_map/all_to_all | solution.py:9
  254.2 19.1 %all-to-all-start.12 = ((bf16[16,128,256]{2,1,0:T(8,128)(2,1)}), bf16[16,128,256]{2,1,0:T(8,128)(2,1)S(1)}, u32[]{:S(2)}, u32[]{:S(2)}) async-start(bf16[16,128,256]{2,1,0:T(8,128)(2,1)} %broadcast_in_dim.87), calls=%async_computation.12 | async-start | bytes 2097152 | tf_op jit(solution)/shard_map/all_to_all | solution.py:9
  283.3 4.2 copy-start.5
  307.9 19.0 %all-to-all-start.15 = ((bf16[16,128,256]{2,1,0:T(8,128)(2,1)}), bf16[16,128,256]{2,1,0:T(8,128)(2,1)S(1)}, u32[]{:S(2)}, u32[]{:S(2)}) async-start(bf16[16,128,256]{2,1,0:T(8,128)(2,1)} %broadcast_in_dim.89), calls=%async_computation.15 | async-start | bytes 2097152 | tf_op jit(solution)/shard_map/all_to_all | solution.py:9
  316.3 12.1 %copy-start.11 = (bf16[1,1,32,128,128]{4,3,2,1,0:T(8,128)(2,1)S(1)}, bf16[1,1,32,128,128]{4,3,2,1,0:T(8,128)(2,1)}, u32[]{:S(2)}) copy-start(bf16[1,1,32,128,128]{4,3,2,1,0:T(8,128)(2,1)} %get-tuple-element.2) | copy-start | bytes 3145732
  329.0 8.5 %copy-start.4 = (f32[2048,256]{1,0:T(8,128)S(1)}, f32[2048,256]{1,0:T(8,128)}, u32[]{:S(2)}) copy-start(f32[2048,256]{1,0:T(8,128)} %convolution_add_fusion.4) | copy-start | bytes 6291460
  329.1 8.4 %copy-start.2 = (bf16[3,256,2048]{2,1,0:T(8,128)(2,1)S(1)}, bf16[3,256,2048]{2,1,0:T(8,128)(2,1)}, u32[]{:S(2)}) copy-start(bf16[3,256,2048]{2,1,0:T(8,128)(2,1)} %copy-done.1) | copy-start | bytes 9437188
  361.2 19.8 %all-to-all-start.18 = ((bf16[16,128,256]{2,1,0:T(8,128)(2,1)}), bf16[16,128,256]{2,1,0:T(8,128)(2,1)}, u32[]{:S(2)}, u32[]{:S(2)}) async-start(bf16[16,128,256]{2,1,0:T(8,128)(2,1)} %broadcast_in_dim.91), calls=%async_computation.18 | async-start | bytes 2097152 | tf_op jit(solution)/shard_map/all_to_all | solution.py:9
  383.6 8.2 %copy-start.3 = (f32[2048,256]{1,0:T(8,128)S(1)}, f32[2048,256]{1,0:T(8,128)}, u32[]{:S(2)}) copy-start(f32[2048,256]{1,0:T(8,128)} %convolution_add_fusion.5) | copy-start | bytes 6291460
  415.0 19.1 %all-to-all-start.21 = ((bf16[16,128,256]{2,1,0:T(8,128)(2,1)}), bf16[16,128,256]{2,1,0:T(8,128)(2,1)S(1)}, u32[]{:S(2)}, u32[]{:S(2)}) async-start(bf16[16,128,256]{2,1,0:T(8,128)(2,1)} %broadcast_in_dim.93), calls=%async_computation.21 | async-start | bytes 2097152 | tf_op jit(solution)/shard_map/all_to_all | solution.py:9
  419.6 16.1 %copy-start.9 = (bf16[1,1,32,128,128]{4,3,2,1,0:T(8,128)(2,1)S(1)}, bf16[1,1,32,128,128]{4,3,2,1,0:T(8,128)(2,1)}, u32[]{:S(2)}) copy-start(bf16[1,1,32,128,128]{4,3,2,1,0:T(8,128)(2,1)} %copy-done.8) | copy-start | bytes 3145732
  (6 other events, 11.5 us)
where the time goes:
time: 448 us; the launch traced here: 445 us
  blocking collectives  153 us (34%)
  waiting for transfers between devices  140 us (31%)
  local copies, waits for them, and re-layouts  49.9 us (11%)
  matrix products  43.6 us (10%)
  starting transfers between devices  39.5 us (9%)
  other arithmetic  18.1 us (4%)
    all_to_all x9, waiting for transfers between devices, copy_for_each(): return lax.all_to_all(copies, axis, split_axis=0, concat_axis=0, tiled=True)  140 us
    all_to_all x5, blocking collectives, sent_and_summed(): pieces = lax.all_to_all(in_blocks(x, dim, peers), axis, 0, 0, tiled=True)  82.6 us
    all_to_all x8, blocking collectives, copy_for_each(): return lax.all_to_all(copies, axis, split_axis=0, concat_axis=0, tiled=True)  54.5 us
    all_to_all x9, starting transfers between devices, copy_for_each(): return lax.all_to_all(copies, axis, split_axis=0, concat_axis=0, tiled=True)  39.5 us
    dot_general x10, matrix products, forward_product(): return jnp.dot(masked, vector, preferred_element_type=jnp.float32)  19.8 us
    dot_general x10, matrix products, backward_product(): lax.dot_general(masked, vector, (((0,), (0,)), ((), ())), preferred_eleme...  18 us
    all_to_all x1, blocking collectives, sum_by_axis(): lax.all_to_all(own.astype(jnp.bfloat16), far, 0, 0, tiled=True)  15.9 us
    convert_element_type x3, local copies, waits for them, and re-layouts, expand_mask(): return tiles * grown.astype(tiles.dtype)  15.2 us
  transfers between devices with their start and end apart: 9, of which 9 were waited for; matrix products, arithmetic and copies ran while one was open for 13% of the time, Pallas kernels for 0%

commit v1 on v0

v1 whole, which is shorter than its diff:
```python
import functools

import jax
import jax.numpy as jnp
from jax import lax
from jax.experimental import pallas as pl
from jax.experimental.pallas import tpu as pltpu
from jax.sharding import PartitionSpec as P

F32 = jnp.float32
BF16 = jnp.bfloat16
TILE = 128
SWAP = [(0, 1), (1, 0)]

VMEM = pl.BlockSpec(memory_space=pltpu.VMEM)
SMEM = pl.BlockSpec(memory_space=pltpu.SMEM)


def nt(a, b):
    return lax.dot_general(a, b, (((1,), (1,)), ((), ())), preferred_element_type=F32)


def nn(a, b):
    return jnp.dot(a, b, preferred_element_type=F32)


def masked(tiles, pattern, slab, block):
    lines = []
    for upper in range(2):
        row = []
        for side in range(2):
            at = 2 * block + side
            tile = tiles[slab, TILE * upper : TILE * (upper + 1), TILE * at : TILE * (at + 1)]
            kept = pattern[(slab * 2 + upper) * 16 + at] != 0
            row.append(lax.select(kept, tile, jnp.zeros_like(tile)))
        lines.append(jnp.concatenate(row, axis=1))
    return jnp.concatenate(lines, axis=0)


def halves(where, own, other):
    return ((own, 0, where[0] * 8), (other, 1, (1 - where[0]) * 8))


def solved(residual, inverse):
    cut = residual.astype(BF16)
    return jnp.concatenate(
        [nt(cut[:, TILE * s : TILE * (s + 1)], inverse[s]) for s in range(2)], axis=1
    ).astype(BF16)


def solved_back(residual, inverse):
    cut = residual.astype(BF16)
    return jnp.concatenate(
        [nn(cut[:, TILE * s : TILE * (s + 1)], inverse[s]) for s in range(2)], axis=1
    ).astype(BF16)


def forward_sum(where, tiles, patterns, slab, values):
    total = None
    for half in range(2):
        first = (where[0] if half == 0 else 1 - where[0]) * 8
        for block in range(8):
            term = nt(values[first + block], masked(tiles[half], patterns[half], slab, block))
            total = term if total is None else total + term
    return total


def to_copies(out, value):
    for peer in range(out.shape[0]):
        out[peer] = value


def total_of(pieces):
    total = pieces[0].astype(F32)
    for peer in range(1, pieces.shape[0]):
        total = total + pieces[peer].astype(F32)
    return total


def call(body, out_shape, operands, flops, name):
    specs = [SMEM if x.dtype == jnp.int32 else VMEM for x in operands]
    single = not isinstance(out_shape, (list, tuple))
    shapes = [out_shape] if single else list(out_shape)
    moved = sum(x.size * x.dtype.itemsize for x in operands)
    out = pl.pallas_call(
        body,
        out_shape=shapes,
        in_specs=specs,
        out_specs=[VMEM] * len(shapes),
        compiler_params=pltpu.CompilerParams(vmem_limit_bytes=24 * 1024 * 1024),
        cost_estimate=pl.CostEstimate(flops=flops, bytes_accessed=moved, transcendentals=0),
        name=name,
    )(*operands)
    return out[0] if single else out


def shape(*dims, dtype=BF16):
    return jax.ShapeDtypeStruct(dims, dtype)


SLAB_FLOPS = 2 * 256 * 4096 * 128


def first_kernel(rhs, inverse, out):
    to_copies(out, solved(rhs[...].T, inverse))


def next_kernel(slabs, slab_of_last, *refs):
    where, pat_own, pat_oth, own, oth, values, rhs, inverse, *rest = refs
    out = rest[-1]
    total = forward_sum(where, (own, oth), (pat_own, pat_oth), slab_of_last, values)
    if len(rest) > 1:
        total = total + rest[0][...]
    to_copies(out, solved(rhs[...].T - total, inverse))


def part_kernel(slabs, where, pat_own, pat_oth, own, oth, values, out):
    for at, slab in enumerate(slabs):
        out[at] = forward_sum(where, (own, oth), (pat_own, pat_oth), slab, values)


def more_kernel(slabs, where, pat_own, pat_oth, own, oth, values, before, out):
    for at, slab in enumerate(slabs):
        out[at] = before[at] + forward_sum(where, (own, oth), (pat_own, pat_oth), slab, values)


def cross_kernel(slabs, where, pat_own, pat_oth, own, oth, values, before, out):
    layers = out.shape[0]
    for at, slab in enumerate(slabs):
        total = before[at] + forward_sum(where, (own, oth), (pat_own, pat_oth), slab, values)
        total = total.astype(BF16).reshape(layers, -1, total.shape[1])
        out[:, at] = total


def anc_first_kernel(pieces, rhs, inverse, out, rest):
    value = solved(rhs[0] - total_of(pieces.at[:, 0]), inverse)
    to_copies(out, value)
    rest[...] = rhs[1] - total_of(pieces.at[:, 1])


def anc_second_kernel(where, pat_own, pat_oth, own, oth, values, rest, inverse, out, top):
    total = forward_sum(where, (own, oth), (pat_own, pat_oth), 0, values)
    value = solved(rest[...] - total, inverse)
    back = solved_back(value.astype(F32), inverse)
    top[...] = back
    for half, tiles in enumerate((own, oth)):
        pattern = (pat_own, pat_oth)[half]
        first = (where[0] if half == 0 else 1 - where[0]) * 8
        for block in range(8):
            out[first + block] = nn(back, masked(tiles, pattern, 0, block)).astype(BF16)


def anc_third_kernel(row, pieces, lower, top, inverse, out):
    residual = lower[row[0]].astype(F32) - total_of(pieces)
    value = solved_back(residual, inverse)
    for peer in range(out.shape[0]):
        out[peer, 0] = value
        out[peer, 1] = top[...]


def back_parts(where, groups, out):
    for half in range(2):
        first = (where[0] if half == 0 else 1 - where[0]) * 8
        for block in range(8):
            total = None
            for tiles, patterns, slab, values in groups:
                term = nn(values, masked(tiles[half], patterns[half], slab, block))
                total = term if total is None else total + term
            out[first + block] = total.astype(BF16)


def of_layers(pieces, at):
    value = pieces[:, at]
    return value.reshape(-1, value.shape[-1])


def back_first_kernel(slabs, where, pat_own, pat_oth, own, oth, anc, out):
    groups = [
        ((own, oth), (pat_own, pat_oth), slab, of_layers(anc, at)) for at, slab in enumerate(slabs)
    ]
    back_parts(where, groups, out)


def back_next_kernel(
    cross_slabs, leaf_slabs, row, where, cpat_own, cpat_oth, lpat_own, lpat_oth, cown, coth, lown, loth,
    anc, pieces, value, inverse, *rest
):
    *earlier, out, solution, flipped = rest
    now = solved_back(value[row[0]].astype(F32) - total_of(pieces), inverse)
    solution[...] = now
    flipped[...] = now.astype(F32).T.astype(BF16)
    groups = [
        ((cown, coth), (cpat_own, cpat_oth), slab, of_layers(anc, at))
        for at, slab in enumerate(cross_slabs)
    ]
    known = [now, *(e[...] for e in earlier)]
    groups += [
        ((lown, loth), (lpat_own, lpat_oth), slab, values)
        for slab, values in zip(leaf_slabs, known)
    ]
    back_parts(where, groups, out)


def back_last_kernel(row, pieces, value, inverse, flipped):
    now = solved_back(value[row[0]].astype(F32) - total_of(pieces), inverse)
    flipped[...] = now.astype(F32).T.astype(BF16)


def flip_kernel(anc, out):
    for at in range(2):
        out[at] = of_layers(anc, at).astype(F32).T.astype(BF16)


def spread(x, axis):
    return lax.all_to_all(x, axis, split_axis=0, concat_axis=0, tiled=True)


def local(
    leaf_rhs, anc_rhs, leaf_tiles, cross_tiles, top_tiles, leaf_pattern, cross_pattern, top_pattern,
    leaf_inverse, anc_inverse,
):
    row = lax.axis_index("row")
    col = lax.axis_index("col")
    layer = lax.axis_index("layer")
    layers = lax.axis_size("layer")
    rows = lax.axis_size("row")
    leaf_own = leaf_tiles[0]
    cross_own = cross_tiles[0].reshape(6, 256, 2048)
    top_own = top_tiles
    patterns = jnp.concatenate(
        [leaf_pattern.reshape(-1), cross_pattern.reshape(-1), top_pattern.reshape(-1)]
    )
    pat_other = lax.ppermute(patterns, "col", SWAP)
    leaf_oth = lax.ppermute(leaf_own, "col", SWAP)
    cross_oth = lax.ppermute(cross_own, "col", SWAP)
    top_oth = lax.ppermute(top_own, "col", SWAP)
    lp = (patterns[:96], pat_other[:96])
    cp = (patterns[96:288], pat_other[96:288])
    tp = (patterns[288:], pat_other[288:])
    leaf_args = (*lp, leaf_own, leaf_oth)
    cross_args = (*cp, cross_own, cross_oth)
    top_args = (*tp, top_own, top_oth)
    where = col.astype(jnp.int32).reshape(1)
    here = row.astype(jnp.int32).reshape(1)

    rhs = lax.dynamic_slice_in_dim(leaf_rhs[0], col * 128, 128, 2)
    width = 128 // layers
    anc_part = lax.dynamic_slice_in_dim(anc_rhs, col * 128 + layer * width, width, 2).swapaxes(1, 2)
    inverse = lax.dynamic_slice_in_dim(leaf_inverse[0], 2 * row, 2, 1)
    inverse_anc = lax.dynamic_slice_in_dim(anc_inverse, 2 * row, 2, 1)

    wide = shape(rows, 128, 256)
    y0 = spread(call(first_kernel, wide, (rhs[0], inverse[0]), 1, "y0"), "row")
    y1 = spread(
        call(
            functools.partial(next_kernel, None, 0), wide, (where, *leaf_args, y0, rhs[1], inverse[1]), SLAB_FLOPS, "y1"
        ),
        "row",
    )
    part2 = call(
        functools.partial(part_kernel, (1,)), shape(1, 128, 256, dtype=F32), (where, *leaf_args, y0), SLAB_FLOPS, "p2"
    )[0]
    cross0 = call(
        functools.partial(part_kernel, (0, 3)), shape(2, 128, 256, dtype=F32), (where, *cross_args, y0), 2 * SLAB_FLOPS, "c0"
    )
    y2 = spread(
        call(
            functools.partial(next_kernel, None, 2), wide, (where, *leaf_args, y1, rhs[2], inverse[2], part2), SLAB_FLOPS, "y2"
        ),
        "row",
    )
    cross1 = call(
        functools.partial(more_kernel, (1, 4)), shape(2, 128, 256, dtype=F32), (where, *cross_args, y1, cross0), 2 * SLAB_FLOPS, "c1"
    )
    lower = spread(
        call(
            functools.partial(cross_kernel, (2, 5)), shape(layers, 2, width, 256), (where, *cross_args, y2, cross1), 2 * SLAB_FLOPS, "c2"
        ),
        "layer",
    )
    z0, rest = call(
        anc_first_kernel, [shape(rows, width, 256), shape(width, 256, dtype=F32)], (lower, anc_part, inverse_anc[0]), 1, "z0"
    )
    z0 = spread(z0, "row")
    pieces, top = call(
        anc_second_kernel, [shape(rows, width, 256), shape(width, 256)], (where, *top_args, z0, rest, inverse_anc[1]), SLAB_FLOPS // 4, "z1"
    )
    pieces = spread(pieces, "row")
    anc = call(
        anc_third_kernel, shape(layers, 2, width, 256), (here, pieces, z0, top, inverse_anc[0]), 1, "a0"
    )
    anc = spread(anc, "layer")
    pieces = spread(
        call(functools.partial(back_first_kernel, (2, 5)), wide, (where, *cross_args, anc), 2 * SLAB_FLOPS, "b2"), "row"
    )
    flat = (shape(128, 256), shape(256, 128))
    both = (*cp, *lp, cross_own, cross_oth, leaf_own, leaf_oth)
    pieces, x2, f2 = call(
        functools.partial(back_next_kernel, (1, 4), (2,)), [wide, *flat],
        (here, where, *both, anc, pieces, y2, inverse[2]), 3 * SLAB_FLOPS, "b1",
    )
    pieces = spread(pieces, "row")
    pieces, x1, f1 = call(
        functools.partial(back_next_kernel, (0, 3), (0, 1)), [wide, *flat],
        (here, where, *both, anc, pieces, y1, inverse[1], x2), 4 * SLAB_FLOPS, "b0",
    )
    pieces = spread(pieces, "row")
    f0 = call(back_last_kernel, shape(256, 128), (here, pieces, y0, inverse[0]), 1, "x0")
    fa = call(flip_kernel, shape(2, 256, 128), (anc,), 1, "fa")

    def joined(mine):
        theirs = lax.ppermute(mine, "col", SWAP)
        return jnp.where(
            col == 0,
            jnp.concatenate([mine, theirs], axis=-1),
            jnp.concatenate([theirs, mine], axis=-1),
        )

    return (jnp.stack([joined(f0), joined(f1), joined(f2)])[None], joined(fa))


def solution(mesh):
    in_specs = (
        P("layer", None, "row", None),
        P(None, "row", None),
        P("layer", None, "row", "col"),
        P("layer", None, None, "row", "col"),
        P(None, "row", "col"),
        P("layer", None, "row", "col"),
        P("layer", None, None, "row", "col"),
        P(None, "row", "col"),
        P("layer", None, None, None, None),
        P(),
    )
    out_specs = (P("layer", None, "row", None), P(None, "row", None))
    return jax.shard_map(local, mesh=mesh, in_specs=in_specs, out_specs=out_specs, check_vma=False)
```

time: 448 us -> 223 us (0.50)
  blocking collectives: 153 us -> 49.5 us
  waiting for transfers between devices: 140 us -> 43.3 us
  matrix products: 43.6 us -> 0 us
  Pallas kernels: 0 us -> 43.6 us
  local copies, waits for them, and re-layouts: 49.9 us -> 24.5 us
  starting transfers between devices: 39.5 us -> 58.1 us
  other arithmetic: 18.1 us -> 1.77 us
    all_to_all x9 -> x6, waiting for transfers between devices: 140 us -> 36.4 us  [spread(): return lax.all_to_all(x, axis, split_axis=0, concat_axis=0, tiled=True)]
    all_to_all x14 -> x4, blocking collectives: 153 us -> 49.5 us  [spread(): return lax.all_to_all(x, axis, split_axis=0, concat_axis=0, tiled=True)]
    dot_general x29 -> x0, matrix products: 43.6 us -> none  [the longest x10 19.8 us: forward_product(): return jnp.dot(masked, vector, preferred_element_type=jnp.float32)]
    pallas_call x0 -> x15, Pallas kernels: none -> 43.6 us  [call(): pl.pallas_call(body, out_shape=shapes, in_specs=specs, out_specs=[VMEM] *...]
    ppermute x0 -> x8, starting transfers between devices: none -> 25.6 us  [the longest x4 18.5 us: joined(): theirs = lax.ppermute(mine, 'col', SWAP)]
    broadcast_in_dim x23 -> x0, local copies, waits for them, and re-layouts: 21.1 us -> none  [the longest x17 11.9 us: copy_for_each(): copies = jnp.broadcast_to(x, (lax.axis_size(axis), *x.shape))]
    unnamed x42 -> x37, local copies, waits for them, and re-layouts: 2.62 us -> 21.1 us
    convert_element_type x4 -> x0, local copies, waits for them, and re-layouts: 15.2 us -> none  [the longest x3 15.2 us: expand_mask(): return tiles * grown.astype(tiles.dtype)]
  transfers between devices with their start and end apart: 9 -> 14, of which waited for: 9 -> 9; matrix products, arithmetic and copies ran while one was open for 13% -> 2% of each run, Pallas kernels for 0% -> 11%
where the time goes in v1:
time: 223 us; the launch traced here: 222 us
  starting transfers between devices  58.1 us (26%)
  blocking collectives  49.5 us (22%)
  Pallas kernels  43.6 us (20%)
  waiting for transfers between devices  43.3 us (19%)
  local copies, waits for them, and re-layouts  24.5 us (11%)
    all_to_all x4, blocking collectives, spread(): return lax.all_to_all(x, axis, split_axis=0, concat_axis=0, tiled=True)  49.5 us
    pallas_call x15, Pallas kernels, call(): pl.pallas_call(body, out_shape=shapes, in_specs=specs, out_specs=[VMEM] *...  43.6 us
    all_to_all x6, waiting for transfers between devices, spread(): return lax.all_to_all(x, axis, split_axis=0, concat_axis=0, tiled=True)  36.4 us
    all_to_all x6, starting transfers between devices, spread(): return lax.all_to_all(x, axis, split_axis=0, concat_axis=0, tiled=True)  32.6 us
    unnamed x37, local copies, waits for them, and re-layouts  21.1 us
    ppermute x4, starting transfers between devices, joined(): theirs = lax.ppermute(mine, 'col', SWAP)  18.5 us
    ppermute x1, waiting for transfers between devices, local(): pat_other = lax.ppermute(patterns, 'col', SWAP)  5.16 us
  transfers between devices with their start and end apart: 14, of which 9 were waited for; matrix products, arithmetic and copies ran while one was open for 2% of the time, Pallas kernels for 11%

profile of v1, /device:TPU:1, one launch (start us, length us, event | category | flops | bytes accessed | tf_op | source)
XLA Modules:
  0.0 221.7 jit_solution(5141333888123974130)
XLA Ops:
  0.7 3.3 %collective-permute-start.1 = (bf16[6,256,2048]{2,1,0:T(8,128)(2,1)}, bf16[6,256,2048]{2,1,0:T(8,128)(2,1)}, u32[]{:S(2)}, u32[]{:S(2)}) collective-permute-start(bf16[6,256,2048]{2,1,0:T(8,128)(2,1)} %bitcast.30), channel_id=1, source_target_pairs={{0,1},{1,0},{2,3},{3,2},{4,5},{5,4},{6,7},{7,6},{8,9},{9,8},{10,11... | collective-permute-start | bytes 18874376 | tf_op jit(solution)/shard_map/ppermute | solution.py:235
  7.3 5.0 %all-to-all-start = ((bf16[16,128,256]{2,1,0:T(8,128)(2,1)}), bf16[16,128,256]{2,1,0:T(8,128)(2,1)S(1)}, u32[]{:S(2)}, u32[]{:S(2)}) async-start(bf16[16,128,256]{2,1,0:T(8,128)(2,1)} %y0.1), calls=%async_computation | async-start | bytes 2097152 | tf_op jit(solution)/shard_map/all_to_all | solution.py:215
  13.4 5.2 %collective-permute-done = s32[320]{0:T(512)S(1)} collective-permute-done((s32[320]{0:T(512)S(1)}, s32[320]{0:T(512)S(1)}, u32[]{:S(2)}, u32[]{:S(2)}) %collective-permute-start) | collective-permute-done | bytes 1312 | tf_op jit(solution)/shard_map/ppermute | solution.py:233
  18.6 10.1 %all-to-all-done.refs_5_.values.value = bf16[16,128,256]{2,1,0:T(8,128)(2,1)S(1)} async-done(((bf16[16,128,256]{2,1,0:T(8,128)(2,1)}), bf16[16,128,256]{2,1,0:T(8,128)(2,1)S(1)}, u32[]{:S(2)}, u32[]{:S(2)}) %all-to-all-start) | async-done | bytes 1048608 | tf_op jit(solution)/shard_map/all_to_all | solution.py:215
  34.5 4.5 %all-to-all-start.1 = ((bf16[16,128,256]{2,1,0:T(8,128)(2,1)}), bf16[16,128,256]{2,1,0:T(8,128)(2,1)S(1)}, u32[]{:S(2)}, u32[]{:S(2)}) async-start(bf16[16,128,256]{2,1,0:T(8,128)(2,1)} %copy-done.10), calls=%async_computation.1 | async-start | bytes 2097152 | tf_op jit(solution)/shard_map/all_to_all | solution.py:215
  43.6 11.1 %all-to-all-done.1.refs_5_.values.value = bf16[16,128,256]{2,1,0:T(8,128)(2,1)S(1)} async-done(((bf16[16,128,256]{2,1,0:T(8,128)(2,1)}), bf16[16,128,256]{2,1,0:T(8,128)(2,1)S(1)}, u32[]{:S(2)}, u32[]{:S(2)}) %all-to-all-start.1) | async-done | bytes 1048608 | tf_op jit(solution)/shard_map/all_to_all | solution.py:215
  60.5 4.3 %all-to-all-start.2 = ((bf16[16,128,256]{2,1,0:T(8,128)(2,1)}), bf16[16,128,256]{2,1,0:T(8,128)(2,1)}, u32[]{:S(2)}, u32[]{:S(2)}) async-start(bf16[16,128,256]{2,1,0:T(8,128)(2,1)} %copy-done.9), calls=%async_computation.2 | async-start | bytes 2097152 | tf_op jit(solution)/shard_map/all_to_all | solution.py:215
  70.7 4.3 %c0.1.before = f32[2,128,256]{2,1,0:T(8,128)S(1)} custom-call(s32[1]{0:T(128)} %bitcast.1.refs_0_.where, s32[192]{0:T(256)S(1)} %reshape.200.pat_own.cpat_own, s32[192]{0:T(256)S(1)} %slice.43.pat_oth.cpat_oth, bf16[6,256,2048]{2,1,0:T(8,128)(2,1)S(1)} %bitcast.31, bf16[6,256,2048]{2,1,0:T(8,128)(2,1)} %collective-permute-done.1.oth.coth, ...), custom_call_target="tpu_custom_call" | custom-call | flops 536870912 | bytes 13633028 | tf_op jit(solution)/shard_map/c0/pallas_call | solution.py:85
  75.0 4.3 %c1.1.before = f32[2,128,256]{2,1,0:T(8,128)S(1)} custom-call(s32[1]{0:T(128)} %bitcast.1.refs_0_.where, s32[192]{0:T(256)S(1)} %reshape.200.pat_own.cpat_own, s32[192]{0:T(256)S(1)} %slice.43.pat_oth.cpat_oth, bf16[6,256,2048]{2,1,0:T(8,128)(2,1)S(1)} %bitcast.32, bf16[6,256,2048]{2,1,0:T(8,128)(2,1)} %collective-permute-done.1.oth.coth, ...), custom_call_target="tpu_custom_call" | custom-call | flops 536870912 | bytes 13895172 | tf_op jit(solution)/shard_map/c1/pallas_call | solution.py:85
  82.3 5.2 %c2.1 = bf16[8,2,16,256]{3,2,1,0:T(8,128)(2,1)} custom-call(s32[1]{0:T(128)} %bitcast.1.refs_0_.where, s32[192]{0:T(256)S(1)} %reshape.200.pat_own.cpat_own, s32[192]{0:T(256)S(1)} %slice.43.pat_oth.cpat_oth, bf16[6,256,2048]{2,1,0:T(8,128)(2,1)S(1)} %bitcast.33, bf16[6,256,2048]{2,1,0:T(8,128)(2,1)} %collective-permute-done.1.oth.coth, ...), custom_call_target="tpu_custom_call" | custom-call | flops 536870912 | bytes 13895172 | tf_op jit(solution)/shard_map/c2/pallas_call | solution.py:85
  87.5 8.2 %all-to-all-start.3 = ((bf16[8,2,16,256]{3,2,1,0:T(8,128)(2,1)}), bf16[8,2,16,256]{3,2,1,0:T(8,128)(2,1)S(1)}, u32[]{:S(2)}, u32[]{:S(2)}) async-start(bf16[8,2,16,256]{3,2,1,0:T(8,128)(2,1)} %c2.1), calls=%async_computation.3 | async-start | bytes 262144 | tf_op jit(solution)/shard_map/all_to_all | solution.py:215
  96.9 6.8 %all-to-all-done.3.pieces = bf16[8,2,16,256]{3,2,1,0:T(8,128)(2,1)S(1)} async-done(((bf16[8,2,16,256]{3,2,1,0:T(8,128)(2,1)}), bf16[8,2,16,256]{3,2,1,0:T(8,128)(2,1)S(1)}, u32[]{:S(2)}, u32[]{:S(2)}) %all-to-all-start.3) | async-done | bytes 131104 | tf_op jit(solution)/shard_map/all_to_all | solution.py:215
  104.5 6.8 %all-to-all-start.4 = ((bf16[16,16,256]{2,1,0:T(8,128)(2,1)}), bf16[16,16,256]{2,1,0:T(8,128)(2,1)S(1)}, u32[]{:S(2)}, u32[]{:S(2)}) async-start(bf16[16,16,256]{2,1,0:T(8,128)(2,1)} %get-tuple-element.11), calls=%async_computation.4 | async-start | bytes 262144 | tf_op jit(solution)/shard_map/all_to_all | solution.py:215
  111.4 6.8 %all-to-all-done.4.values.lower = bf16[16,16,256]{2,1,0:T(8,128)(2,1)S(1)} async-done(((bf16[16,16,256]{2,1,0:T(8,128)(2,1)}), bf16[16,16,256]{2,1,0:T(8,128)(2,1)S(1)}, u32[]{:S(2)}, u32[]{:S(2)}) %all-to-all-start.4) | async-done | bytes 131104 | tf_op jit(solution)/shard_map/all_to_all | solution.py:215
  122.5 9.9 %all_to_all.50.pieces = bf16[16,16,256]{2,1,0:T(8,128)(2,1)S(1)} all-to-all(bf16[16,16,256]{2,1,0:T(8,128)(2,1)S(1)} %get-tuple-element.13), channel_id=1, replica_groups=mesh['layer'=8,'row'=16,'col'=2] {'row'}, dimensions={0} | all-to-all | bytes 262144 | tf_op jit(solution)/shard_map/all_to_all | solution.py:215
  132.6 10.3 %all_to_all.51.anc = bf16[8,2,16,256]{3,2,1,0:T(8,128)(2,1)S(1)} all-to-all(bf16[8,2,16,256]{3,2,1,0:T(8,128)(2,1)S(1)} %a0.1), channel_id=1, replica_groups=mesh['layer'=8,'row'=16,'col'=2] {'layer'}, dimensions={0} | all-to-all | bytes 262144 | tf_op jit(solution)/shard_map/all_to_all | solution.py:215
  145.6 3.9 %b2.1 = bf16[16,128,256]{2,1,0:T(8,128)(2,1)S(1)} custom-call(s32[1]{0:T(128)} %bitcast.1.refs_0_.where, s32[192]{0:T(256)S(1)} %reshape.200.pat_own.cpat_own, s32[192]{0:T(256)S(1)} %slice.43.pat_oth.cpat_oth, bf16[6,256,2048]{2,1,0:T(8,128)(2,1)S(1)} %bitcast.34, bf16[6,256,2048]{2,1,0:T(8,128)(2,1)} %collective-permute-done.1.oth.coth, ...), custom_call_target="tpu_custom_call" | custom-call | flops 536870912 | bytes 12715524 | tf_op jit(solution)/shard_map/b2/pallas_call | solution.py:85
  149.5 14.8 %all_to_all.52.pieces = bf16[16,128,256]{2,1,0:T(8,128)(2,1)S(1)} all-to-all(bf16[16,128,256]{2,1,0:T(8,128)(2,1)S(1)} %b2.1), channel_id=1, replica_groups=mesh['layer'=8,'row'=16,'col'=2] {'row'}, dimensions={0} | all-to-all | bytes 2097152 | tf_op jit(solution)/shard_map/all_to_all | solution.py:215
  167.2 5.5 %b1.1 = (bf16[16,128,256]{2,1,0:T(8,128)(2,1)S(1)}, bf16[128,256]{1,0:T(8,128)(2,1)S(1)}, bf16[256,128]{1,0:T(8,128)(2,1)S(1)}) custom-call(s32[1]{0:T(128)} %bitcast.row, s32[1]{0:T(128)} %bitcast.1.refs_0_.where, s32[192]{0:T(256)S(1)} %reshape.200.pat_own.cpat_own, s32[192]{0:T(256)S(1)} %slice.43.pat_oth.cpat_oth, ...), custom_call_target="tpu_custom_call" | custom-call | flops 805306368 | bytes 21170440 | tf_op jit(solution)/shard_map/b1/pallas_call | solution.py:85
  172.7 14.5 %all_to_all.53.pieces = bf16[16,128,256]{2,1,0:T(8,128)(2,1)S(1)} all-to-all(bf16[16,128,256]{2,1,0:T(8,128)(2,1)S(1)} %get-tuple-element.15), channel_id=1, replica_groups=mesh['layer'=8,'row'=16,'col'=2] {'row'}, dimensions={0} | all-to-all | bytes 2097152 | tf_op jit(solution)/shard_map/all_to_all | solution.py:215
  187.2 6.0 %b0.1 = (bf16[16,128,256]{2,1,0:T(8,128)(2,1)S(1)}, bf16[128,256]{1,0:T(8,128)(2,1)}, bf16[256,128]{1,0:T(8,128)(2,1)S(1)}) custom-call(s32[1]{0:T(128)} %bitcast.row, s32[1]{0:T(128)} %bitcast.1.refs_0_.where, s32[192]{0:T(256)S(1)} %reshape.200.pat_own.cpat_own, s32[192]{0:T(256)S(1)} %slice.43.pat_oth.cpat_oth, s32[96]{0:T(128)S(1)} %reshape.201.refs_1_.pat_own.lpat_own, ...), custom_call_target="tpu_custom_call" | custom-call | flops 1073741824 | bytes 21235976 | tf_op jit(solution)/shard_map/b0/pallas_call | solution.py:85
  194.2 3.7 %all-to-all-start.9 = ((bf16[16,128,256]{2,1,0:T(8,128)(2,1)}), bf16[16,128,256]{2,1,0:T(8,128)(2,1)S(1)}, u32[]{:S(2)}, u32[]{:S(2)}) async-start(bf16[16,128,256]{2,1,0:T(8,128)(2,1)} %copy-done.12), calls=%async_computation.9 | async-start | bytes 2097152 | tf_op jit(solution)/shard_map/all_to_all | solution.py:215
  197.9 8.4 %collective-permute-start.7 = (bf16[2,256,128]{2,1,0:T(8,128)(2,1)S(1)}, bf16[2,256,128]{2,1,0:T(8,128)(2,1)S(1)}, u32[]{:S(2)}, u32[]{:S(2)}) collective-permute-start(bf16[2,256,128]{2,1,0:T(8,128)(2,1)S(1)} %fa.1), channel_id=1, source_target_pairs={{0,1},{1,0},{2,3},{3,2},{4,5},{5,4},{6,7},{7,6},{8,9},{9,8},{10,11... | collective-permute-start | bytes 393224 | tf_op jit(solution)/shard_map/ppermute | solution.py:312
  210.3 9.6 %collective-permute-start.4 = (bf16[256,128]{1,0:T(8,128)(2,1)S(1)}, bf16[256,128]{1,0:T(8,128)(2,1)S(1)}, u32[]{:S(2)}, u32[]{:S(2)}) collective-permute-start(bf16[256,128]{1,0:T(8,128)(2,1)S(1)} %x0.1), channel_id=1, source_target_pairs={{0,1},{1,0},{2,3},{3,2},{4,5},{5,4},{6,7},{7,6},{8,9},{9,8},{10,11... | collective-permute-start | bytes 196616 | tf_op jit(solution)/shard_map/ppermute | solution.py:312
  (77 shorter events, 48.2 us)
Async XLA Ops:
  0.6 95.1 %copy-start = (f32[2,256,256]{2,1,0:T(8,128)S(1)}, f32[2,256,256]{2,1,0:T(8,128)}, u32[]{:S(2)}) copy-start(f32[2,256,256]{2,1,0:T(8,128)} %param.11) | copy-start | bytes 1572868
  0.6 11.7 %copy-start.13 = (s32[1,2,3,2,16]{4,3,2,1,0:T(2,128)S(1)}, s32[1,2,3,2,16]{4,3,2,1,0:T(2,128)}, u32[]{:S(2)}) copy-start(s32[1,2,3,2,16]{4,3,2,1,0:T(2,128)} %param.16) | copy-start | bytes 2308
  0.7 11.8 %copy-start.15 = (s32[1,2,16]{2,1,0:T(2,128)S(1)}, s32[1,2,16]{2,1,0:T(2,128)}, u32[]{:S(2)}) copy-start(s32[1,2,16]{2,1,0:T(2,128)} %param.17) | copy-start | bytes 388
  0.7 11.9 %copy-start.14 = (s32[1,3,2,16]{3,2,1,0:T(2,128)S(1)}, s32[1,3,2,16]{3,2,1,0:T(2,128)}, u32[]{:S(2)}) copy-start(s32[1,3,2,16]{3,2,1,0:T(2,128)} %param.15) | copy-start | bytes 1156
  0.7 67.2 %collective-permute-start.1 = (bf16[6,256,2048]{2,1,0:T(8,128)(2,1)}, bf16[6,256,2048]{2,1,0:T(8,128)(2,1)}, u32[]{:S(2)}, u32[]{:S(2)}) collective-permute-start(bf16[6,256,2048]{2,1,0:T(8,128)(2,1)} %bitcast.30), channel_id=1, source_target_pairs={{0,1},{1,0},{2,3},{3,2},{4,5},{5,4},{6,7},{7,6},{8,9},{9,8},{10,11... | collective-permute-start | bytes 18874376 | tf_op jit(solution)/shard_map/ppermute | solution.py:235
  4.0 24.7 %collective-permute-start.2 = (bf16[3,256,2048]{2,1,0:T(8,128)(2,1)}, bf16[3,256,2048]{2,1,0:T(8,128)(2,1)}, u32[]{:S(2)}, u32[]{:S(2)}) collective-permute-start(bf16[3,256,2048]{2,1,0:T(8,128)(2,1)} %bitcast.39), channel_id=1, source_target_pairs={{0,1},{1,0},{2,3},{3,2},{4,5},{5,4},{6,7},{7,6},{8,9},{9,8},{10,11... | collective-permute-start | bytes 9437192 | tf_op jit(solution)/shard_map/ppermute | solution.py:234
  7.3 21.4 %all-to-all-start = ((bf16[16,128,256]{2,1,0:T(8,128)(2,1)}), bf16[16,128,256]{2,1,0:T(8,128)(2,1)S(1)}, u32[]{:S(2)}, u32[]{:S(2)}) async-start(bf16[16,128,256]{2,1,0:T(8,128)(2,1)} %y0.1), calls=%async_computation | async-start | bytes 2097152 | tf_op jit(solution)/shard_map/all_to_all | solution.py:215
  12.7 5.9 %collective-permute-start = (s32[320]{0:T(512)S(1)}, s32[320]{0:T(512)S(1)}, u32[]{:S(2)}, u32[]{:S(2)}) collective-permute-start(s32[320]{0:T(512)S(1)} %pad_add_fusion), channel_id=1, source_target_pairs={{0,1},{1,0},{2,3},{3,2},{4,5},{5,4},{6,7},{7,6},{8,9},{9,8},{10,11... | collective-permute-start | bytes 3848 | tf_op jit(solution)/shard_map/ppermute | solution.py:233
  34.5 20.2 %all-to-all-start.1 = ((bf16[16,128,256]{2,1,0:T(8,128)(2,1)}), bf16[16,128,256]{2,1,0:T(8,128)(2,1)S(1)}, u32[]{:S(2)}, u32[]{:S(2)}) async-start(bf16[16,128,256]{2,1,0:T(8,128)(2,1)} %copy-done.10), calls=%async_computation.1 | async-start | bytes 2097152 | tf_op jit(solution)/shard_map/all_to_all | solution.py:215
  60.5 19.0 %all-to-all-start.2 = ((bf16[16,128,256]{2,1,0:T(8,128)(2,1)}), bf16[16,128,256]{2,1,0:T(8,128)(2,1)}, u32[]{:S(2)}, u32[]{:S(2)}) async-start(bf16[16,128,256]{2,1,0:T(8,128)(2,1)} %copy-done.9), calls=%async_computation.2 | async-start | bytes 2097152 | tf_op jit(solution)/shard_map/all_to_all | solution.py:215
  64.9 46.5 %collective-permute-start.3 = (bf16[1,256,2048]{2,1,0:T(8,128)(2,1)}, bf16[1,256,2048]{2,1,0:T(8,128)(2,1)}, u32[]{:S(2)}, u32[]{:S(2)}) collective-permute-start(bf16[1,256,2048]{2,1,0:T(8,128)(2,1)} %own.1), channel_id=1, source_target_pairs={{0,1},{1,0},{2,3},{3,2},{4,5},{5,4},{6,7},{7,6},{8,9},{9,8},{10,11... | collective-permute-start | bytes 3145736 | tf_op jit(solution)/shard_map/ppermute | solution.py:236
  67.9 2.8 %copy-start.1 = (bf16[1,2,3,256,2048]{4,3,2,1,0:T(8,128)(2,1)S(1)}, bf16[1,2,3,256,2048]{4,3,2,1,0:T(8,128)(2,1)}, u32[]{:S(2)}) copy-start(bf16[1,2,3,256,2048]{4,3,2,1,0:T(8,128)(2,1)} %param.13) | copy-start | bytes 18874372
  79.5 2.8 %copy-start.2 = (bf16[1,2,3,256,2048]{4,3,2,1,0:T(8,128)(2,1)S(1)}, bf16[1,2,3,256,2048]{4,3,2,1,0:T(8,128)(2,1)}, u32[]{:S(2)}) copy-start(bf16[1,2,3,256,2048]{4,3,2,1,0:T(8,128)(2,1)} %param.13) | copy-start | bytes 18874372
  87.5 16.1 %all-to-all-start.3 = ((bf16[8,2,16,256]{3,2,1,0:T(8,128)(2,1)}), bf16[8,2,16,256]{3,2,1,0:T(8,128)(2,1)S(1)}, u32[]{:S(2)}, u32[]{:S(2)}) async-start(bf16[8,2,16,256]{3,2,1,0:T(8,128)(2,1)} %c2.1), calls=%async_computation.3 | async-start | bytes 262144 | tf_op jit(solution)/shard_map/all_to_all | solution.py:215
  104.5 13.7 %all-to-all-start.4 = ((bf16[16,16,256]{2,1,0:T(8,128)(2,1)}), bf16[16,16,256]{2,1,0:T(8,128)(2,1)S(1)}, u32[]{:S(2)}, u32[]{:S(2)}) async-start(bf16[16,16,256]{2,1,0:T(8,128)(2,1)} %get-tuple-element.11), calls=%async_computation.4 | async-start | bytes 262144 | tf_op jit(solution)/shard_map/all_to_all | solution.py:215
  145.6 18.7 %copy-start.8 = (bf16[1,3,256,2048]{3,2,1,0:T(8,128)(2,1)S(1)}, bf16[1,3,256,2048]{3,2,1,0:T(8,128)(2,1)}, u32[]{:S(2)}) copy-start(bf16[1,3,256,2048]{3,2,1,0:T(8,128)(2,1)} %param.12) | copy-start | bytes 9437188
  145.6 41.5 %slice-start = ((s8[6291456]{0:T(1024)(128)(4,1)}), s8[4194304]{0:T(1024)(128)(4,1)S(1)}, s32[]{:S(2)}) async-start(s8[6291456]{0:T(1024)(128)(4,1)} %bitcast.36), calls=%async_computation.10 | async-start | bytes 8388608
  164.4 2.8 %copy-start.4 = (bf16[1,2,3,256,2048]{4,3,2,1,0:T(8,128)(2,1)S(1)}, bf16[1,2,3,256,2048]{4,3,2,1,0:T(8,128)(2,1)}, u32[]{:S(2)}) copy-start(bf16[1,2,3,256,2048]{4,3,2,1,0:T(8,128)(2,1)} %param.13) | copy-start | bytes 18874372
  167.2 20.0 %slice-start.1 = ((s8[6291456]{0:T(1024)(128)(4,1)}), s8[2097152]{0:T(1024)(128)(4,1)S(1)}, s32[]{:S(2)}) async-start(s8[6291456]{0:T(1024)(128)(4,1)} %bitcast.36), calls=%async_computation.11 | async-start | bytes 4194304
  194.2 15.8 %all-to-all-start.9 = ((bf16[16,128,256]{2,1,0:T(8,128)(2,1)}), bf16[16,128,256]{2,1,0:T(8,128)(2,1)S(1)}, u32[]{:S(2)}, u32[]{:S(2)}) async-start(bf16[16,128,256]{2,1,0:T(8,128)(2,1)} %copy-done.12), calls=%async_computation.9 | async-start | bytes 2097152 | tf_op jit(solution)/shard_map/all_to_all | solution.py:215
  197.9 9.4 %collective-permute-start.7 = (bf16[2,256,128]{2,1,0:T(8,128)(2,1)S(1)}, bf16[2,256,128]{2,1,0:T(8,128)(2,1)S(1)}, u32[]{:S(2)}, u32[]{:S(2)}) collective-permute-start(bf16[2,256,128]{2,1,0:T(8,128)(2,1)S(1)} %fa.1), channel_id=1, source_target_pairs={{0,1},{1,0},{2,3},{3,2},{4,5},{5,4},{6,7},{7,6},{8,9},{9,8},{10,11... | collective-permute-start | bytes 393224 | tf_op jit(solution)/shard_map/ppermute | solution.py:312
  206.4 2.1 collective-permute-start.6
  208.2 11.8 %collective-permute-start.5 = (bf16[256,128]{1,0:T(8,128)(2,1)S(1)}, bf16[256,128]{1,0:T(8,128)(2,1)S(1)}, u32[]{:S(2)}, u32[]{:S(2)}) collective-permute-start(bf16[256,128]{1,0:T(8,128)(2,1)S(1)} %get-tuple-element.18), channel_id=1, source_target_pairs={{0,1},{1,0},{2,3},{3,2},{4,5},{5,4},{6,7},{7,6},{8,9},{9,8},{10,11... | collective-permute-start | bytes 196616 | tf_op jit(solution)/shard_map/ppermute | solution.py:312
  210.3 10.5 %collective-permute-start.4 = (bf16[256,128]{1,0:T(8,128)(2,1)S(1)}, bf16[256,128]{1,0:T(8,128)(2,1)S(1)}, u32[]{:S(2)}, u32[]{:S(2)}) collective-permute-start(bf16[256,128]{1,0:T(8,128)(2,1)S(1)} %x0.1), channel_id=1, source_target_pairs={{0,1},{1,0},{2,3},{3,2},{4,5},{5,4},{6,7},{7,6},{8,9},{9,8},{10,11... | collective-permute-start | bytes 196616 | tf_op jit(solution)/shard_map/ppermute | solution.py:312
  (8 other events, 12.6 us)

commit v2 on v1

v2 whole, which is shorter than its diff:
```python
import functools

import jax
import jax.numpy as jnp
from jax import lax
from jax.experimental import pallas as pl
from jax.experimental.pallas import tpu as pltpu
from jax.sharding import PartitionSpec as P

F32 = jnp.float32
BF16 = jnp.bfloat16
TILE = 128
SWAP = [(0, 1), (1, 0)]
SLAB_FLOPS = 2 * 256 * 4096 * 128
LEAF, CROSS, TOP = 0, 96, 288

VMEM = pl.BlockSpec(memory_space=pltpu.VMEM)
SMEM = pl.BlockSpec(memory_space=pltpu.SMEM)
HBM = pl.BlockSpec(memory_space=pltpu.HBM)


def nt(a, b):
    return lax.dot_general(a, b, (((1,), (1,)), ((), ())), preferred_element_type=F32)


def nn(a, b):
    return jnp.dot(a, b, preferred_element_type=F32)


class Slab:
    def __init__(self, refs, buffer, sems, index, place):
        self.patterns, self.first = refs[2:4], refs[4] + index * 32
        self.sources = [buffer.at[place, half] for half in range(2)]
        self.copies = [
            pltpu.make_async_copy(refs[half].at[index], buffer.at[place, half], sems.at[place, half])
            for half in range(2)
            if refs[4] != LEAF or half == 0
        ]
        if refs[4] == LEAF:
            self.sources[1] = refs[1].at[index]
        for copy in self.copies:
            copy.start()

    def wait(self):
        for copy in self.copies:
            copy.wait()

    def tile(self, half, upper, at):
        tile = self.sources[half][TILE * upper : TILE * (upper + 1), TILE * at : TILE * (at + 1)]
        kept = self.patterns[half][self.first + 16 * upper + at] != 0
        return lax.select(kept, tile, jnp.zeros_like(tile))

    def block(self, half, block):
        return jnp.concatenate(
            [
                jnp.concatenate([self.tile(half, u, 2 * block + s) for s in range(2)], axis=1)
                for u in range(2)
            ],
            axis=0,
        )

    def line(self, half):
        return jnp.concatenate([self.block(half, b) for b in range(8)], axis=1)


def first_block(where, half):
    return (where[1] if half == 0 else 1 - where[1]) * 8


def product(where, slab, values):
    total = None
    for half in range(2):
        first = pl.multiple_of(first_block(where, half) * 256, 2048)
        term = nn(slab.line(half), values[pl.ds(first, 2048), :])
        total = term if total is None else total + term
    return total


def solved(inverse, residual):
    cut = residual.astype(BF16)
    return jnp.concatenate(
        [nn(inverse[s], cut[TILE * s : TILE * (s + 1)]) for s in range(2)], axis=0
    ).astype(BF16)


def solved_flat(inverse, residual):
    cut = residual.astype(BF16)
    return jnp.concatenate(
        [nt(cut[:, TILE * s : TILE * (s + 1)], inverse[s]) for s in range(2)], axis=1
    ).astype(BF16)


def solved_back(inverse, residual):
    cut = residual.astype(BF16)
    return jnp.concatenate(
        [nn(cut[:, TILE * s : TILE * (s + 1)], inverse[s]) for s in range(2)], axis=1
    ).astype(BF16)


def to_copies(out, value):
    for peer in range(out.shape[0]):
        out[peer] = value


def total_of(pieces):
    total = pieces[0].astype(F32)
    for peer in range(1, pieces.shape[0]):
        total = total + pieces[peer].astype(F32)
    return total


def flipped(value):
    return value.astype(F32).T


def fetch(source, target, sem):
    copy = pltpu.make_async_copy(source, target, sem)
    copy.start()
    return copy


def own_inverse(where, inverse, level, target, sem):
    return fetch(inverse.at[level, pl.ds(2 * where[0], 2)], target, sem)


def own_columns(where, rhs, level, target, sem):
    return fetch(rhs.at[level, :, pl.ds(pl.multiple_of(where[1] * 128, 128), 128)], target, sem)


def forward_kernel(level, slabs, where, own, oth, pat_own, pat_oth, rhs, inverse, *rest):
    *values, out, buffer, sems, rhs_here, inv_here, sem = rest
    small = [
        own_columns(where, rhs, level, rhs_here, sem.at[0]),
        own_inverse(where, inverse, level, inv_here, sem.at[1]),
    ]
    refs = (own, oth, pat_own, pat_oth, LEAF)
    moving = [Slab(refs, buffer, sems, index, place) for place, index in enumerate(slabs)]
    for copy in small:
        copy.wait()
    residual = rhs_here[...]
    for slab, value in zip(moving, values):
        slab.wait()
        residual = residual - product(where, slab, value)
    to_copies(out, solved(inv_here, residual))


def first_kernel(where, rhs, inverse, out, rhs_here, inv_here, sem):
    small = [
        own_columns(where, rhs, 0, rhs_here, sem.at[0]),
        own_inverse(where, inverse, 0, inv_here, sem.at[1]),
    ]
    for copy in small:
        copy.wait()
    to_copies(out, solved(inv_here, rhs_here[...]))


def cross_kernel(where, own, oth, pat_own, pat_oth, *rest):
    *values, out, buffer, sems = rest
    layers, levels, width, _ = out.shape
    refs = (own, oth, pat_own, pat_oth, CROSS)
    order = [(a, s) for s in range(len(values)) for a in range(levels)]
    moving = [
        Slab(refs, buffer, sems, a * len(values) + s, place) for place, (a, s) in enumerate(order)
    ]
    totals = [None] * levels
    for slab, (a, s) in zip(moving, order):
        slab.wait()
        term = product(where, slab, values[s])
        totals[a] = term if totals[a] is None else totals[a] + term
    for a in range(levels):
        out[:, a] = totals[a].T.astype(BF16).reshape(layers, width, -1)


def anc_first_kernel(where, pieces, rhs, inverse, out, left, rhs_here, inv_here, turned, sem):
    copies = [
        own_columns(where, rhs, 0, rhs_here.at[0], sem.at[0]),
        own_columns(where, rhs, 1, rhs_here.at[1], sem.at[1]),
        own_inverse(where, inverse, 0, inv_here, sem.at[2]),
    ]
    for copy in copies:
        copy.wait()
    width = out.shape[1]
    mine = pl.ds(pl.multiple_of(where[2] * width, width), width)
    turned[0] = rhs_here[0].T
    turned[1] = rhs_here[1].T
    to_copies(out, solved_flat(inv_here, turned[0, mine] - total_of(pieces.at[:, 0])))
    left[...] = turned[1, mine] - total_of(pieces.at[:, 1])


def anc_second_kernel(
    where, own, oth, pat_own, pat_oth, values, left, inverse, out, top, buffer, sems, inv_here, sem
):
    copy = own_inverse(where, inverse, 1, inv_here, sem.at[0])
    slab = Slab((own, oth, pat_own, pat_oth, TOP), buffer, sems, 0, 0)
    copy.wait()
    slab.wait()
    residual = left[...]
    for half in range(2):
        first = first_block(where, half)
        for block in range(8):
            residual = residual - nt(values[first + block], slab.block(half, block))
    back = solved_back(inv_here, solved_flat(inv_here, residual).astype(F32))
    top[...] = back
    for half in range(2):
        first = first_block(where, half)
        for block in range(8):
            out[first + block] = nn(back, slab.block(half, block)).astype(BF16)


def anc_third_kernel(where, pieces, lower, top, inverse, out, inv_here, sem):
    own_inverse(where, inverse, 0, inv_here, sem.at[0]).wait()
    residual = lower[where[0]].astype(F32) - total_of(pieces)
    value = solved_back(inv_here, residual)
    for peer in range(out.shape[0]):
        out[peer, 0] = value
        out[peer, 1] = top[...]


def back_sums(where, moving, values, out):
    for half in range(2):
        first = first_block(where, half)
        for block in range(8):
            total = None
            for slab, value in zip(moving, values):
                term = nn(value, slab.block(half, block))
                total = term if total is None else total + term
            out[first + block] = total.astype(BF16)


def of_layers(pieces, at):
    value = pieces[:, at]
    return value.reshape(-1, value.shape[-1])


def back_first_kernel(slabs, where, own, oth, pat_own, pat_oth, anc, out, natural, buffer, sems):
    refs = (own, oth, pat_own, pat_oth, CROSS)
    moving = [Slab(refs, buffer, sems, index, place) for place, index in enumerate(slabs)]
    values = [of_layers(anc, at) for at in range(2)]
    for at in range(2):
        natural[at] = flipped(values[at]).astype(BF16)
    for slab in moving:
        slab.wait()
    back_sums(where, moving, values, out)


def back_kernel(level, cross_slabs, leaf_slabs, where, cross, leaf, anc, pieces, value, inverse, *rest):
    *earlier, out, solution, natural, buffer, sems, inv_here, sem = rest
    copy = own_inverse(where, inverse, level, inv_here, sem.at[0])
    moving = [Slab(leaf, buffer, sems, index, place) for place, index in enumerate(leaf_slabs)]
    moving += [
        Slab(cross, buffer, sems, index, len(leaf_slabs) + place)
        for place, index in enumerate(cross_slabs)
    ]
    copy.wait()
    now = solved_back(inv_here, flipped(value[where[0]]) - total_of(pieces))
    solution[...] = now
    natural[...] = flipped(now).astype(BF16)
    values = [now, *(e[...] for e in earlier), *(of_layers(anc, at) for at in range(2))]
    for slab in moving:
        slab.wait()
    back_sums(where, moving, values, out)


def back_body(level, cross_slabs, leaf_slabs, where, *refs):
    patterns, rest = refs[4:6], refs[6:]
    cross, leaf = (*refs[:2], *patterns, CROSS), (*refs[2:4], *patterns, LEAF)
    back_kernel(level, cross_slabs, leaf_slabs, where, cross, leaf, *rest)


def last_kernel(where, pieces, value, inverse, second, third, anc, out, inv_here, sem):
    own_inverse(where, inverse, 0, inv_here, sem.at[0]).wait()
    now = solved_back(inv_here, flipped(value[where[0]]) - total_of(pieces))
    out[0] = flipped(now).astype(BF16)
    out[1] = second[...]
    out[2] = third[...]
    out[3] = anc[0]
    out[4] = anc[1]


def join_kernel(where, mine, theirs, leaf, anc, sem):
    copies = []
    for at in range(5):
        for side, half in enumerate((mine, theirs)):
            col = where[1] if side == 0 else 1 - where[1]
            columns = pl.ds(pl.multiple_of(col * 128, 128), 128)
            target = leaf.at[0, at, :, columns] if at < 3 else anc.at[at - 3, :, columns]
            copies.append(fetch(half.at[at], target, sem.at[at, side]))
    for copy in copies:
        copy.wait()


def shape(*dims, dtype=BF16):
    return jax.ShapeDtypeStruct(dims, dtype)


def slab_scratch(count):
    return [pltpu.VMEM((count, 2, 256, 2048), BF16), pltpu.SemaphoreType.DMA((count, 2))]


RHS_SCRATCH = pltpu.VMEM((256, 128), F32)
INV_SCRATCH = pltpu.VMEM((2, TILE, TILE), BF16)


def sem_scratch(count):
    return pltpu.SemaphoreType.DMA((count,))


def call(name, body, outs, operands, scratch, slabs=0, out_specs=None, limit=8):
    specs, arrays = [], []
    for x in operands:
        far = isinstance(x, tuple)
        x = pltpu.with_memory_space_constraint(x[1], pltpu.HBM) if far else x
        specs.append(HBM if far else SMEM if x.dtype == jnp.int32 else VMEM)
        arrays.append(x)
    single = not isinstance(outs, list)
    shapes = [outs] if single else outs
    made = pl.pallas_call(
        body,
        out_shape=shapes,
        in_specs=specs,
        out_specs=out_specs or [VMEM] * len(shapes),
        scratch_shapes=scratch,
        compiler_params=pltpu.CompilerParams(vmem_limit_bytes=limit * 1024 * 1024),
        cost_estimate=pl.CostEstimate(
            flops=max(1, slabs) * SLAB_FLOPS, bytes_accessed=2**21 * max(1, slabs), transcendentals=0
        ),
        name=name,
    )(*arrays)
    return made[0] if single else made


def spread(x, axis):
    return lax.all_to_all(x, axis, split_axis=0, concat_axis=0, tiled=True)


def local(
    leaf_rhs, anc_rhs, leaf_tiles, cross_tiles, top_tiles, leaf_pattern, cross_pattern, top_pattern,
    leaf_inverse, anc_inverse,
):
    layers = lax.axis_size("layer")
    rows = lax.axis_size("row")
    width = 128 // layers
    where = jnp.stack(
        [lax.axis_index(axis).astype(jnp.int32) for axis in ("row", "col", "layer")]
    )
    patterns = jnp.concatenate(
        [leaf_pattern.reshape(-1), cross_pattern.reshape(-1), top_pattern.reshape(-1)]
    )
    pat_other = lax.ppermute(patterns, "col", SWAP)
    tiles = (leaf_tiles[0], cross_tiles[0].reshape(6, 256, 2048), top_tiles)
    leaf_other, cross_other, top_other = (lax.ppermute(x, "col", SWAP) for x in tiles)
    leaf_own, cross_own, top_own = (("hbm", x) for x in tiles)
    rhs, rhs_anc = ("hbm", leaf_rhs[0]), ("hbm", anc_rhs)
    inv, inv_anc = ("hbm", leaf_inverse[0]), ("hbm", anc_inverse)
    small = [RHS_SCRATCH, INV_SCRATCH, sem_scratch(2)]

    wide = shape(rows, 256, 128)
    flat = shape(rows, 128, 256)
    thin = shape(rows, width, 256)

    def gathered(block):
        return spread(block, "row").reshape(rows * 256, 128)

    block = call("y0", first_kernel, wide, (where, rhs, inv), small)
    block, pat_other = lax.optimization_barrier((block, pat_other))
    patterns = (patterns, pat_other)
    y0 = gathered(block)
    leaf = (leaf_own, leaf_other, *patterns)
    block = call(
        "y1", functools.partial(forward_kernel, 1, (0,)), wide, (where, *leaf, rhs, inv, y0),
        [*slab_scratch(1), *small], 1, limit=12,
    )
    block, top_other = lax.optimization_barrier((block, top_other))
    y1 = gathered(block)
    block = call(
        "y2", functools.partial(forward_kernel, 2, (1, 2)), wide, (where, *leaf, rhs, inv, y0, y1),
        [*slab_scratch(2), *small], 2, limit=16,
    )
    block, cross_other = lax.optimization_barrier((block, cross_other))
    y2 = gathered(block)
    cross = (cross_own, ("hbm", cross_other), *patterns)
    lower = spread(
        call("zs", cross_kernel, shape(layers, 2, width, 256), (where, *cross, y0, y1, y2),
             slab_scratch(6), 6, limit=24),
        "layer",
    )
    z0, left = call(
        "z0", anc_first_kernel, [thin, shape(width, 256, dtype=F32)], (where, lower, rhs_anc, inv_anc),
        [pltpu.VMEM((2, 256, 128), F32), INV_SCRATCH, pltpu.VMEM((2, 128, 256), F32), sem_scratch(3)],
    )
    z0 = spread(z0, "row")
    top = (top_own, ("hbm", top_other), *patterns)
    pieces, high = call(
        "z1", anc_second_kernel, [thin, shape(width, 256)], (where, *top, z0, left, inv_anc),
        [*slab_scratch(1), INV_SCRATCH, sem_scratch(1)], 1,
    )
    pieces = spread(pieces, "row")
    anc = call(
        "a0", anc_third_kernel, shape(layers, 2, width, 256), (where, pieces, z0, high, inv_anc),
        [INV_SCRATCH, sem_scratch(1)],
    )
    anc = spread(anc, "layer")
    pieces, natural = call(
        "b2", functools.partial(back_first_kernel, (2, 5)), [flat, shape(2, 256, 128)], (where, *cross, anc),
        slab_scratch(2), 2, limit=12,
    )
    pieces = spread(pieces, "row")
    both = (cross_own, ("hbm", cross_other), leaf_own, leaf_other, *patterns)
    solved_outs = [flat, shape(128, 256), shape(256, 128)]
    y2, y1, y0 = (y.reshape(rows, 256, 128) for y in (y2, y1, y0))
    pieces, x2, n2 = call(
        "b1", functools.partial(back_body, 2, (1, 4), (2,)), solved_outs,
        (where, *both, anc, pieces, y2, inv), [*slab_scratch(3), INV_SCRATCH, sem_scratch(1)], 3, limit=20,
    )
    pieces = spread(pieces, "row")
    pieces, _, n1 = call(
        "b0", functools.partial(back_body, 1, (0, 3), (0, 1)), solved_outs,
        (where, *both, anc, pieces, y1, inv, x2), [*slab_scratch(4), INV_SCRATCH, sem_scratch(1)], 4, limit=20,
    )
    pieces = spread(pieces, "row")
    mine = call(
        "x0", last_kernel, shape(5, 256, 128), (where, pieces, y0, inv, n1, n2, natural),
        [INV_SCRATCH, sem_scratch(1)],
    )
    theirs = lax.ppermute(mine, "col", SWAP)
    return tuple(
        call("join", join_kernel, [shape(1, 3, 256, 256), shape(2, 256, 256)], (where, mine, theirs),
             [pltpu.SemaphoreType.DMA((5, 2))], out_specs=[HBM, HBM])
    )


def solution(mesh):
    in_specs = (
        P("layer", None, "row", None),
        P(None, "row", None),
        P("layer", None, "row", "col"),
        P("layer", None, None, "row", "col"),
        P(None, "row", "col"),
        P("layer", None, "row", "col"),
        P("layer", None, None, "row", "col"),
        P(None, "row", "col"),
        P("layer", None, None, None, None),
        P(),
    )
    out_specs = (P("layer", None, "row", None), P(None, "row", None))
    return jax.shard_map(local, mesh=mesh, in_specs=in_specs, out_specs=out_specs, check_vma=False)
```

time: 223 us -> 218 us (0.978)
  blocking collectives: 49.5 us -> 148 us
  starting transfers between devices: 58.1 us -> 16.5 us
  waiting for transfers between devices: 43.3 us -> 10.9 us
  local copies, waits for them, and re-layouts: 24.5 us -> 2.3 us
  Pallas kernels: 43.6 us -> 38.5 us
    all_to_all x4 -> x10, blocking collectives: 49.5 us -> 148 us  [spread(): return lax.all_to_all(x, axis, split_axis=0, concat_axis=0, tiled=True)]
    all_to_all x6 -> x0, waiting for transfers between devices: 36.4 us -> none  [spread(): return lax.all_to_all(x, axis, split_axis=0, concat_axis=0, tiled=True)]
    all_to_all x6 -> x0, starting transfers between devices: 32.6 us -> none  [spread(): return lax.all_to_all(x, axis, split_axis=0, concat_axis=0, tiled=True)]
    unnamed x37 -> x0, local copies, waits for them, and re-layouts: 21.1 us -> none
    ppermute x7 -> x4, starting transfers between devices: 24.9 us -> 16.1 us  [the longest x1 12.6 us: local(): theirs = lax.ppermute(mine, 'col', SWAP)]
    pallas_call x15 -> x12, Pallas kernels: 43.6 us -> 38.5 us  [call(): pl.pallas_call(body, out_shape=shapes, in_specs=specs, out_specs=out_spec...]
    ppermute x1, waiting for transfers between devices: 5.16 us -> 9.68 us  [local(): pat_other = lax.ppermute(patterns, 'col', SWAP)]
    squeeze x3 -> x0, local copies, waits for them, and re-layouts: 2.88 us -> none  [the longest x1 1.07 us: local(): rhs[2]]
  transfers between devices with their start and end apart: 14 -> 5, of which waited for: 9 -> 2; matrix products, arithmetic and copies ran while one was open for 2% -> 1% of each run, Pallas kernels for 11% -> 4%
where the time goes in v2:
time: 218 us; the launch traced here: 217 us
  blocking collectives  148 us (68%)
  Pallas kernels  38.5 us (18%)
  starting transfers between devices  16.5 us (8%)
  waiting for transfers between devices  10.9 us (5%)
  local copies, waits for them, and re-layouts  2.3 us (1%)
    all_to_all x10, blocking collectives, spread(): return lax.all_to_all(x, axis, split_axis=0, concat_axis=0, tiled=True)  148 us
    pallas_call x12, Pallas kernels, call(): pl.pallas_call(body, out_shape=shapes, in_specs=specs, out_specs=out_spec...  38.5 us
    ppermute x1, starting transfers between devices, local(): theirs = lax.ppermute(mine, 'col', SWAP)  12.6 us
    ppermute x1, waiting for transfers between devices, local(): pat_other = lax.ppermute(patterns, 'col', SWAP)  9.68 us
  transfers between devices with their start and end apart: 5, of which 2 were waited for; matrix products, arithmetic and copies ran while one was open for 1% of the time, Pallas kernels for 4%

profile of v2, /device:TPU:1, one launch (start us, length us, event | category | flops | bytes accessed | tf_op | source)
XLA Modules:
  0.0 217.0 jit_solution(7012538146741001592)
XLA Ops:
  0.6 3.3 %collective-permute-start.3 = (bf16[6,256,2048]{2,1,0:T(8,128)(2,1)}, bf16[6,256,2048]{2,1,0:T(8,128)(2,1)}, u32[]{:S(2)}, u32[]{:S(2)}) collective-permute-start(bf16[6,256,2048]{2,1,0:T(8,128)(2,1)} %bitcast.22), channel_id=1, source_target_pairs={{0,1},{1,0},{2,3},{3,2},{4,5},{5,4},{6,7},{7,6},{8,9},{9,8},{10,11... | collective-permute-start | bytes 18874376 | tf_op jit(solution)/shard_map/ppermute | solution.py:351
  7.0 1.7 y0.1
  8.7 9.7 %collective-permute-done.1.pat_oth.refs_5_ = s32[320]{0:T(512)S(1)} collective-permute-done((s32[320]{0:T(512)S(1)}, s32[320]{0:T(512)S(1)}, u32[]{:S(2)}, u32[]{:S(2)}) %collective-permute-start.1) | collective-permute-done | bytes 1312 | tf_op jit(solution)/shard_map/ppermute | solution.py:349
  18.4 21.2 %all_to_all.50.value = bf16[16,256,128]{2,1,0:T(8,128)(2,1)S(1)} all-to-all(bf16[16,256,128]{2,1,0:T(8,128)(2,1)S(1)} %y0.1), channel_id=1, replica_groups=mesh['layer'=8,'row'=16,'col'=2] {'row'}, dimensions={0} | all-to-all | bytes 2097152 | tf_op jit(solution)/shard_map/all_to_all | solution.py:333
  39.6 2.9 %y1.1 = bf16[16,256,128]{2,1,0:T(8,128)(2,1)S(1)} custom-call(s32[3]{0:T(128)S(1)} %pad_add_fusion.1.where, bf16[3,256,2048]{2,1,0:T(8,128)(2,1)} %bitcast.28, bf16[3,256,2048]{2,1,0:T(8,128)(2,1)S(1)} %collective-permute-done.oth.refs_3_, s32[320]{0:T(512)S(1)} %pad_add_fusion.pat_own.refs_4_, s32[320]{0:T(512)S(1)} %collective-permute-done.1.pat_oth.refs_5_, ...), custom_call_target="tpu_custom_call" | custom-call | flops 268435456 | bytes 2097152 | tf_op jit(solution)/shard_map/y1/pallas_call | solution.py:317
  42.5 19.1 %all_to_all.51.refs_8_ = bf16[16,256,128]{2,1,0:T(8,128)(2,1)S(1)} all-to-all(bf16[16,256,128]{2,1,0:T(8,128)(2,1)S(1)} %y1.1), channel_id=1, replica_groups=mesh['layer'=8,'row'=16,'col'=2] {'row'}, dimensions={0} | all-to-all | bytes 2097152 | tf_op jit(solution)/shard_map/all_to_all | solution.py:333
  61.6 3.6 %y2.1 = bf16[16,256,128]{2,1,0:T(8,128)(2,1)S(1)} custom-call(s32[3]{0:T(128)S(1)} %pad_add_fusion.1.where, bf16[3,256,2048]{2,1,0:T(8,128)(2,1)} %bitcast.29, bf16[3,256,2048]{2,1,0:T(8,128)(2,1)S(1)} %collective-permute-done.oth.refs_3_, s32[320]{0:T(512)S(1)} %pad_add_fusion.pat_own.refs_4_, s32[320]{0:T(512)S(1)} %collective-permute-done.1.pat_oth.refs_5_, ...), custom_call_target="tpu_custom_call" | custom-call | flops 536870912 | bytes 4194304 | tf_op jit(solution)/shard_map/y2/pallas_call | solution.py:317
  65.2 18.5 %all_to_all.52.refs_8_ = bf16[16,256,128]{2,1,0:T(8,128)(2,1)S(1)} all-to-all(bf16[16,256,128]{2,1,0:T(8,128)(2,1)S(1)} %y2.1), channel_id=1, replica_groups=mesh['layer'=8,'row'=16,'col'=2] {'row'}, dimensions={0} | all-to-all | bytes 2097152 | tf_op jit(solution)/shard_map/all_to_all | solution.py:333
  83.7 6.7 %zs.1 = bf16[8,2,16,256]{3,2,1,0:T(8,128)(2,1)S(1)} custom-call(s32[3]{0:T(128)S(1)} %pad_add_fusion.1.where, bf16[6,256,2048]{2,1,0:T(8,128)(2,1)} %bitcast.23, bf16[6,256,2048]{2,1,0:T(8,128)(2,1)} %collective-permute-done.3.oth.refs_1_, s32[320]{0:T(512)S(1)} %pad_add_fusion.pat_own.refs_4_, s32[320]{0:T(512)S(1)} %collective-permute-done.1.pat_oth.refs_5_, ...), custom_call_target="tpu_custom_call" | custom-call | flops 1610612736 | bytes 12582912 | tf_op jit(solution)/shard_map/zs/pallas_call | solution.py:317
  90.4 16.0 %all_to_all.53.pieces = bf16[8,2,16,256]{3,2,1,0:T(8,128)(2,1)S(1)} all-to-all(bf16[8,2,16,256]{3,2,1,0:T(8,128)(2,1)S(1)} %zs.1), channel_id=1, replica_groups=mesh['layer'=8,'row'=16,'col'=2] {'layer'}, dimensions={0} | all-to-all | bytes 262144 | tf_op jit(solution)/shard_map/all_to_all | solution.py:333
  106.3 1.8 z0.1
  108.1 9.4 %all_to_all.54.values.lower = bf16[16,16,256]{2,1,0:T(8,128)(2,1)S(1)} all-to-all(bf16[16,16,256]{2,1,0:T(8,128)(2,1)S(1)} %get-tuple-element.25), channel_id=1, replica_groups=mesh['layer'=8,'row'=16,'col'=2] {'row'}, dimensions={0} | all-to-all | bytes 262144 | tf_op jit(solution)/shard_map/all_to_all | solution.py:333
  117.5 3.4 %z1.1 = (bf16[16,16,256]{2,1,0:T(8,128)(2,1)S(1)}, bf16[16,256]{1,0:T(8,128)(2,1)S(1)}) custom-call(s32[3]{0:T(128)S(1)} %pad_add_fusion.1.where, bf16[1,256,2048]{2,1,0:T(8,128)(2,1)} %own.1, bf16[1,256,2048]{2,1,0:T(8,128)(2,1)} %collective-permute-done.2.oth, s32[320]{0:T(512)S(1)} %pad_add_fusion.pat_own.refs_4_, ...), custom_call_target="tpu_custom_call" | custom-call | flops 268435456 | bytes 2097152 | tf_op jit(solution)/shard_map/z1/pallas_call | solution.py:317
  121.0 9.6 %all_to_all.55.pieces = bf16[16,16,256]{2,1,0:T(8,128)(2,1)S(1)} all-to-all(bf16[16,16,256]{2,1,0:T(8,128)(2,1)S(1)} %get-tuple-element.27), channel_id=1, replica_groups=mesh['layer'=8,'row'=16,'col'=2] {'row'}, dimensions={0} | all-to-all | bytes 262144 | tf_op jit(solution)/shard_map/all_to_all | solution.py:333
  130.6 1.5 a0.1
  132.2 10.3 %all_to_all.56.anc.refs_6_ = bf16[8,2,16,256]{3,2,1,0:T(8,128)(2,1)S(1)} all-to-all(bf16[8,2,16,256]{3,2,1,0:T(8,128)(2,1)S(1)} %a0.1), channel_id=1, replica_groups=mesh['layer'=8,'row'=16,'col'=2] {'layer'}, dimensions={0} | all-to-all | bytes 262144 | tf_op jit(solution)/shard_map/all_to_all | solution.py:333
  142.5 3.7 %b2.1 = (bf16[16,128,256]{2,1,0:T(8,128)(2,1)S(1)}, bf16[2,256,128]{2,1,0:T(8,128)(2,1)S(1)}) custom-call(s32[3]{0:T(128)S(1)} %pad_add_fusion.1.where, bf16[6,256,2048]{2,1,0:T(8,128)(2,1)} %bitcast.24, bf16[6,256,2048]{2,1,0:T(8,128)(2,1)} %collective-permute-done.3.oth.refs_1_, s32[320]{0:T(512)S(1)} %pad_add_fusion.pat_own.refs_4_, ...), custom_call_target="tpu_custom_call" | custom-call | flops 536870912 | bytes 4194304 | tf_op jit(solution)/shard_map/b2/pallas_call | solution.py:317
  146.2 14.6 %all_to_all.57.refs_7_ = bf16[16,128,256]{2,1,0:T(8,128)(2,1)S(1)} all-to-all(bf16[16,128,256]{2,1,0:T(8,128)(2,1)S(1)} %get-tuple-element.29), channel_id=1, replica_groups=mesh['layer'=8,'row'=16,'col'=2] {'row'}, dimensions={0} | all-to-all | bytes 2097152 | tf_op jit(solution)/shard_map/all_to_all | solution.py:333
  160.8 4.4 %b1.1 = (bf16[16,128,256]{2,1,0:T(8,128)(2,1)S(1)}, bf16[128,256]{1,0:T(8,128)(2,1)S(1)}, bf16[256,128]{1,0:T(8,128)(2,1)S(1)}) custom-call(s32[3]{0:T(128)S(1)} %pad_add_fusion.1.where, bf16[6,256,2048]{2,1,0:T(8,128)(2,1)} %bitcast.25, bf16[6,256,2048]{2,1,0:T(8,128)(2,1)} %collective-permute-done.3.oth.refs_1_, bf16[3,256,2048]{2,1,0:T(8,128)(2,1)} %bitcast.30, ...), custom_call_target="tpu_custom_call" | custom-call | flops 805306368 | bytes 6291456 | tf_op jit(solution)/shard_map/b1/pallas_call | solution.py:317
  165.2 14.5 %all_to_all.58.refs_7_ = bf16[16,128,256]{2,1,0:T(8,128)(2,1)S(1)} all-to-all(bf16[16,128,256]{2,1,0:T(8,128)(2,1)S(1)} %get-tuple-element.30), channel_id=1, replica_groups=mesh['layer'=8,'row'=16,'col'=2] {'row'}, dimensions={0} | all-to-all | bytes 2097152 | tf_op jit(solution)/shard_map/all_to_all | solution.py:333
  179.7 5.6 %b0.1 = (bf16[16,128,256]{2,1,0:T(8,128)(2,1)S(1)}, bf16[128,256]{1,0:T(8,128)(2,1)}, bf16[256,128]{1,0:T(8,128)(2,1)S(1)}) custom-call(s32[3]{0:T(128)S(1)} %pad_add_fusion.1.where, bf16[6,256,2048]{2,1,0:T(8,128)(2,1)} %bitcast.26, bf16[6,256,2048]{2,1,0:T(8,128)(2,1)} %collective-permute-done.3.oth.refs_1_, bf16[3,256,2048]{2,1,0:T(8,128)(2,1)} %bitcast.31, ...), custom_call_target="tpu_custom_call" | custom-call | flops 1073741824 | bytes 8388608 | tf_op jit(solution)/shard_map/b0/pallas_call | solution.py:317
  185.3 14.5 %all_to_all.59.pieces = bf16[16,128,256]{2,1,0:T(8,128)(2,1)S(1)} all-to-all(bf16[16,128,256]{2,1,0:T(8,128)(2,1)S(1)} %get-tuple-element.32), channel_id=1, replica_groups=mesh['layer'=8,'row'=16,'col'=2] {'row'}, dimensions={0} | all-to-all | bytes 2097152 | tf_op jit(solution)/shard_map/all_to_all | solution.py:333
  199.8 1.8 x0.1.mine
  201.5 12.6 %collective-permute-start.4 = (bf16[5,256,128]{2,1,0:T(8,128)(2,1)S(1)}, bf16[5,256,128]{2,1,0:T(8,128)(2,1)S(1)}, u32[]{:S(2)}, u32[]{:S(2)}) collective-permute-start(bf16[5,256,128]{2,1,0:T(8,128)(2,1)S(1)} %x0.1.mine), channel_id=1, source_target_pairs={{0,1},{1,0},{2,3},{3,2},{4,5},{5,4},{6,7},{7,6},{8,9},{9,8},{10,11... | collective-permute-start | bytes 983048 | tf_op jit(solution)/shard_map/ppermute | solution.py:425
  (13 shorter events, 5.8 us)
Async XLA Ops:
  0.6 64.5 %collective-permute-start.3 = (bf16[6,256,2048]{2,1,0:T(8,128)(2,1)}, bf16[6,256,2048]{2,1,0:T(8,128)(2,1)}, u32[]{:S(2)}, u32[]{:S(2)}) collective-permute-start(bf16[6,256,2048]{2,1,0:T(8,128)(2,1)} %bitcast.22), channel_id=1, source_target_pairs={{0,1},{1,0},{2,3},{3,2},{4,5},{5,4},{6,7},{7,6},{8,9},{9,8},{10,11... | collective-permute-start | bytes 18874376 | tf_op jit(solution)/shard_map/ppermute | solution.py:351
  3.9 35.7 %collective-permute-start = (bf16[3,256,2048]{2,1,0:T(8,128)(2,1)}, bf16[3,256,2048]{2,1,0:T(8,128)(2,1)S(1)}, u32[]{:S(2)}, u32[]{:S(2)}) collective-permute-start(bf16[3,256,2048]{2,1,0:T(8,128)(2,1)} %bitcast.27), channel_id=1, source_target_pairs={{0,1},{1,0},{2,3},{3,2},{4,5},{5,4},{6,7},{7,6},{8,9},{9,8},{10,11... | collective-permute-start | bytes 9437192 | tf_op jit(solution)/shard_map/ppermute | solution.py:351
  6.4 12.0 %collective-permute-start.1 = (s32[320]{0:T(512)S(1)}, s32[320]{0:T(512)S(1)}, u32[]{:S(2)}, u32[]{:S(2)}) collective-permute-start(s32[320]{0:T(512)S(1)} %pad_add_fusion.pat_own.refs_4_), channel_id=1, source_target_pairs={{0,1},{1,0},{2,3},{3,2},{4,5},{5,4},{6,7},{7,6},{8,9},{9,8},{10,11... | collective-permute-start | bytes 3848 | tf_op jit(solution)/shard_map/ppermute | solution.py:349
  6.8 35.6 %collective-permute-start.2 = (bf16[1,256,2048]{2,1,0:T(8,128)(2,1)}, bf16[1,256,2048]{2,1,0:T(8,128)(2,1)}, u32[]{:S(2)}, u32[]{:S(2)}) collective-permute-start(bf16[1,256,2048]{2,1,0:T(8,128)(2,1)} %own.1), channel_id=1, source_target_pairs={{0,1},{1,0},{2,3},{3,2},{4,5},{5,4},{6,7},{7,6},{8,9},{9,8},{10,11... | collective-permute-start | bytes 3145736 | tf_op jit(solution)/shard_map/ppermute | solution.py:351
  201.5 13.8 %collective-permute-start.4 = (bf16[5,256,128]{2,1,0:T(8,128)(2,1)S(1)}, bf16[5,256,128]{2,1,0:T(8,128)(2,1)S(1)}, u32[]{:S(2)}, u32[]{:S(2)}) collective-permute-start(bf16[5,256,128]{2,1,0:T(8,128)(2,1)S(1)} %x0.1.mine), channel_id=1, source_target_pairs={{0,1},{1,0},{2,3},{3,2},{4,5},{5,4},{6,7},{7,6},{8,9},{9,8},{10,11... | collective-permute-start | bytes 983048 | tf_op jit(solution)/shard_map/ppermute | solution.py:425

commit v3 on v2

v3 whole, which is shorter than its diff:
```python
import functools

import jax
import jax.numpy as jnp
from jax import lax
from jax.experimental import pallas as pl
from jax.experimental.pallas import tpu as pltpu
from jax.sharding import PartitionSpec as P

F32 = jnp.float32
BF16 = jnp.bfloat16
TILE = 128
LINES = 16
SWAP = [(0, 1), (1, 0)]
SLAB_FLOPS = 2 * 256 * 4096 * 128

VMEM = pl.BlockSpec(memory_space=pltpu.VMEM)
SMEM = pl.BlockSpec(memory_space=pltpu.SMEM)
HBM = pl.BlockSpec(memory_space=pltpu.HBM)


def nt(a, b):
    return lax.dot_general(a, b, (((1,), (1,)), ((), ())), preferred_element_type=F32)


def nn(a, b):
    return jnp.dot(a, b, preferred_element_type=F32)


def packed(value):
    return jnp.concatenate(
        [value[LINES * k : LINES * (k + 1)] for k in range(value.shape[0] // LINES)], axis=1
    )


def unpacked(value, width):
    return jnp.concatenate(
        [value[:, width * k : width * (k + 1)] for k in range(value.shape[1] // width)], axis=0
    )


def first_block(half):
    col = lax.axis_index("col")
    return (col if half == 0 else 1 - col) * 8


def product(pair, slab, values):
    total = None
    for half in range(2):
        first = first_block(half)
        column = jnp.concatenate([unpacked(values[first + b], TILE) for b in range(8)], axis=0)
        term = nn(pair[half][slab], column)
        total = term if total is None else total + term
    return total


def solved(inverse, residual):
    cut = residual.astype(BF16)
    return jnp.concatenate(
        [nn(inverse[s], cut[TILE * s : TILE * (s + 1)]) for s in range(2)], axis=0
    ).astype(BF16)


def solved_flat(inverse, residual):
    cut = residual.astype(BF16)
    return jnp.concatenate(
        [nt(cut[:, TILE * s : TILE * (s + 1)], inverse[s]) for s in range(2)], axis=1
    ).astype(BF16)


def solved_back(inverse, residual):
    cut = residual.astype(BF16)
    return jnp.concatenate(
        [nn(cut[:, TILE * s : TILE * (s + 1)], inverse[s]) for s in range(2)], axis=1
    ).astype(BF16)


def to_copies(out, value):
    for peer in range(out.shape[0]):
        out[peer] = value


def total_of(pieces):
    total = pieces[0].astype(F32)
    for peer in range(1, pieces.shape[0]):
        total = total + pieces[peer].astype(F32)
    return total


def flipped(value):
    return value.astype(F32).T


def fetch(source, target, sem):
    copy = pltpu.make_async_copy(source, target, sem)
    copy.start()
    return copy


def mask_in_place(tiles, slab, pattern, at):
    for upper in range(2):
        for k in range(16):
            place = (slab, pl.ds(TILE * upper, TILE), pl.ds(TILE * k, TILE))
            tile = tiles[place]
            tiles[place] = lax.select(pattern[(*at, upper, k)] != 0, tile, jnp.zeros_like(tile))


def first_kernel(
    leaf_rhs, anc_rhs, leaf_tiles, cross_tiles, top_tiles, leaf_pattern, cross_pattern, top_pattern,
    leaf_inverse, anc_inverse,
    block, leaf, cross, top, rhs, rhs_anc, inv, inv_anc, rhs_here, anc_here, turned, sem, tile_sem,
):
    row, col, layer = (lax.axis_index(axis) for axis in ("row", "col", "layer"))
    columns = pl.ds(pl.multiple_of(col * 128, 128), 128)
    two = pl.ds(2 * row, 2)
    urgent = [
        fetch(leaf_rhs.at[0, 0, :, columns], rhs_here, sem.at[0]),
        fetch(leaf_inverse.at[0, :, two], inv, sem.at[1]),
    ]
    moving = [fetch(leaf_tiles.at[0, p], leaf.at[p], tile_sem.at[p]) for p in range(3)]
    moving += [
        fetch(cross_tiles.at[0, a, s], cross.at[3 * a + s], tile_sem.at[3 + 3 * a + s])
        for a in range(2)
        for s in range(3)
    ]
    moving += [fetch(top_tiles.at[0], top.at[0], tile_sem.at[9])]
    later = [
        fetch(leaf_rhs.at[0, pl.ds(1, 2), :, columns], rhs, sem.at[2]),
        fetch(anc_rhs.at[:, :, columns], anc_here, sem.at[3]),
        fetch(anc_inverse.at[:, two], inv_anc, sem.at[4]),
    ]
    for copy in urgent:
        copy.wait()
    to_copies(block, packed(solved(inv.at[0], rhs_here[...])))
    for p in range(3):
        moving[p].wait()
        mask_in_place(leaf, p, leaf_pattern, (0, p))
    for a in range(2):
        for s in range(3):
            moving[3 + 3 * a + s].wait()
            mask_in_place(cross, 3 * a + s, cross_pattern, (0, a, s))
    moving[9].wait()
    mask_in_place(top, 0, top_pattern, (0,))
    for copy in later:
        copy.wait()
    width = rhs_anc.shape[1]
    mine = pl.ds(pl.multiple_of(layer * width, width), width)
    for a in range(2):
        turned[a] = anc_here[a].T
        rhs_anc[a] = turned[a, mine]


def forward_kernel(level, slabs, own, oth, rhs, inverse, *rest):
    *values, out = rest
    residual = rhs[level - 1]
    for slab, value in zip(slabs, values):
        residual = residual - product((own, oth), slab, value)
    to_copies(out, packed(solved(inverse.at[level], residual)))


def cross_kernel(own, oth, *rest):
    *values, out = rest
    layers, width, _ = out.shape
    for a in range(2):
        total = None
        for s, value in enumerate(values):
            term = product((own, oth), a * len(values) + s, value)
            total = term if total is None else total + term
        out[:, :, 256 * a : 256 * (a + 1)] = total.T.astype(BF16).reshape(layers, width, -1)


def anc_first_kernel(pieces, rhs, inverse, out, left):
    total = total_of(pieces)
    to_copies(out, solved_flat(inverse.at[0], rhs[0] - total[:, :256]))
    left[...] = rhs[1] - total[:, 256:]


def anc_second_kernel(own, oth, values, left, inverse, out, top):
    residual = left[...]
    for half, tiles in enumerate((own, oth)):
        first = first_block(half)
        for block in range(8):
            residual = residual - nt(
                values[first + block], tiles[0, :, 256 * block : 256 * (block + 1)]
            )
    here = inverse.at[1]
    back = solved_back(here, solved_flat(here, residual).astype(F32))
    top[...] = back
    for half, tiles in enumerate((own, oth)):
        first = first_block(half)
        for block in range(8):
            out[first + block] = nn(back, tiles[0, :, 256 * block : 256 * (block + 1)]).astype(BF16)


def anc_third_kernel(pieces, lower, top, inverse, out):
    residual = lower[lax.axis_index("row")].astype(F32) - total_of(pieces)
    value = jnp.concatenate([solved_back(inverse.at[0], residual), top[...]], axis=1)
    to_copies(out, value)


def back_sums(terms, out):
    for half in range(2):
        first = first_block(half)
        for block in range(8):
            total = None
            for pair, slab, value in terms:
                term = nn(value, pair[half][slab, :, 256 * block : 256 * (block + 1)])
                total = term if total is None else total + term
            out[first + block] = packed(total.astype(BF16))


def of_layers(pieces, at):
    value = pieces[:, :, 256 * at : 256 * (at + 1)]
    return value.reshape(-1, value.shape[-1])


def back_first_kernel(slabs, own, oth, anc, out, natural):
    values = [of_layers(anc, at) for at in range(2)]
    back_sums([((own, oth), slab, value) for slab, value in zip(slabs, values)], out)
    for at in range(2):
        natural[at] = flipped(values[at]).astype(BF16)


def residual_of(value, pieces):
    own = unpacked(value[lax.axis_index("row")], TILE)
    return flipped(own) - unpacked(total_of(pieces), 256)


def back_kernel(level, cross_slabs, leaf_slabs, cown, coth, lown, loth, anc, pieces, value, inverse, *rest):
    *earlier, out, solution, natural = rest
    now = solved_back(inverse.at[level], residual_of(value, pieces))
    terms = [((cown, coth), slab, of_layers(anc, at)) for at, slab in enumerate(cross_slabs)]
    known = [now, *(e[...] for e in earlier)]
    terms += [((lown, loth), slab, x) for slab, x in zip(leaf_slabs, known)]
    back_sums(terms, out)
    solution[...] = now
    natural[...] = flipped(now).astype(BF16)


def last_kernel(pieces, value, inverse, second, third, anc, out):
    out[0] = flipped(solved_back(inverse.at[0], residual_of(value, pieces))).astype(BF16)
    out[1] = second[...]
    out[2] = third[...]
    out[3] = anc[0]
    out[4] = anc[1]


def join_kernel(mine, theirs, leaf, anc, sem):
    copies = []
    col = lax.axis_index("col")
    for at in range(5):
        for side, half in enumerate((mine, theirs)):
            columns = pl.ds(pl.multiple_of((col if side == 0 else 1 - col) * 128, 128), 128)
            target = leaf.at[0, at, :, columns] if at < 3 else anc.at[at - 3, :, columns]
            copies.append(fetch(half.at[at], target, sem.at[at, side]))
    for copy in copies:
        copy.wait()


def shape(*dims, dtype=BF16):
    return jax.ShapeDtypeStruct(dims, dtype)


def call(name, body, outs, operands, slabs=0, scratch=(), in_specs=None, out_specs=None, limit=6):
    single = not isinstance(outs, list)
    shapes = [outs] if single else outs
    made = pl.pallas_call(
        body,
        out_shape=shapes,
        in_specs=in_specs or [VMEM] * len(operands),
        out_specs=out_specs or [VMEM] * len(shapes),
        scratch_shapes=scratch,
        compiler_params=pltpu.CompilerParams(vmem_limit_bytes=limit * 1024 * 1024),
        cost_estimate=pl.CostEstimate(
            flops=max(1, slabs) * SLAB_FLOPS, bytes_accessed=2**21 * max(1, slabs), transcendentals=0
        ),
        name=name,
    )(*operands)
    return made[0] if single else made


def spread(x, axis):
    return lax.all_to_all(x, axis, split_axis=0, concat_axis=0, tiled=True)


def local(*args):
    layers = lax.axis_size("layer")
    rows = lax.axis_size("row")
    width = 128 // layers
    wide = shape(rows, LINES, 256 * 128 // LINES)
    thin = shape(rows, width, 256)
    far = pltpu.HBM
    args = tuple(
        x if x.dtype == jnp.int32 else pltpu.with_memory_space_constraint(x, far) for x in args
    )
    block, leaf, cross, top, rhs, rhs_anc, inv, inv_anc = call(
        "y0", first_kernel,
        [wide, shape(3, 256, 2048), shape(6, 256, 2048), shape(1, 256, 2048), shape(2, 256, 128, dtype=F32),
         shape(2, width, 256, dtype=F32), shape(3, 2, TILE, TILE), shape(2, 2, TILE, TILE)],
        args, 4,
        [pltpu.VMEM((256, 128), F32), pltpu.VMEM((2, 256, 128), F32), pltpu.VMEM((2, 128, 256), F32),
         pltpu.SemaphoreType.DMA((5,)), pltpu.SemaphoreType.DMA((10,))],
        in_specs=[SMEM if x.dtype == jnp.int32 else HBM for x in args], limit=16,
    )
    leaf, top, cross = ((x, lax.ppermute(x, "col", SWAP)) for x in (leaf, top, cross))
    y0 = spread(block, "row")
    block = call(
        "y1", functools.partial(forward_kernel, 1, (0,)), wide, (*leaf, rhs, inv, y0), 1
    )
    block, top = lax.optimization_barrier((block, top))
    y1 = spread(block, "row")
    block = call(
        "y2", functools.partial(forward_kernel, 2, (1, 2)), wide, (*leaf, rhs, inv, y0, y1), 2
    )
    block, cross = lax.optimization_barrier((block, cross))
    y2 = spread(block, "row")
    lower = spread(
        call("zs", cross_kernel, shape(layers, width, 512), (*cross, y0, y1, y2), 6), "layer"
    )
    z0, left = call(
        "z0", anc_first_kernel, [thin, shape(width, 256, dtype=F32)], (lower, rhs_anc, inv_anc)
    )
    z0 = spread(z0, "row")
    pieces, high = call(
        "z1", anc_second_kernel, [thin, shape(width, 256)], (*top, z0, left, inv_anc), 1
    )
    pieces = spread(pieces, "row")
    anc = call("a0", anc_third_kernel, shape(layers, width, 512), (pieces, z0, high, inv_anc))
    anc = spread(anc, "layer")
    pieces, natural = call(
        "b2", functools.partial(back_first_kernel, (2, 5)), [wide, shape(2, 256, 128)], (*cross, anc), 2
    )
    pieces = spread(pieces, "row")
    outs = [wide, shape(128, 256), shape(256, 128)]
    pieces, x2, n2 = call(
        "b1", functools.partial(back_kernel, 2, (1, 4), (2,)), outs, (*cross, *leaf, anc, pieces, y2, inv), 3
    )
    pieces = spread(pieces, "row")
    pieces, _, n1 = call(
        "b0", functools.partial(back_kernel, 1, (0, 3), (0, 1)), outs, (*cross, *leaf, anc, pieces, y1, inv, x2), 4
    )
    pieces = spread(pieces, "row")
    mine = call("x0", last_kernel, shape(5, 256, 128), (pieces, y0, inv, n1, n2, natural))
    theirs = lax.ppermute(mine, "col", SWAP)
    return tuple(
        call("join", join_kernel, [shape(1, 3, 256, 256), shape(2, 256, 256)], (mine, theirs),
             scratch=[pltpu.SemaphoreType.DMA((5, 2))], out_specs=[HBM, HBM])
    )


def solution(mesh):
    in_specs = (
        P("layer", None, "row", None),
        P(None, "row", None),
        P("layer", None, "row", "col"),
        P("layer", None, None, "row", "col"),
        P(None, "row", "col"),
        P("layer", None, "row", "col"),
        P("layer", None, None, "row", "col"),
        P(None, "row", "col"),
        P("layer", None, None, None, None),
        P(),
    )
    out_specs = (P("layer", None, "row", None), P(None, "row", None))
    return jax.shard_map(local, mesh=mesh, in_specs=in_specs, out_specs=out_specs, check_vma=False)
```

time: 218 us -> 188 us (0.86)
  Pallas kernels: 38.5 us -> 19.2 us
  waiting for transfers between devices: 10.9 us -> 1.26 us
    pallas_call x12, Pallas kernels: 38.5 us -> 19.2 us  [call(): pl.pallas_call(body, out_shape=shapes, in_specs=in_specs or [VMEM] * len(...]
    ppermute x1 -> x0, waiting for transfers between devices: 9.68 us -> none  [local(): pat_other = lax.ppermute(patterns, 'col', SWAP)]
    reshape x3 -> x0, local copies, waits for them, and re-layouts: 2.3 us -> none  [the longest x1 0.77 us: local(): cross_pattern.reshape(-1)]
  transfers between devices with their start and end apart: 5 -> 4, of which waited for: 2 -> 1; matrix products, arithmetic and copies ran while one was open for 1% -> 0% of each run, Pallas kernels for 4% -> 1%
where the time goes in v3:
time: 188 us
  blocking collectives  148 us (79%)
  Pallas kernels  19.2 us (10%)
  starting transfers between devices  16.5 us (9%)
  local copies, waits for them, and re-layouts  2.05 us (1%)
    all_to_all x10, blocking collectives, spread(): return lax.all_to_all(x, axis, split_axis=0, concat_axis=0, tiled=True)  148 us
    pallas_call x12, Pallas kernels, call(): pl.pallas_call(body, out_shape=shapes, in_specs=in_specs or [VMEM] * len(...  19.2 us
    ppermute x1, starting transfers between devices, local(): theirs = lax.ppermute(mine, 'col', SWAP)  12.7 us
    ppermute x3, starting transfers between devices, local(): lax.ppermute(x, 'col', SWAP)  3.84 us
  transfers between devices with their start and end apart: 4, of which 1 were waited for; matrix products, arithmetic and copies ran while one was open for 0% of the time, Pallas kernels for 1%

profile of v3, /device:TPU:1, one launch (start us, length us, event | category | flops | bytes accessed | tf_op | source)
XLA Modules:
  0.0 187.8 jit_solution(11222640556732090233)
XLA Ops:
  0.6 0.7 copy-done
  1.3 0.7 copy-done.1
  2.7 7.2 %y0.1 = (bf16[16,16,2048]{2,1,0:T(8,128)(2,1)S(1)}, bf16[3,256,2048]{2,1,0:T(8,128)(2,1)S(1)}, bf16[6,256,2048]{2,1,0:T(8,128)(2,1)S(1)}, bf16[1,256,2048]{2,1,0...) custom-call(f32[1,3,256,256]{3,2,1,0:T(8,128)} %leaf_rhs.1, ...), custom_call_target="tpu_custom_call" | custom-call | flops 1073741824 | bytes 8388608 | tf_op jit(solution)/shard_map/y0/pallas_call | solution.py:267
  9.9 3.3 %collective-permute-start.2 = (bf16[6,256,2048]{2,1,0:T(8,128)(2,1)S(1)}, bf16[6,256,2048]{2,1,0:T(8,128)(2,1)S(1)}, u32[]{:S(2)}, u32[]{:S(2)}) collective-permute-start(bf16[6,256,2048]{2,1,0:T(8,128)(2,1)S(1)} %get-tuple-element.34.own.cown), channel_id=1, source_target_pairs={{0,1},{1,0},{2,3},{3,2},{4,5},{5,4},{6,7},{7,6},{8,9},{9,8},{10,11... | collective-permute-start | bytes 18874376 | tf_op jit(solution)/shard_map/ppermute | solution.py:305
  13.7 21.4 %all_to_all.50.rest_0_.value = bf16[16,16,2048]{2,1,0:T(8,128)(2,1)S(1)} all-to-all(bf16[16,16,2048]{2,1,0:T(8,128)(2,1)S(1)} %get-tuple-element.30), channel_id=1, replica_groups=mesh['layer'=8,'row'=16,'col'=2] {'row'}, dimensions={0} | all-to-all | bytes 2097152 | tf_op jit(solution)/shard_map/all_to_all | solution.py:283
  35.2 0.9 y1.1
  36.1 18.9 %all_to_all.51.rest_1_.value = bf16[16,16,2048]{2,1,0:T(8,128)(2,1)S(1)} all-to-all(bf16[16,16,2048]{2,1,0:T(8,128)(2,1)S(1)} %y1.1), channel_id=1, replica_groups=mesh['layer'=8,'row'=16,'col'=2] {'row'}, dimensions={0} | all-to-all | bytes 2097152 | tf_op jit(solution)/shard_map/all_to_all | solution.py:283
  55.0 1.4 y2.1
  56.5 18.3 %all_to_all.52.rest_2_.value = bf16[16,16,2048]{2,1,0:T(8,128)(2,1)S(1)} all-to-all(bf16[16,16,2048]{2,1,0:T(8,128)(2,1)S(1)} %y2.1), channel_id=1, replica_groups=mesh['layer'=8,'row'=16,'col'=2] {'row'}, dimensions={0} | all-to-all | bytes 2097152 | tf_op jit(solution)/shard_map/all_to_all | solution.py:283
  74.8 3.5 %zs.1 = bf16[8,16,512]{2,1,0:T(8,128)(2,1)S(1)} custom-call(bf16[6,256,2048]{2,1,0:T(8,128)(2,1)S(1)} %get-tuple-element.34.own.cown, bf16[6,256,2048]{2,1,0:T(8,128)(2,1)S(1)} %collective-permute-done.2.oth.coth, bf16[16,16,2048]{2,1,0:T(8,128)(2,1)S(1)} %all_to_all.50.rest_0_.value, bf16[16,16,2048]{2,1,0:T(8,128)(2,1)S(1)} %all_to_all.51.rest_1_.value, ...), custom_call_target="tpu_custom_call" | custom-call | flops 1610612736 | bytes 12582912 | tf_op jit(solution)/shard_map/zs/pallas_call | solution.py:267
  78.3 16.0 %all_to_all.53.pieces = bf16[8,16,512]{2,1,0:T(8,128)(2,1)S(1)} all-to-all(bf16[8,16,512]{2,1,0:T(8,128)(2,1)S(1)} %zs.1), channel_id=1, replica_groups=mesh['layer'=8,'row'=16,'col'=2] {'layer'}, dimensions={0} | all-to-all | bytes 262144 | tf_op jit(solution)/shard_map/all_to_all | solution.py:283
  94.5 9.4 %all_to_all.54.values.lower = bf16[16,16,256]{2,1,0:T(8,128)(2,1)S(1)} all-to-all(bf16[16,16,256]{2,1,0:T(8,128)(2,1)S(1)} %get-tuple-element.41), channel_id=1, replica_groups=mesh['layer'=8,'row'=16,'col'=2] {'row'}, dimensions={0} | all-to-all | bytes 262144 | tf_op jit(solution)/shard_map/all_to_all | solution.py:283
  103.9 1.2 z1.1
  105.2 9.6 %all_to_all.55.pieces = bf16[16,16,256]{2,1,0:T(8,128)(2,1)S(1)} all-to-all(bf16[16,16,256]{2,1,0:T(8,128)(2,1)S(1)} %get-tuple-element.43), channel_id=1, replica_groups=mesh['layer'=8,'row'=16,'col'=2] {'row'}, dimensions={0} | all-to-all | bytes 262144 | tf_op jit(solution)/shard_map/all_to_all | solution.py:283
  115.0 10.3 %all_to_all.56.anc = bf16[8,16,512]{2,1,0:T(8,128)(2,1)S(1)} all-to-all(bf16[8,16,512]{2,1,0:T(8,128)(2,1)S(1)} %a0.1), channel_id=1, replica_groups=mesh['layer'=8,'row'=16,'col'=2] {'layer'}, dimensions={0} | all-to-all | bytes 262144 | tf_op jit(solution)/shard_map/all_to_all | solution.py:283
  125.3 0.7 b2.1
  126.0 14.6 %all_to_all.57.pieces = bf16[16,16,2048]{2,1,0:T(8,128)(2,1)S(1)} all-to-all(bf16[16,16,2048]{2,1,0:T(8,128)(2,1)S(1)} %get-tuple-element.45), channel_id=1, replica_groups=mesh['layer'=8,'row'=16,'col'=2] {'row'}, dimensions={0} | all-to-all | bytes 2097152 | tf_op jit(solution)/shard_map/all_to_all | solution.py:283
  140.6 1.2 b1.1
  141.8 14.5 %all_to_all.58.pieces = bf16[16,16,2048]{2,1,0:T(8,128)(2,1)S(1)} all-to-all(bf16[16,16,2048]{2,1,0:T(8,128)(2,1)S(1)} %get-tuple-element.46), channel_id=1, replica_groups=mesh['layer'=8,'row'=16,'col'=2] {'row'}, dimensions={0} | all-to-all | bytes 2097152 | tf_op jit(solution)/shard_map/all_to_all | solution.py:283
  156.3 1.5 b0.1
  157.8 14.7 %all_to_all.59.pieces = bf16[16,16,2048]{2,1,0:T(8,128)(2,1)S(1)} all-to-all(bf16[16,16,2048]{2,1,0:T(8,128)(2,1)S(1)} %get-tuple-element.48), channel_id=1, replica_groups=mesh['layer'=8,'row'=16,'col'=2] {'row'}, dimensions={0} | all-to-all | bytes 2097152 | tf_op jit(solution)/shard_map/all_to_all | solution.py:283
  172.8 12.7 %collective-permute-start.3 = (bf16[5,256,128]{2,1,0:T(8,128)(2,1)S(1)}, bf16[5,256,128]{2,1,0:T(8,128)(2,1)S(1)}, u32[]{:S(2)}, u32[]{:S(2)}) collective-permute-start(bf16[5,256,128]{2,1,0:T(8,128)(2,1)S(1)} %x0.1.mine), channel_id=1, source_target_pairs={{0,1},{1,0},{2,3},{3,2},{4,5},{5,4},{6,7},{7,6},{8,9},{9,8},{10,11... | collective-permute-start | bytes 983048 | tf_op jit(solution)/shard_map/ppermute | solution.py:344
  185.5 1.3 collective-permute-done.3.theirs
  186.8 0.9 join.1
  (12 shorter events, 1.9 us)
Async XLA Ops:
  0.6 0.7 copy-start
  1.3 0.7 copy-start.1
  2.0 0.7 copy-start.2
  9.9 46.6 %collective-permute-start.2 = (bf16[6,256,2048]{2,1,0:T(8,128)(2,1)S(1)}, bf16[6,256,2048]{2,1,0:T(8,128)(2,1)S(1)}, u32[]{:S(2)}, u32[]{:S(2)}) collective-permute-start(bf16[6,256,2048]{2,1,0:T(8,128)(2,1)S(1)} %get-tuple-element.34.own.cown), channel_id=1, source_target_pairs={{0,1},{1,0},{2,3},{3,2},{4,5},{5,4},{6,7},{7,6},{8,9},{9,8},{10,11... | collective-permute-start | bytes 18874376 | tf_op jit(solution)/shard_map/ppermute | solution.py:305
  13.2 21.9 %collective-permute-start = (bf16[3,256,2048]{2,1,0:T(8,128)(2,1)S(1)}, bf16[3,256,2048]{2,1,0:T(8,128)(2,1)S(1)}, u32[]{:S(2)}, u32[]{:S(2)}) collective-permute-start(bf16[3,256,2048]{2,1,0:T(8,128)(2,1)S(1)} %get-tuple-element.27.own.lown), channel_id=1, source_target_pairs={{0,1},{1,0},{2,3},{3,2},{4,5},{5,4},{6,7},{7,6},{8,9},{9,8},{10,11... | collective-permute-start | bytes 9437192 | tf_op jit(solution)/shard_map/ppermute | solution.py:305
  13.3 22.8 %collective-permute-start.1 = (bf16[1,256,2048]{2,1,0:T(8,128)(2,1)S(1)}, bf16[1,256,2048]{2,1,0:T(8,128)(2,1)S(1)}, u32[]{:S(2)}, u32[]{:S(2)}) collective-permute-start(bf16[1,256,2048]{2,1,0:T(8,128)(2,1)S(1)} %get-tuple-element.36.own), channel_id=1, source_target_pairs={{0,1},{1,0},{2,3},{3,2},{4,5},{5,4},{6,7},{7,6},{8,9},{9,8},{10,11... | collective-permute-start | bytes 3145736 | tf_op jit(solution)/shard_map/ppermute | solution.py:305
  172.8 13.9 %collective-permute-start.3 = (bf16[5,256,128]{2,1,0:T(8,128)(2,1)S(1)}, bf16[5,256,128]{2,1,0:T(8,128)(2,1)S(1)}, u32[]{:S(2)}, u32[]{:S(2)}) collective-permute-start(bf16[5,256,128]{2,1,0:T(8,128)(2,1)S(1)} %x0.1.mine), channel_id=1, source_target_pairs={{0,1},{1,0},{2,3},{3,2},{4,5},{5,4},{6,7},{7,6},{8,9},{9,8},{10,11... | collective-permute-start | bytes 983048 | tf_op jit(solution)/shard_map/ppermute | solution.py:344

commit v4 on v3

--- a/solution.py
+++ b/solution.py
@@ -12,11 +12,13 @@
 TILE = 128
 LINES = 16
 SWAP = [(0, 1), (1, 0)]
+HOLD_START, HOLD_MIDDLE = 4500, 4500
 SLAB_FLOPS = 2 * 256 * 4096 * 128
 
 VMEM = pl.BlockSpec(memory_space=pltpu.VMEM)
 SMEM = pl.BlockSpec(memory_space=pltpu.SMEM)
 HBM = pl.BlockSpec(memory_space=pltpu.HBM)
+ANY = pl.BlockSpec(memory_space=pl.ANY)
 
 
 def nt(a, b):
@@ -44,14 +46,13 @@
     return (col if half == 0 else 1 - col) * 8
 
 
+def gathered_column(values, half):
+    first = first_block(half)
+    return jnp.concatenate([unpacked(values[first + b], TILE) for b in range(8)], axis=0)
+
+
 def product(pair, slab, values):
-    total = None
-    for half in range(2):
-        first = first_block(half)
-        column = jnp.concatenate([unpacked(values[first + b], TILE) for b in range(8)], axis=0)
-        term = nn(pair[half][slab], column)
-        total = term if total is None else total + term
-    return total
+    return sum(nn(pair[half][slab], gathered_column(values, half)) for half in range(2))
 
 
 def solved(inverse, residual):
@@ -91,24 +92,34 @@
     return value.astype(F32).T
 
 
+def linger(core, nanos):
+    @pl.when(lax.axis_index("col") == core)
+    def _():
+        pl.delay(nanos)
+
+
 def fetch(source, target, sem):
     copy = pltpu.make_async_copy(source, target, sem)
     copy.start()
     return copy
 
 
-def mask_in_place(tiles, slab, pattern, at):
+def mask_in_place(tiles, slab, kept):
+    grow = lax.broadcasted_iota(jnp.int32, (16, 2048), 1) // TILE
+    grow = (grow == lax.broadcasted_iota(jnp.int32, (16, 2048), 0)).astype(BF16)
+    lines = nn((kept != 0).astype(F32).astype(BF16), grow)
     for upper in range(2):
-        for k in range(16):
-            place = (slab, pl.ds(TILE * upper, TILE), pl.ds(TILE * k, TILE))
-            tile = tiles[place]
-            tiles[place] = lax.select(pattern[(*at, upper, k)] != 0, tile, jnp.zeros_like(tile))
+        mask = jnp.broadcast_to(lines[upper : upper + 1], (LINES, 2048)).astype(BF16)
+        for k in range(TILE // LINES):
+            place = pl.ds(TILE * upper + LINES * k, LINES)
+            tiles[slab, place, :] = tiles[slab, place, :] * mask
 
 
 def first_kernel(
-    leaf_rhs, anc_rhs, leaf_tiles, cross_tiles, top_tiles, leaf_pattern, cross_pattern, top_pattern,
+    leaf_rhs, anc_rhs, leaf_tiles, cross_tiles, top_tiles, leaf_kept, cross_kept, top_kept,
     leaf_inverse, anc_inverse,
-    block, leaf, cross, top, rhs, rhs_anc, inv, inv_anc, rhs_here, anc_here, turned, sem, tile_sem,
+    block, leaf, cross, top, rhs, rhs_anc, inv, inv_anc, rhs_here, anc_here, turned,
+    leaf_pattern, cross_pattern, top_pattern, sem, tile_sem,
 ):
     row, col, layer = (lax.axis_index(axis) for axis in ("row", "col", "layer"))
     columns = pl.ds(pl.multiple_of(col * 128, 128), 128)
@@ -124,6 +135,11 @@
         for s in range(3)
     ]
     moving += [fetch(top_tiles.at[0], top.at[0], tile_sem.at[9])]
+    patterns = [
+        fetch(leaf_kept, leaf_pattern, sem.at[5]),
+        fetch(cross_kept, cross_pattern, sem.at[6]),
+        fetch(top_kept, top_pattern, sem.at[7]),
+    ]
     later = [
         fetch(leaf_rhs.at[0, pl.ds(1, 2), :, columns], rhs, sem.at[2]),
         fetch(anc_rhs.at[:, :, columns], anc_here, sem.at[3]),
@@ -132,15 +148,17 @@
     for copy in urgent:
         copy.wait()
     to_copies(block, packed(solved(inv.at[0], rhs_here[...])))
+    for copy in patterns:
+        copy.wait()
     for p in range(3):
         moving[p].wait()
-        mask_in_place(leaf, p, leaf_pattern, (0, p))
+        mask_in_place(leaf, p, leaf_pattern[0, p])
     for a in range(2):
         for s in range(3):
             moving[3 + 3 * a + s].wait()
-            mask_in_place(cross, 3 * a + s, cross_pattern, (0, a, s))
+            mask_in_place(cross, 3 * a + s, cross_pattern[0, a, s])
     moving[9].wait()
-    mask_in_place(top, 0, top_pattern, (0,))
+    mask_in_place(top, 0, top_pattern[0])
     for copy in later:
         copy.wait()
     width = rhs_anc.shape[1]
@@ -150,6 +168,11 @@
         rhs_anc[a] = turned[a, mine]
 
 
+def hold_kernel(block, out):
+    del block, out
+    linger(0, HOLD_START)
+
+
 def forward_kernel(level, slabs, own, oth, rhs, inverse, *rest):
     *values, out = rest
     residual = rhs[level - 1]
@@ -161,12 +184,15 @@
 def cross_kernel(own, oth, *rest):
     *values, out = rest
     layers, width, _ = out.shape
+    totals = [None, None]
+    for s, value in enumerate(values):
+        for half, tiles in enumerate((own, oth)):
+            column = gathered_column(value, half)
+            for a in range(2):
+                term = nn(tiles[a * len(values) + s], column)
+                totals[a] = term if totals[a] is None else totals[a] + term
     for a in range(2):
-        total = None
-        for s, value in enumerate(values):
-            term = product((own, oth), a * len(values) + s, value)
-            total = term if total is None else total + term
-        out[:, :, 256 * a : 256 * (a + 1)] = total.T.astype(BF16).reshape(layers, width, -1)
+        out[:, :, 256 * a : 256 * (a + 1)] = totals[a].T.astype(BF16).reshape(layers, width, -1)
 
 
 def anc_first_kernel(pieces, rhs, inverse, out, left):
@@ -196,6 +222,7 @@
     residual = lower[lax.axis_index("row")].astype(F32) - total_of(pieces)
     value = jnp.concatenate([solved_back(inverse.at[0], residual), top[...]], axis=1)
     to_copies(out, value)
+    linger(1, HOLD_MIDDLE)
 
 
 def back_sums(terms, out):
@@ -261,7 +288,7 @@
     return jax.ShapeDtypeStruct(dims, dtype)
 
 
-def call(name, body, outs, operands, slabs=0, scratch=(), in_specs=None, out_specs=None, limit=6):
+def call(name, body, outs, operands, slabs=0, scratch=(), in_specs=None, out_specs=None, limit=6, alias={}):
     single = not isinstance(outs, list)
     shapes = [outs] if single else outs
     made = pl.pallas_call(
@@ -270,6 +297,7 @@
         in_specs=in_specs or [VMEM] * len(operands),
         out_specs=out_specs or [VMEM] * len(shapes),
         scratch_shapes=scratch,
+        input_output_aliases=alias,
         compiler_params=pltpu.CompilerParams(vmem_limit_bytes=limit * 1024 * 1024),
         cost_estimate=pl.CostEstimate(
             flops=max(1, slabs) * SLAB_FLOPS, bytes_accessed=2**21 * max(1, slabs), transcendentals=0
@@ -290,19 +318,19 @@
     wide = shape(rows, LINES, 256 * 128 // LINES)
     thin = shape(rows, width, 256)
     far = pltpu.HBM
-    args = tuple(
-        x if x.dtype == jnp.int32 else pltpu.with_memory_space_constraint(x, far) for x in args
-    )
+    args = tuple(pltpu.with_memory_space_constraint(x, far) for x in args)
     block, leaf, cross, top, rhs, rhs_anc, inv, inv_anc = call(
         "y0", first_kernel,
         [wide, shape(3, 256, 2048), shape(6, 256, 2048), shape(1, 256, 2048), shape(2, 256, 128, dtype=F32),
          shape(2, width, 256, dtype=F32), shape(3, 2, TILE, TILE), shape(2, 2, TILE, TILE)],
         args, 4,
         [pltpu.VMEM((256, 128), F32), pltpu.VMEM((2, 256, 128), F32), pltpu.VMEM((2, 128, 256), F32),
-         pltpu.SemaphoreType.DMA((5,)), pltpu.SemaphoreType.DMA((10,))],
-        in_specs=[SMEM if x.dtype == jnp.int32 else HBM for x in args], limit=16,
+         *(pltpu.VMEM(x.shape, jnp.int32) for x in args[5:8]), pltpu.SemaphoreType.DMA((8,)),
+         pltpu.SemaphoreType.DMA((10,))],
+        in_specs=[HBM] * len(args), limit=16,
     )
     leaf, top, cross = ((x, lax.ppermute(x, "col", SWAP)) for x in (leaf, top, cross))
+    block = call("hold", hold_kernel, wide, (block,), in_specs=[ANY], out_specs=[ANY], alias={0: 0})
     y0 = spread(block, "row")
     block = call(
         "y1", functools.partial(forward_kernel, 1, (0,)), wide, (*leaf, rhs, inv, y0), 1

time: 188 us -> 180 us (0.957)
  blocking collectives: 148 us -> 141 us
  local copies, waits for them, and re-layouts: 2.05 us -> 0 us
    all_to_all x10, blocking collectives: 148 us -> 141 us  [spread(): return lax.all_to_all(x, axis, split_axis=0, concat_axis=0, tiled=True)]
    unnamed x6 -> x0, local copies, waits for them, and re-layouts: 2.05 us -> none
    pallas_call x12 -> x13, Pallas kernels: 19.2 us -> 18.1 us  [call(): pl.pallas_call(body, out_shape=shapes, in_specs=in_specs or [VMEM] * len(...]
where the time goes in v4:
time: 180 us
  blocking collectives  141 us (78%)
  Pallas kernels  18.1 us (10%)
  starting transfers between devices  17.8 us (10%)
    all_to_all x10, blocking collectives, spread(): return lax.all_to_all(x, axis, split_axis=0, concat_axis=0, tiled=True)  141 us
    pallas_call x13, Pallas kernels, call(): pl.pallas_call(body, out_shape=shapes, in_specs=in_specs or [VMEM] * len(...  18.1 us
    ppermute x1, starting transfers between devices, local(): theirs = lax.ppermute(mine, 'col', SWAP)  14 us
    ppermute x3, starting transfers between devices, local(): lax.ppermute(x, 'col', SWAP)  3.85 us
  transfers between devices with their start and end apart: 4, of which 1 were waited for; matrix products, arithmetic and copies ran while one was open for 0% of the time, Pallas kernels for 1%

profile of v4, /device:TPU:1, one launch (start us, length us, event | category | flops | bytes accessed | tf_op | source)
XLA Modules:
  0.0 179.5 jit_solution(9091944123001996707)
XLA Ops:
  0.6 6.1 %y0.1 = (bf16[16,16,2048]{2,1,0:T(8,128)(2,1)S(1)}, bf16[3,256,2048]{2,1,0:T(8,128)(2,1)S(1)}, bf16[6,256,2048]{2,1,0:T(8,128)(2,1)S(1)}, bf16[1,256,2048]{2,1,0...) custom-call(f32[1,3,256,256]{3,2,1,0:T(8,128)} %leaf_rhs.1, ...), custom_call_target="tpu_custom_call" | custom-call | flops 1073741824 | bytes 8388608 | tf_op jit(solution)/shard_map/y0/pallas_call | solution.py:294
  6.7 3.3 %collective-permute-start.2 = (bf16[6,256,2048]{2,1,0:T(8,128)(2,1)S(1)}, bf16[6,256,2048]{2,1,0:T(8,128)(2,1)S(1)}, u32[]{:S(2)}, u32[]{:S(2)}) collective-permute-start(bf16[6,256,2048]{2,1,0:T(8,128)(2,1)S(1)} %get-tuple-element.34.own.cown), channel_id=1, source_target_pairs={{0,1},{1,0},{2,3},{3,2},{4,5},{5,4},{6,7},{7,6},{8,9},{9,8},{10,11... | collective-permute-start | bytes 18874376 | tf_op jit(solution)/shard_map/ppermute | solution.py:332
  10.2 0.4 collective-permute-start.1
  10.6 17.5 %all_to_all.50.rest_0_.value = bf16[16,16,2048]{2,1,0:T(8,128)(2,1)S(1)} all-to-all(bf16[16,16,2048]{2,1,0:T(8,128)(2,1)S(1)} %hold.1), channel_id=1, replica_groups=mesh['layer'=8,'row'=16,'col'=2] {'row'}, dimensions={0} | all-to-all | bytes 2097152 | tf_op jit(solution)/shard_map/all_to_all | solution.py:311
  28.1 0.9 y1.1
  29.0 14.6 %all_to_all.51.rest_1_.value = bf16[16,16,2048]{2,1,0:T(8,128)(2,1)S(1)} all-to-all(bf16[16,16,2048]{2,1,0:T(8,128)(2,1)S(1)} %y1.1), channel_id=1, replica_groups=mesh['layer'=8,'row'=16,'col'=2] {'row'}, dimensions={0} | all-to-all | bytes 2097152 | tf_op jit(solution)/shard_map/all_to_all | solution.py:311
  43.5 1.4 y2.1
  45.0 14.5 %all_to_all.52.rest_2_.value = bf16[16,16,2048]{2,1,0:T(8,128)(2,1)S(1)} all-to-all(bf16[16,16,2048]{2,1,0:T(8,128)(2,1)S(1)} %y2.1), channel_id=1, replica_groups=mesh['layer'=8,'row'=16,'col'=2] {'row'}, dimensions={0} | all-to-all | bytes 2097152 | tf_op jit(solution)/shard_map/all_to_all | solution.py:311
  59.5 3.5 %zs.1 = bf16[8,16,512]{2,1,0:T(8,128)(2,1)S(1)} custom-call(bf16[6,256,2048]{2,1,0:T(8,128)(2,1)S(1)} %get-tuple-element.34.own.cown, bf16[6,256,2048]{2,1,0:T(8,128)(2,1)S(1)} %collective-permute-done.2.oth.coth, bf16[16,16,2048]{2,1,0:T(8,128)(2,1)S(1)} %all_to_all.50.rest_0_.value, bf16[16,16,2048]{2,1,0:T(8,128)(2,1)S(1)} %all_to_all.51.rest_1_.value, ...), custom_call_target="tpu_custom_call" | custom-call | flops 1610612736 | bytes 12582912 | tf_op jit(solution)/shard_map/zs/pallas_call | solution.py:294
  63.0 15.9 %all_to_all.53.pieces = bf16[8,16,512]{2,1,0:T(8,128)(2,1)S(1)} all-to-all(bf16[8,16,512]{2,1,0:T(8,128)(2,1)S(1)} %zs.1), channel_id=1, replica_groups=mesh['layer'=8,'row'=16,'col'=2] {'layer'}, dimensions={0} | all-to-all | bytes 262144 | tf_op jit(solution)/shard_map/all_to_all | solution.py:311
  79.1 9.4 %all_to_all.54.values.lower = bf16[16,16,256]{2,1,0:T(8,128)(2,1)S(1)} all-to-all(bf16[16,16,256]{2,1,0:T(8,128)(2,1)S(1)} %get-tuple-element.41), channel_id=1, replica_groups=mesh['layer'=8,'row'=16,'col'=2] {'row'}, dimensions={0} | all-to-all | bytes 262144 | tf_op jit(solution)/shard_map/all_to_all | solution.py:311
  88.5 1.2 z1.1
  89.8 10.0 %all_to_all.55.pieces = bf16[16,16,256]{2,1,0:T(8,128)(2,1)S(1)} all-to-all(bf16[16,16,256]{2,1,0:T(8,128)(2,1)S(1)} %get-tuple-element.43), channel_id=1, replica_groups=mesh['layer'=8,'row'=16,'col'=2] {'row'}, dimensions={0} | all-to-all | bytes 262144 | tf_op jit(solution)/shard_map/all_to_all | solution.py:311
  99.9 14.8 %all_to_all.56.anc = bf16[8,16,512]{2,1,0:T(8,128)(2,1)S(1)} all-to-all(bf16[8,16,512]{2,1,0:T(8,128)(2,1)S(1)} %a0.1), channel_id=1, replica_groups=mesh['layer'=8,'row'=16,'col'=2] {'layer'}, dimensions={0} | all-to-all | bytes 262144 | tf_op jit(solution)/shard_map/all_to_all | solution.py:311
  114.7 0.7 b2.1
  115.4 14.6 %all_to_all.57.pieces = bf16[16,16,2048]{2,1,0:T(8,128)(2,1)S(1)} all-to-all(bf16[16,16,2048]{2,1,0:T(8,128)(2,1)S(1)} %get-tuple-element.45), channel_id=1, replica_groups=mesh['layer'=8,'row'=16,'col'=2] {'row'}, dimensions={0} | all-to-all | bytes 2097152 | tf_op jit(solution)/shard_map/all_to_all | solution.py:311
  130.0 1.2 b1.1
  131.2 14.4 %all_to_all.58.pieces = bf16[16,16,2048]{2,1,0:T(8,128)(2,1)S(1)} all-to-all(bf16[16,16,2048]{2,1,0:T(8,128)(2,1)S(1)} %get-tuple-element.46), channel_id=1, replica_groups=mesh['layer'=8,'row'=16,'col'=2] {'row'}, dimensions={0} | all-to-all | bytes 2097152 | tf_op jit(solution)/shard_map/all_to_all | solution.py:311
  145.7 1.5 b0.1
  147.1 15.8 %all_to_all.59.pieces = bf16[16,16,2048]{2,1,0:T(8,128)(2,1)S(1)} all-to-all(bf16[16,16,2048]{2,1,0:T(8,128)(2,1)S(1)} %get-tuple-element.48), channel_id=1, replica_groups=mesh['layer'=8,'row'=16,'col'=2] {'row'}, dimensions={0} | all-to-all | bytes 2097152 | tf_op jit(solution)/shard_map/all_to_all | solution.py:311
  162.9 0.4 x0.1.mine
  163.3 14.0 %collective-permute-start.3 = (bf16[5,256,128]{2,1,0:T(8,128)(2,1)S(1)}, bf16[5,256,128]{2,1,0:T(8,128)(2,1)S(1)}, u32[]{:S(2)}, u32[]{:S(2)}) collective-permute-start(bf16[5,256,128]{2,1,0:T(8,128)(2,1)S(1)} %x0.1.mine), channel_id=1, source_target_pairs={{0,1},{1,0},{2,3},{3,2},{4,5},{5,4},{6,7},{7,6},{8,9},{9,8},{10,11... | collective-permute-start | bytes 983048 | tf_op jit(solution)/shard_map/ppermute | solution.py:372
  177.2 1.3 collective-permute-done.3.theirs
  178.5 0.9 join.1
  (7 shorter events, 0.4 us)
Async XLA Ops:
  6.7 38.2 %collective-permute-start.2 = (bf16[6,256,2048]{2,1,0:T(8,128)(2,1)S(1)}, bf16[6,256,2048]{2,1,0:T(8,128)(2,1)S(1)}, u32[]{:S(2)}, u32[]{:S(2)}) collective-permute-start(bf16[6,256,2048]{2,1,0:T(8,128)(2,1)S(1)} %get-tuple-element.34.own.cown), channel_id=1, source_target_pairs={{0,1},{1,0},{2,3},{3,2},{4,5},{5,4},{6,7},{7,6},{8,9},{9,8},{10,11... | collective-permute-start | bytes 18874376 | tf_op jit(solution)/shard_map/ppermute | solution.py:332
  10.1 18.0 %collective-permute-start = (bf16[3,256,2048]{2,1,0:T(8,128)(2,1)S(1)}, bf16[3,256,2048]{2,1,0:T(8,128)(2,1)S(1)}, u32[]{:S(2)}, u32[]{:S(2)}) collective-permute-start(bf16[3,256,2048]{2,1,0:T(8,128)(2,1)S(1)} %get-tuple-element.27.own.lown), channel_id=1, source_target_pairs={{0,1},{1,0},{2,3},{3,2},{4,5},{5,4},{6,7},{7,6},{8,9},{9,8},{10,11... | collective-permute-start | bytes 9437192 | tf_op jit(solution)/shard_map/ppermute | solution.py:332
  10.2 18.8 %collective-permute-start.1 = (bf16[1,256,2048]{2,1,0:T(8,128)(2,1)S(1)}, bf16[1,256,2048]{2,1,0:T(8,128)(2,1)S(1)}, u32[]{:S(2)}, u32[]{:S(2)}) collective-permute-start(bf16[1,256,2048]{2,1,0:T(8,128)(2,1)S(1)} %get-tuple-element.36.own), channel_id=1, source_target_pairs={{0,1},{1,0},{2,3},{3,2},{4,5},{5,4},{6,7},{7,6},{8,9},{9,8},{10,11... | collective-permute-start | bytes 3145736 | tf_op jit(solution)/shard_map/ppermute | solution.py:332
  163.3 15.2 %collective-permute-start.3 = (bf16[5,256,128]{2,1,0:T(8,128)(2,1)S(1)}, bf16[5,256,128]{2,1,0:T(8,128)(2,1)S(1)}, u32[]{:S(2)}, u32[]{:S(2)}) collective-permute-start(bf16[5,256,128]{2,1,0:T(8,128)(2,1)S(1)} %x0.1.mine), channel_id=1, source_target_pairs={{0,1},{1,0},{2,3},{3,2},{4,5},{5,4},{6,7},{7,6},{8,9},{9,8},{10,11... | collective-permute-start | bytes 983048 | tf_op jit(solution)/shard_map/ppermute | solution.py:372

commit v5 on v4

--- a/solution.py
+++ b/solution.py
@@ -12,7 +12,7 @@
 TILE = 128
 LINES = 16
 SWAP = [(0, 1), (1, 0)]
-HOLD_START, HOLD_MIDDLE = 4500, 4500
+HOLD_START, HOLD_MIDDLE = 9500, 4000
 SLAB_FLOPS = 2 * 256 * 4096 * 128
 
 VMEM = pl.BlockSpec(memory_space=pltpu.VMEM)
@@ -104,12 +104,18 @@
     return copy
 
 
-def mask_in_place(tiles, slab, kept):
+def grow_masks(patterns, masks):
     grow = lax.broadcasted_iota(jnp.int32, (16, 2048), 1) // TILE
     grow = (grow == lax.broadcasted_iota(jnp.int32, (16, 2048), 0)).astype(BF16)
-    lines = nn((kept != 0).astype(F32).astype(BF16), grow)
+    for p in range(patterns.shape[0]):
+        lines = nn((patterns[p] != 0).astype(F32).astype(BF16), grow)
+        for upper in range(2):
+            masks[p, upper] = jnp.broadcast_to(lines[upper : upper + 1], (LINES, 2048)).astype(BF16)
+
+
+def mask_in_place(tiles, slab, masks, at):
     for upper in range(2):
-        mask = jnp.broadcast_to(lines[upper : upper + 1], (LINES, 2048)).astype(BF16)
+        mask = masks[at, upper]
         for k in range(TILE // LINES):
             place = pl.ds(TILE * upper + LINES * k, LINES)
             tiles[slab, place, :] = tiles[slab, place, :] * mask
@@ -119,11 +125,17 @@
     leaf_rhs, anc_rhs, leaf_tiles, cross_tiles, top_tiles, leaf_kept, cross_kept, top_kept,
     leaf_inverse, anc_inverse,
     block, leaf, cross, top, rhs, rhs_anc, inv, inv_anc, rhs_here, anc_here, turned,
-    leaf_pattern, cross_pattern, top_pattern, sem, tile_sem,
+    patterns, masks, sem, tile_sem,
 ):
     row, col, layer = (lax.axis_index(axis) for axis in ("row", "col", "layer"))
     columns = pl.ds(pl.multiple_of(col * 128, 128), 128)
     two = pl.ds(2 * row, 2)
+    kept = [
+        fetch(leaf_kept.at[0], patterns.at[pl.ds(0, 3)], sem.at[5]),
+        fetch(cross_kept.at[0, 0], patterns.at[pl.ds(3, 3)], sem.at[6]),
+        fetch(cross_kept.at[0, 1], patterns.at[pl.ds(6, 3)], sem.at[7]),
+        fetch(top_kept, patterns.at[pl.ds(9, 1)], sem.at[8]),
+    ]
     urgent = [
         fetch(leaf_rhs.at[0, 0, :, columns], rhs_here, sem.at[0]),
         fetch(leaf_inverse.at[0, :, two], inv, sem.at[1]),
@@ -135,30 +147,19 @@
         for s in range(3)
     ]
     moving += [fetch(top_tiles.at[0], top.at[0], tile_sem.at[9])]
-    patterns = [
-        fetch(leaf_kept, leaf_pattern, sem.at[5]),
-        fetch(cross_kept, cross_pattern, sem.at[6]),
-        fetch(top_kept, top_pattern, sem.at[7]),
-    ]
     later = [
         fetch(leaf_rhs.at[0, pl.ds(1, 2), :, columns], rhs, sem.at[2]),
         fetch(anc_rhs.at[:, :, columns], anc_here, sem.at[3]),
         fetch(anc_inverse.at[:, two], inv_anc, sem.at[4]),
     ]
-    for copy in urgent:
+    for copy in (*kept, *urgent):
         copy.wait()
+    grow_masks(patterns, masks)
     to_copies(block, packed(solved(inv.at[0], rhs_here[...])))
-    for copy in patterns:
+    places = [(leaf, p) for p in range(3)] + [(cross, p) for p in range(6)] + [(top, 0)]
+    for at, (copy, (tiles, slab)) in enumerate(zip(moving, places)):
         copy.wait()
-    for p in range(3):
-        moving[p].wait()
-        mask_in_place(leaf, p, leaf_pattern[0, p])
-    for a in range(2):
-        for s in range(3):
-            moving[3 + 3 * a + s].wait()
-            mask_in_place(cross, 3 * a + s, cross_pattern[0, a, s])
-    moving[9].wait()
-    mask_in_place(top, 0, top_pattern[0])
+        mask_in_place(tiles, slab, masks, at)
     for copy in later:
         copy.wait()
     width = rhs_anc.shape[1]
@@ -170,7 +171,7 @@
 
 def hold_kernel(block, out):
     del block, out
-    linger(0, HOLD_START)
+    linger(1, HOLD_START)
 
 
 def forward_kernel(level, slabs, own, oth, rhs, inverse, *rest):
@@ -222,7 +223,7 @@
     residual = lower[lax.axis_index("row")].astype(F32) - total_of(pieces)
     value = jnp.concatenate([solved_back(inverse.at[0], residual), top[...]], axis=1)
     to_copies(out, value)
-    linger(1, HOLD_MIDDLE)
+    linger(0, HOLD_MIDDLE)
 
 
 def back_sums(terms, out):
@@ -325,7 +326,7 @@
          shape(2, width, 256, dtype=F32), shape(3, 2, TILE, TILE), shape(2, 2, TILE, TILE)],
         args, 4,
         [pltpu.VMEM((256, 128), F32), pltpu.VMEM((2, 256, 128), F32), pltpu.VMEM((2, 128, 256), F32),
-         *(pltpu.VMEM(x.shape, jnp.int32) for x in args[5:8]), pltpu.SemaphoreType.DMA((8,)),
+         pltpu.VMEM((10, 2, 16), jnp.int32), pltpu.VMEM((10, 2, LINES, 2048), BF16), pltpu.SemaphoreType.DMA((9,)),
          pltpu.SemaphoreType.DMA((10,))],
         in_specs=[HBM] * len(args), limit=16,
     )

time: 180 us -> 177 us (0.983)
  starting transfers between devices: 17.8 us -> 11.6 us
  blocking collectives: 141 us -> 146 us
    ppermute x1, starting transfers between devices: 14 us -> 7.79 us  [local(): theirs = lax.ppermute(mine, 'col', SWAP)]
    all_to_all x10, blocking collectives: 141 us -> 146 us  [spread(): return lax.all_to_all(x, axis, split_axis=0, concat_axis=0, tiled=True)]
where the time goes in v5:
time: 177 us; the launch traced here: 176 us
  blocking collectives  146 us (82%)
  Pallas kernels  17 us (10%)
  starting transfers between devices  11.6 us (7%)
    all_to_all x10, blocking collectives, spread(): return lax.all_to_all(x, axis, split_axis=0, concat_axis=0, tiled=True)  146 us
    pallas_call x13, Pallas kernels, call(): pl.pallas_call(body, out_shape=shapes, in_specs=in_specs or [VMEM] * len(...  17 us
    ppermute x1, starting transfers between devices, local(): theirs = lax.ppermute(mine, 'col', SWAP)  7.79 us
    ppermute x3, starting transfers between devices, local(): lax.ppermute(x, 'col', SWAP)  3.8 us
  transfers between devices with their start and end apart: 4, of which 1 were waited for; matrix products, arithmetic and copies ran while one was open for 0% of the time, Pallas kernels for 1%

profile of v5, /device:TPU:1, one launch (start us, length us, event | category | flops | bytes accessed | tf_op | source)
XLA Modules:
  0.0 176.4 jit_solution(4701591625453823154)
XLA Ops:
  0.6 5.0 %y0.1 = (bf16[16,16,2048]{2,1,0:T(8,128)(2,1)S(1)}, bf16[3,256,2048]{2,1,0:T(8,128)(2,1)S(1)}, bf16[6,256,2048]{2,1,0:T(8,128)(2,1)S(1)}, bf16[1,256,2048]{2,1,0...) custom-call(f32[1,3,256,256]{3,2,1,0:T(8,128)} %leaf_rhs.1, ...), custom_call_target="tpu_custom_call" | custom-call | flops 1073741824 | bytes 8388608 | tf_op jit(solution)/shard_map/y0/pallas_call | solution.py:295
  5.6 3.3 %collective-permute-start.2 = (bf16[6,256,2048]{2,1,0:T(8,128)(2,1)S(1)}, bf16[6,256,2048]{2,1,0:T(8,128)(2,1)S(1)}, u32[]{:S(2)}, u32[]{:S(2)}) collective-permute-start(bf16[6,256,2048]{2,1,0:T(8,128)(2,1)S(1)} %get-tuple-element.34.own.cown), channel_id=1, source_target_pairs={{0,1},{1,0},{2,3},{3,2},{4,5},{5,4},{6,7},{7,6},{8,9},{9,8},{10,11... | collective-permute-start | bytes 18874376 | tf_op jit(solution)/shard_map/ppermute | solution.py:333
  9.0 0.4 collective-permute-start.1
  9.4 26.2 %all_to_all.50.rest_0_.value = bf16[16,16,2048]{2,1,0:T(8,128)(2,1)S(1)} all-to-all(bf16[16,16,2048]{2,1,0:T(8,128)(2,1)S(1)} %hold.1), channel_id=1, replica_groups=mesh['layer'=8,'row'=16,'col'=2] {'row'}, dimensions={0} | all-to-all | bytes 2097152 | tf_op jit(solution)/shard_map/all_to_all | solution.py:312
  35.6 0.9 y1.1
  36.5 14.5 %all_to_all.51.rest_1_.value = bf16[16,16,2048]{2,1,0:T(8,128)(2,1)S(1)} all-to-all(bf16[16,16,2048]{2,1,0:T(8,128)(2,1)S(1)} %y1.1), channel_id=1, replica_groups=mesh['layer'=8,'row'=16,'col'=2] {'row'}, dimensions={0} | all-to-all | bytes 2097152 | tf_op jit(solution)/shard_map/all_to_all | solution.py:312
  51.0 1.4 y2.1
  52.4 14.4 %all_to_all.52.rest_2_.value = bf16[16,16,2048]{2,1,0:T(8,128)(2,1)S(1)} all-to-all(bf16[16,16,2048]{2,1,0:T(8,128)(2,1)S(1)} %y2.1), channel_id=1, replica_groups=mesh['layer'=8,'row'=16,'col'=2] {'row'}, dimensions={0} | all-to-all | bytes 2097152 | tf_op jit(solution)/shard_map/all_to_all | solution.py:312
  66.9 3.5 %zs.1 = bf16[8,16,512]{2,1,0:T(8,128)(2,1)S(1)} custom-call(bf16[6,256,2048]{2,1,0:T(8,128)(2,1)S(1)} %get-tuple-element.34.own.cown, bf16[6,256,2048]{2,1,0:T(8,128)(2,1)S(1)} %collective-permute-done.2.oth.coth, bf16[16,16,2048]{2,1,0:T(8,128)(2,1)S(1)} %all_to_all.50.rest_0_.value, bf16[16,16,2048]{2,1,0:T(8,128)(2,1)S(1)} %all_to_all.51.rest_1_.value, ...), custom_call_target="tpu_custom_call" | custom-call | flops 1610612736 | bytes 12582912 | tf_op jit(solution)/shard_map/zs/pallas_call | solution.py:295
  70.4 15.9 %all_to_all.53.pieces = bf16[8,16,512]{2,1,0:T(8,128)(2,1)S(1)} all-to-all(bf16[8,16,512]{2,1,0:T(8,128)(2,1)S(1)} %zs.1), channel_id=1, replica_groups=mesh['layer'=8,'row'=16,'col'=2] {'layer'}, dimensions={0} | all-to-all | bytes 262144 | tf_op jit(solution)/shard_map/all_to_all | solution.py:312
  86.5 9.6 %all_to_all.54.values.lower = bf16[16,16,256]{2,1,0:T(8,128)(2,1)S(1)} all-to-all(bf16[16,16,256]{2,1,0:T(8,128)(2,1)S(1)} %get-tuple-element.41), channel_id=1, replica_groups=mesh['layer'=8,'row'=16,'col'=2] {'row'}, dimensions={0} | all-to-all | bytes 262144 | tf_op jit(solution)/shard_map/all_to_all | solution.py:312
  96.0 1.2 z1.1
  97.3 9.6 %all_to_all.55.pieces = bf16[16,16,256]{2,1,0:T(8,128)(2,1)S(1)} all-to-all(bf16[16,16,256]{2,1,0:T(8,128)(2,1)S(1)} %get-tuple-element.43), channel_id=1, replica_groups=mesh['layer'=8,'row'=16,'col'=2] {'row'}, dimensions={0} | all-to-all | bytes 262144 | tf_op jit(solution)/shard_map/all_to_all | solution.py:312
  107.1 10.4 %all_to_all.56.anc = bf16[8,16,512]{2,1,0:T(8,128)(2,1)S(1)} all-to-all(bf16[8,16,512]{2,1,0:T(8,128)(2,1)S(1)} %a0.1), channel_id=1, replica_groups=mesh['layer'=8,'row'=16,'col'=2] {'layer'}, dimensions={0} | all-to-all | bytes 262144 | tf_op jit(solution)/shard_map/all_to_all | solution.py:312
  117.5 0.7 b2.1
  118.2 15.7 %all_to_all.57.pieces = bf16[16,16,2048]{2,1,0:T(8,128)(2,1)S(1)} all-to-all(bf16[16,16,2048]{2,1,0:T(8,128)(2,1)S(1)} %get-tuple-element.45), channel_id=1, replica_groups=mesh['layer'=8,'row'=16,'col'=2] {'row'}, dimensions={0} | all-to-all | bytes 2097152 | tf_op jit(solution)/shard_map/all_to_all | solution.py:312
  133.9 1.2 b1.1
  135.1 14.7 %all_to_all.58.pieces = bf16[16,16,2048]{2,1,0:T(8,128)(2,1)S(1)} all-to-all(bf16[16,16,2048]{2,1,0:T(8,128)(2,1)S(1)} %get-tuple-element.46), channel_id=1, replica_groups=mesh['layer'=8,'row'=16,'col'=2] {'row'}, dimensions={0} | all-to-all | bytes 2097152 | tf_op jit(solution)/shard_map/all_to_all | solution.py:312
  149.8 1.5 b0.1
  151.3 14.7 %all_to_all.59.pieces = bf16[16,16,2048]{2,1,0:T(8,128)(2,1)S(1)} all-to-all(bf16[16,16,2048]{2,1,0:T(8,128)(2,1)S(1)} %get-tuple-element.48), channel_id=1, replica_groups=mesh['layer'=8,'row'=16,'col'=2] {'row'}, dimensions={0} | all-to-all | bytes 2097152 | tf_op jit(solution)/shard_map/all_to_all | solution.py:312
  165.9 0.4 x0.1.mine
  166.3 7.8 %collective-permute-start.3 = (bf16[5,256,128]{2,1,0:T(8,128)(2,1)S(1)}, bf16[5,256,128]{2,1,0:T(8,128)(2,1)S(1)}, u32[]{:S(2)}, u32[]{:S(2)}) collective-permute-start(bf16[5,256,128]{2,1,0:T(8,128)(2,1)S(1)} %x0.1.mine), channel_id=1, source_target_pairs={{0,1},{1,0},{2,3},{3,2},{4,5},{5,4},{6,7},{7,6},{8,9},{9,8},{10,11... | collective-permute-start | bytes 983048 | tf_op jit(solution)/shard_map/ppermute | solution.py:373
  174.1 1.3 collective-permute-done.3.theirs
  175.4 0.9 join.1
  (7 shorter events, 0.4 us)
Async XLA Ops:
  5.6 46.8 %collective-permute-start.2 = (bf16[6,256,2048]{2,1,0:T(8,128)(2,1)S(1)}, bf16[6,256,2048]{2,1,0:T(8,128)(2,1)S(1)}, u32[]{:S(2)}, u32[]{:S(2)}) collective-permute-start(bf16[6,256,2048]{2,1,0:T(8,128)(2,1)S(1)} %get-tuple-element.34.own.cown), channel_id=1, source_target_pairs={{0,1},{1,0},{2,3},{3,2},{4,5},{5,4},{6,7},{7,6},{8,9},{9,8},{10,11... | collective-permute-start | bytes 18874376 | tf_op jit(solution)/shard_map/ppermute | solution.py:333
  8.9 26.7 %collective-permute-start = (bf16[3,256,2048]{2,1,0:T(8,128)(2,1)S(1)}, bf16[3,256,2048]{2,1,0:T(8,128)(2,1)S(1)}, u32[]{:S(2)}, u32[]{:S(2)}) collective-permute-start(bf16[3,256,2048]{2,1,0:T(8,128)(2,1)S(1)} %get-tuple-element.27.own.lown), channel_id=1, source_target_pairs={{0,1},{1,0},{2,3},{3,2},{4,5},{5,4},{6,7},{7,6},{8,9},{9,8},{10,11... | collective-permute-start | bytes 9437192 | tf_op jit(solution)/shard_map/ppermute | solution.py:333
  9.0 27.5 %collective-permute-start.1 = (bf16[1,256,2048]{2,1,0:T(8,128)(2,1)S(1)}, bf16[1,256,2048]{2,1,0:T(8,128)(2,1)S(1)}, u32[]{:S(2)}, u32[]{:S(2)}) collective-permute-start(bf16[1,256,2048]{2,1,0:T(8,128)(2,1)S(1)} %get-tuple-element.36.own), channel_id=1, source_target_pairs={{0,1},{1,0},{2,3},{3,2},{4,5},{5,4},{6,7},{7,6},{8,9},{9,8},{10,11... | collective-permute-start | bytes 3145736 | tf_op jit(solution)/shard_map/ppermute | solution.py:333
  166.3 9.0 %collective-permute-start.3 = (bf16[5,256,128]{2,1,0:T(8,128)(2,1)S(1)}, bf16[5,256,128]{2,1,0:T(8,128)(2,1)S(1)}, u32[]{:S(2)}, u32[]{:S(2)}) collective-permute-start(bf16[5,256,128]{2,1,0:T(8,128)(2,1)S(1)} %x0.1.mine), channel_id=1, source_target_pairs={{0,1},{1,0},{2,3},{3,2},{4,5},{5,4},{6,7},{7,6},{8,9},{9,8},{10,11... | collective-permute-start | bytes 983048 | tf_op jit(solution)/shard_map/ppermute | solution.py:373

commit v6 on v5

--- a/solution.py
+++ b/solution.py
@@ -11,6 +11,7 @@
 BF16 = jnp.bfloat16
 TILE = 128
 LINES = 16
+CROSS, TOP = 3, 9
 SWAP = [(0, 1), (1, 0)]
 HOLD_START, HOLD_MIDDLE = 9500, 4000
 SLAB_FLOPS = 2 * 256 * 4096 * 128
@@ -113,9 +114,9 @@
             masks[p, upper] = jnp.broadcast_to(lines[upper : upper + 1], (LINES, 2048)).astype(BF16)
 
 
-def mask_in_place(tiles, slab, masks, at):
+def mask_in_place(tiles, slab, masks):
     for upper in range(2):
-        mask = masks[at, upper]
+        mask = masks[slab, upper]
         for k in range(TILE // LINES):
             place = pl.ds(TILE * upper + LINES * k, LINES)
             tiles[slab, place, :] = tiles[slab, place, :] * mask
@@ -124,7 +125,7 @@
 def first_kernel(
     leaf_rhs, anc_rhs, leaf_tiles, cross_tiles, top_tiles, leaf_kept, cross_kept, top_kept,
     leaf_inverse, anc_inverse,
-    block, leaf, cross, top, rhs, rhs_anc, inv, inv_anc, rhs_here, anc_here, turned,
+    block, tiles, rhs, rhs_anc, inv, inv_anc, rhs_here, anc_here, turned,
     patterns, masks, sem, tile_sem,
 ):
     row, col, layer = (lax.axis_index(axis) for axis in ("row", "col", "layer"))
@@ -140,13 +141,12 @@
         fetch(leaf_rhs.at[0, 0, :, columns], rhs_here, sem.at[0]),
         fetch(leaf_inverse.at[0, :, two], inv, sem.at[1]),
     ]
-    moving = [fetch(leaf_tiles.at[0, p], leaf.at[p], tile_sem.at[p]) for p in range(3)]
-    moving += [
-        fetch(cross_tiles.at[0, a, s], cross.at[3 * a + s], tile_sem.at[3 + 3 * a + s])
-        for a in range(2)
-        for s in range(3)
+    moving = [
+        fetch(leaf_tiles.at[0], tiles.at[pl.ds(0, 3)], tile_sem.at[0]),
+        fetch(cross_tiles.at[0, 0], tiles.at[pl.ds(CROSS, 3)], tile_sem.at[1]),
+        fetch(cross_tiles.at[0, 1], tiles.at[pl.ds(CROSS + 3, 3)], tile_sem.at[2]),
+        fetch(top_tiles, tiles.at[pl.ds(TOP, 1)], tile_sem.at[3]),
     ]
-    moving += [fetch(top_tiles.at[0], top.at[0], tile_sem.at[9])]
     later = [
         fetch(leaf_rhs.at[0, pl.ds(1, 2), :, columns], rhs, sem.at[2]),
         fetch(anc_rhs.at[:, :, columns], anc_here, sem.at[3]),
@@ -156,10 +156,10 @@
         copy.wait()
     grow_masks(patterns, masks)
     to_copies(block, packed(solved(inv.at[0], rhs_here[...])))
-    places = [(leaf, p) for p in range(3)] + [(cross, p) for p in range(6)] + [(top, 0)]
-    for at, (copy, (tiles, slab)) in enumerate(zip(moving, places)):
-        copy.wait()
-        mask_in_place(tiles, slab, masks, at)
+    for slab in range(10):
+        if slab % 3 == 0:
+            moving[slab // 3].wait()
+        mask_in_place(tiles, slab, masks)
     for copy in later:
         copy.wait()
     width = rhs_anc.shape[1]
@@ -190,7 +190,7 @@
         for half, tiles in enumerate((own, oth)):
             column = gathered_column(value, half)
             for a in range(2):
-                term = nn(tiles[a * len(values) + s], column)
+                term = nn(tiles[CROSS + a * len(values) + s], column)
                 totals[a] = term if totals[a] is None else totals[a] + term
     for a in range(2):
         out[:, :, 256 * a : 256 * (a + 1)] = totals[a].T.astype(BF16).reshape(layers, width, -1)
@@ -208,7 +208,7 @@
         first = first_block(half)
         for block in range(8):
             residual = residual - nt(
-                values[first + block], tiles[0, :, 256 * block : 256 * (block + 1)]
+                values[first + block], tiles[TOP, :, 256 * block : 256 * (block + 1)]
             )
     here = inverse.at[1]
     back = solved_back(here, solved_flat(here, residual).astype(F32))
@@ -216,7 +216,7 @@
     for half, tiles in enumerate((own, oth)):
         first = first_block(half)
         for block in range(8):
-            out[first + block] = nn(back, tiles[0, :, 256 * block : 256 * (block + 1)]).astype(BF16)
+            out[first + block] = nn(back, tiles[TOP, :, 256 * block : 256 * (block + 1)]).astype(BF16)
 
 
 def anc_third_kernel(pieces, lower, top, inverse, out):
@@ -254,12 +254,12 @@
     return flipped(own) - unpacked(total_of(pieces), 256)
 
 
-def back_kernel(level, cross_slabs, leaf_slabs, cown, coth, lown, loth, anc, pieces, value, inverse, *rest):
+def back_kernel(level, cross_slabs, leaf_slabs, own, oth, anc, pieces, value, inverse, *rest):
     *earlier, out, solution, natural = rest
     now = solved_back(inverse.at[level], residual_of(value, pieces))
-    terms = [((cown, coth), slab, of_layers(anc, at)) for at, slab in enumerate(cross_slabs)]
+    terms = [((own, oth), slab, of_layers(anc, at)) for at, slab in enumerate(cross_slabs)]
     known = [now, *(e[...] for e in earlier)]
-    terms += [((lown, loth), slab, x) for slab, x in zip(leaf_slabs, known)]
+    terms += [((own, oth), slab, x) for slab, x in zip(leaf_slabs, known)]
     back_sums(terms, out)
     solution[...] = now
     natural[...] = flipped(now).astype(BF16)
@@ -320,53 +320,51 @@
     thin = shape(rows, width, 256)
     far = pltpu.HBM
     args = tuple(pltpu.with_memory_space_constraint(x, far) for x in args)
-    block, leaf, cross, top, rhs, rhs_anc, inv, inv_anc = call(
+    block, tiles, rhs, rhs_anc, inv, inv_anc = call(
         "y0", first_kernel,
-        [wide, shape(3, 256, 2048), shape(6, 256, 2048), shape(1, 256, 2048), shape(2, 256, 128, dtype=F32),
+        [wide, shape(10, 256, 2048), shape(2, 256, 128, dtype=F32),
          shape(2, width, 256, dtype=F32), shape(3, 2, TILE, TILE), shape(2, 2, TILE, TILE)],
         args, 4,
         [pltpu.VMEM((256, 128), F32), pltpu.VMEM((2, 256, 128), F32), pltpu.VMEM((2, 128, 256), F32),
          pltpu.VMEM((10, 2, 16), jnp.int32), pltpu.VMEM((10, 2, LINES, 2048), BF16), pltpu.SemaphoreType.DMA((9,)),
-         pltpu.SemaphoreType.DMA((10,))],
+         pltpu.SemaphoreType.DMA((4,))],
         in_specs=[HBM] * len(args), limit=16,
     )
-    leaf, top, cross = ((x, lax.ppermute(x, "col", SWAP)) for x in (leaf, top, cross))
+    tiles = (tiles, lax.ppermute(tiles, "col", SWAP))
     block = call("hold", hold_kernel, wide, (block,), in_specs=[ANY], out_specs=[ANY], alias={0: 0})
     y0 = spread(block, "row")
     block = call(
-        "y1", functools.partial(forward_kernel, 1, (0,)), wide, (*leaf, rhs, inv, y0), 1
-    )
-    block, top = lax.optimization_barrier((block, top))
+        "y1", functools.partial(forward_kernel, 1, (0,)), wide, (*tiles, rhs, inv, y0), 1
+    )
     y1 = spread(block, "row")
     block = call(
-        "y2", functools.partial(forward_kernel, 2, (1, 2)), wide, (*leaf, rhs, inv, y0, y1), 2
-    )
-    block, cross = lax.optimization_barrier((block, cross))
+        "y2", functools.partial(forward_kernel, 2, (1, 2)), wide, (*tiles, rhs, inv, y0, y1), 2
+    )
     y2 = spread(block, "row")
     lower = spread(
-        call("zs", cross_kernel, shape(layers, width, 512), (*cross, y0, y1, y2), 6), "layer"
+        call("zs", cross_kernel, shape(layers, width, 512), (*tiles, y0, y1, y2), 6), "layer"
     )
     z0, left = call(
         "z0", anc_first_kernel, [thin, shape(width, 256, dtype=F32)], (lower, rhs_anc, inv_anc)
     )
     z0 = spread(z0, "row")
     pieces, high = call(
-        "z1", anc_second_kernel, [thin, shape(width, 256)], (*top, z0, left, inv_anc), 1
+        "z1", anc_second_kernel, [thin, shape(width, 256)], (*tiles, z0, left, inv_anc), 1
     )
     pieces = spread(pieces, "row")
     anc = call("a0", anc_third_kernel, shape(layers, width, 512), (pieces, z0, high, inv_anc))
     anc = spread(anc, "layer")
     pieces, natural = call(
-        "b2", functools.partial(back_first_kernel, (2, 5)), [wide, shape(2, 256, 128)], (*cross, anc), 2
+        "b2", functools.partial(back_first_kernel, (CROSS + 2, CROSS + 5)), [wide, shape(2, 256, 128)], (*tiles, anc), 2
     )
     pieces = spread(pieces, "row")
     outs = [wide, shape(128, 256), shape(256, 128)]
     pieces, x2, n2 = call(
-        "b1", functools.partial(back_kernel, 2, (1, 4), (2,)), outs, (*cross, *leaf, anc, pieces, y2, inv), 3
+        "b1", functools.partial(back_kernel, 2, (CROSS + 1, CROSS + 4), (2,)), outs, (*tiles, anc, pieces, y2, inv), 3
     )
     pieces = spread(pieces, "row")
     pieces, _, n1 = call(
-        "b0", functools.partial(back_kernel, 1, (0, 3), (0, 1)), outs, (*cross, *leaf, anc, pieces, y1, inv, x2), 4
+        "b0", functools.partial(back_kernel, 1, (CROSS, CROSS + 3), (0, 1)), outs, (*tiles, anc, pieces, y1, inv, x2), 4
     )
     pieces = spread(pieces, "row")
     mine = call("x0", last_kernel, shape(5, 256, 128), (pieces, y0, inv, n1, n2, natural))

time: 177 us -> 176 us (level)
    ppermute x3 -> x1, starting transfers between devices: 3.8 us -> 3.29 us  [local(): tiles = (tiles, lax.ppermute(tiles, 'col', SWAP))]
  transfers between devices with their start and end apart: 4 -> 2, of which waited for: 1 -> 1; matrix products, arithmetic and copies ran while one was open for 0% -> 0% of each run, Pallas kernels for 1% -> 0%
where the time goes in v6:
time: 176 us
  blocking collectives  145 us (82%)
  Pallas kernels  16.7 us (9%)
  starting transfers between devices  11.9 us (7%)
    all_to_all x10, blocking collectives, spread(): return lax.all_to_all(x, axis, split_axis=0, concat_axis=0, tiled=True)  145 us
    pallas_call x13, Pallas kernels, call(): pl.pallas_call(body, out_shape=shapes, in_specs=in_specs or [VMEM] * len(...  16.7 us
    ppermute x1, starting transfers between devices, local(): theirs = lax.ppermute(mine, 'col', SWAP)  8.65 us
  transfers between devices with their start and end apart: 2, of which 1 were waited for; matrix products, arithmetic and copies ran while one was open for 0% of the time, Pallas kernels for 0%

profile of v6, /device:TPU:1, one launch (start us, length us, event | category | flops | bytes accessed | tf_op | source)
XLA Modules:
  0.0 175.5 jit_solution(1076422904260717402)
XLA Ops:
  0.6 4.6 %y0.1 = (bf16[16,16,2048]{2,1,0:T(8,128)(2,1)S(1)}, bf16[10,256,2048]{2,1,0:T(8,128)(2,1)S(1)}, f32[2,256,128]{2,1,0:T(8,128)S(1)}, f32[2,16,256]{2,1,0:T(8,128)...) custom-call(f32[1,3,256,256]{3,2,1,0:T(8,128)} %leaf_rhs.1, f32[2,256,256]{2,1,0:T(8,128)} %anc_rhs.1, ...), custom_call_target="tpu_custom_call" | custom-call | flops 1073741824 | bytes 8388608 | tf_op jit(solution)/shard_map/y0/pallas_call | solution.py:295
  5.3 3.3 %collective-permute-start = (bf16[10,256,2048]{2,1,0:T(8,128)(2,1)S(1)}, bf16[10,256,2048]{2,1,0:T(8,128)(2,1)S(1)}, u32[]{:S(2)}, u32[]{:S(2)}) collective-permute-start(bf16[10,256,2048]{2,1,0:T(8,128)(2,1)S(1)} %get-tuple-element.19.own), channel_id=1, source_target_pairs={{0,1},{1,0},{2,3},{3,2},{4,5},{5,4},{6,7},{7,6},{8,9},{9,8},{10,11... | collective-permute-start | bytes 31457288 | tf_op jit(solution)/shard_map/ppermute | solution.py:333
  8.6 26.2 %all_to_all.50.rest_0_.value = bf16[16,16,2048]{2,1,0:T(8,128)(2,1)S(1)} all-to-all(bf16[16,16,2048]{2,1,0:T(8,128)(2,1)S(1)} %hold.1), channel_id=1, replica_groups=mesh['layer'=8,'row'=16,'col'=2] {'row'}, dimensions={0} | all-to-all | bytes 2097152 | tf_op jit(solution)/shard_map/all_to_all | solution.py:312
  34.8 0.9 y1.1
  35.7 14.5 %all_to_all.51.rest_1_.value = bf16[16,16,2048]{2,1,0:T(8,128)(2,1)S(1)} all-to-all(bf16[16,16,2048]{2,1,0:T(8,128)(2,1)S(1)} %y1.1), channel_id=1, replica_groups=mesh['layer'=8,'row'=16,'col'=2] {'row'}, dimensions={0} | all-to-all | bytes 2097152 | tf_op jit(solution)/shard_map/all_to_all | solution.py:312
  50.1 1.5 y2.1
  51.6 14.6 %all_to_all.52.rest_2_.value = bf16[16,16,2048]{2,1,0:T(8,128)(2,1)S(1)} all-to-all(bf16[16,16,2048]{2,1,0:T(8,128)(2,1)S(1)} %y2.1), channel_id=1, replica_groups=mesh['layer'=8,'row'=16,'col'=2] {'row'}, dimensions={0} | all-to-all | bytes 2097152 | tf_op jit(solution)/shard_map/all_to_all | solution.py:312
  66.1 3.5 %zs.1 = bf16[8,16,512]{2,1,0:T(8,128)(2,1)S(1)} custom-call(bf16[10,256,2048]{2,1,0:T(8,128)(2,1)S(1)} %get-tuple-element.19.own, bf16[10,256,2048]{2,1,0:T(8,128)(2,1)S(1)} %collective-permute-done.oth, bf16[16,16,2048]{2,1,0:T(8,128)(2,1)S(1)} %all_to_all.50.rest_0_.value, bf16[16,16,2048]{2,1,0:T(8,128)(2,1)S(1)} %all_to_all.51.rest_1_.value, ...), custom_call_target="tpu_custom_call" | custom-call | flops 1610612736 | bytes 12582912 | tf_op jit(solution)/shard_map/zs/pallas_call | solution.py:295
  69.7 15.9 %all_to_all.53.pieces = bf16[8,16,512]{2,1,0:T(8,128)(2,1)S(1)} all-to-all(bf16[8,16,512]{2,1,0:T(8,128)(2,1)S(1)} %zs.1), channel_id=1, replica_groups=mesh['layer'=8,'row'=16,'col'=2] {'layer'}, dimensions={0} | all-to-all | bytes 262144 | tf_op jit(solution)/shard_map/all_to_all | solution.py:312
  85.6 0.2 z0.1
  85.8 9.4 %all_to_all.54.values.lower = bf16[16,16,256]{2,1,0:T(8,128)(2,1)S(1)} all-to-all(bf16[16,16,256]{2,1,0:T(8,128)(2,1)S(1)} %get-tuple-element.25), channel_id=1, replica_groups=mesh['layer'=8,'row'=16,'col'=2] {'row'}, dimensions={0} | all-to-all | bytes 262144 | tf_op jit(solution)/shard_map/all_to_all | solution.py:312
  95.2 1.2 z1.1
  96.4 9.6 %all_to_all.55.pieces = bf16[16,16,256]{2,1,0:T(8,128)(2,1)S(1)} all-to-all(bf16[16,16,256]{2,1,0:T(8,128)(2,1)S(1)} %get-tuple-element.27), channel_id=1, replica_groups=mesh['layer'=8,'row'=16,'col'=2] {'row'}, dimensions={0} | all-to-all | bytes 262144 | tf_op jit(solution)/shard_map/all_to_all | solution.py:312
  106.2 10.3 %all_to_all.56.anc = bf16[8,16,512]{2,1,0:T(8,128)(2,1)S(1)} all-to-all(bf16[8,16,512]{2,1,0:T(8,128)(2,1)S(1)} %a0.1), channel_id=1, replica_groups=mesh['layer'=8,'row'=16,'col'=2] {'layer'}, dimensions={0} | all-to-all | bytes 262144 | tf_op jit(solution)/shard_map/all_to_all | solution.py:312
  116.5 0.7 b2.1
  117.3 15.2 %all_to_all.57.pieces = bf16[16,16,2048]{2,1,0:T(8,128)(2,1)S(1)} all-to-all(bf16[16,16,2048]{2,1,0:T(8,128)(2,1)S(1)} %get-tuple-element.29), channel_id=1, replica_groups=mesh['layer'=8,'row'=16,'col'=2] {'row'}, dimensions={0} | all-to-all | bytes 2097152 | tf_op jit(solution)/shard_map/all_to_all | solution.py:312
  132.4 1.2 b1.1
  133.6 14.6 %all_to_all.58.pieces = bf16[16,16,2048]{2,1,0:T(8,128)(2,1)S(1)} all-to-all(bf16[16,16,2048]{2,1,0:T(8,128)(2,1)S(1)} %get-tuple-element.30), channel_id=1, replica_groups=mesh['layer'=8,'row'=16,'col'=2] {'row'}, dimensions={0} | all-to-all | bytes 2097152 | tf_op jit(solution)/shard_map/all_to_all | solution.py:312
  148.2 1.5 b0.1
  149.7 14.5 %all_to_all.59.pieces = bf16[16,16,2048]{2,1,0:T(8,128)(2,1)S(1)} all-to-all(bf16[16,16,2048]{2,1,0:T(8,128)(2,1)S(1)} %get-tuple-element.32), channel_id=1, replica_groups=mesh['layer'=8,'row'=16,'col'=2] {'row'}, dimensions={0} | all-to-all | bytes 2097152 | tf_op jit(solution)/shard_map/all_to_all | solution.py:312
  164.2 0.4 x0.1.mine
  164.5 8.6 %collective-permute-start.1 = (bf16[5,256,128]{2,1,0:T(8,128)(2,1)S(1)}, bf16[5,256,128]{2,1,0:T(8,128)(2,1)S(1)}, u32[]{:S(2)}, u32[]{:S(2)}) collective-permute-start(bf16[5,256,128]{2,1,0:T(8,128)(2,1)S(1)} %x0.1.mine), channel_id=1, source_target_pairs={{0,1},{1,0},{2,3},{3,2},{4,5},{5,4},{6,7},{7,6},{8,9},{9,8},{10,11... | collective-permute-start | bytes 983048 | tf_op jit(solution)/shard_map/ppermute | solution.py:371
  173.2 1.3 collective-permute-done.1.theirs
  174.4 0.9 join.1
  (3 shorter events, 0.2 us)
Async XLA Ops:
  5.3 29.5 %collective-permute-start = (bf16[10,256,2048]{2,1,0:T(8,128)(2,1)S(1)}, bf16[10,256,2048]{2,1,0:T(8,128)(2,1)S(1)}, u32[]{:S(2)}, u32[]{:S(2)}) collective-permute-start(bf16[10,256,2048]{2,1,0:T(8,128)(2,1)S(1)} %get-tuple-element.19.own), channel_id=1, source_target_pairs={{0,1},{1,0},{2,3},{3,2},{4,5},{5,4},{6,7},{7,6},{8,9},{9,8},{10,11... | collective-permute-start | bytes 31457288 | tf_op jit(solution)/shard_map/ppermute | solution.py:333
  164.5 9.9 %collective-permute-start.1 = (bf16[5,256,128]{2,1,0:T(8,128)(2,1)S(1)}, bf16[5,256,128]{2,1,0:T(8,128)(2,1)S(1)}, u32[]{:S(2)}, u32[]{:S(2)}) collective-permute-start(bf16[5,256,128]{2,1,0:T(8,128)(2,1)S(1)} %x0.1.mine), channel_id=1, source_target_pairs={{0,1},{1,0},{2,3},{3,2},{4,5},{5,4},{6,7},{7,6},{8,9},{9,8},{10,11... | collective-permute-start | bytes 983048 | tf_op jit(solution)/shard_map/ppermute | solution.py:371

commit v7 on v6

--- a/solution.py
+++ b/solution.py
@@ -13,7 +13,7 @@
 LINES = 16
 CROSS, TOP = 3, 9
 SWAP = [(0, 1), (1, 0)]
-HOLD_START, HOLD_MIDDLE = 9500, 4000
+HOLD_START, HOLD_MIDDLE = 9500, 3800
 SLAB_FLOPS = 2 * 256 * 4096 * 128
 
 VMEM = pl.BlockSpec(memory_space=pltpu.VMEM)
@@ -152,9 +152,11 @@
         fetch(anc_rhs.at[:, :, columns], anc_here, sem.at[3]),
         fetch(anc_inverse.at[:, two], inv_anc, sem.at[4]),
     ]
-    for copy in (*kept, *urgent):
+    for copy in kept:
         copy.wait()
     grow_masks(patterns, masks)
+    for copy in urgent:
+        copy.wait()
     to_copies(block, packed(solved(inv.at[0], rhs_here[...])))
     for slab in range(10):
         if slab % 3 == 0:
@@ -219,10 +221,12 @@
             out[first + block] = nn(back, tiles[TOP, :, 256 * block : 256 * (block + 1)]).astype(BF16)
 
 
-def anc_third_kernel(pieces, lower, top, inverse, out):
+def anc_third_kernel(pieces, lower, top, inverse, y0, y1, y2, out, turned):
     residual = lower[lax.axis_index("row")].astype(F32) - total_of(pieces)
     value = jnp.concatenate([solved_back(inverse.at[0], residual), top[...]], axis=1)
     to_copies(out, value)
+    for level, value in enumerate((y0, y1, y2)):
+        turned[level] = flipped(unpacked(value[lax.axis_index("row")], TILE))
     linger(0, HOLD_MIDDLE)
 
 
@@ -250,13 +254,12 @@
 
 
 def residual_of(value, pieces):
-    own = unpacked(value[lax.axis_index("row")], TILE)
-    return flipped(own) - unpacked(total_of(pieces), 256)
+    return value - unpacked(total_of(pieces), 256)
 
 
 def back_kernel(level, cross_slabs, leaf_slabs, own, oth, anc, pieces, value, inverse, *rest):
     *earlier, out, solution, natural = rest
-    now = solved_back(inverse.at[level], residual_of(value, pieces))
+    now = solved_back(inverse.at[level], residual_of(value[level], pieces))
     terms = [((own, oth), slab, of_layers(anc, at)) for at, slab in enumerate(cross_slabs)]
     known = [now, *(e[...] for e in earlier)]
     terms += [((own, oth), slab, x) for slab, x in zip(leaf_slabs, known)]
@@ -266,7 +269,7 @@
 
 
 def last_kernel(pieces, value, inverse, second, third, anc, out):
-    out[0] = flipped(solved_back(inverse.at[0], residual_of(value, pieces))).astype(BF16)
+    out[0] = flipped(solved_back(inverse.at[0], residual_of(value[0], pieces))).astype(BF16)
     out[1] = second[...]
     out[2] = third[...]
     out[3] = anc[0]
@@ -352,7 +355,10 @@
         "z1", anc_second_kernel, [thin, shape(width, 256)], (*tiles, z0, left, inv_anc), 1
     )
     pieces = spread(pieces, "row")
-    anc = call("a0", anc_third_kernel, shape(layers, width, 512), (pieces, z0, high, inv_anc))
+    anc, turned = call(
+        "a0", anc_third_kernel, [shape(layers, width, 512), shape(3, 128, 256, dtype=F32)],
+        (pieces, z0, high, inv_anc, y0, y1, y2),
+    )
     anc = spread(anc, "layer")
     pieces, natural = call(
         "b2", functools.partial(back_first_kernel, (CROSS + 2, CROSS + 5)), [wide, shape(2, 256, 128)], (*tiles, anc), 2
@@ -360,14 +366,14 @@
     pieces = spread(pieces, "row")
     outs = [wide, shape(128, 256), shape(256, 128)]
     pieces, x2, n2 = call(
-        "b1", functools.partial(back_kernel, 2, (CROSS + 1, CROSS + 4), (2,)), outs, (*tiles, anc, pieces, y2, inv), 3
+        "b1", functools.partial(back_kernel, 2, (CROSS + 1, CROSS + 4), (2,)), outs, (*tiles, anc, pieces, turned, inv), 3
     )
     pieces = spread(pieces, "row")
     pieces, _, n1 = call(
-        "b0", functools.partial(back_kernel, 1, (CROSS, CROSS + 3), (0, 1)), outs, (*tiles, anc, pieces, y1, inv, x2), 4
+        "b0", functools.partial(back_kernel, 1, (CROSS, CROSS + 3), (0, 1)), outs, (*tiles, anc, pieces, turned, inv, x2), 4
     )
     pieces = spread(pieces, "row")
-    mine = call("x0", last_kernel, shape(5, 256, 128), (pieces, y0, inv, n1, n2, natural))
+    mine = call("x0", last_kernel, shape(5, 256, 128), (pieces, turned, inv, n1, n2, natural))
     theirs = lax.ppermute(mine, "col", SWAP)
     return tuple(
         call("join", join_kernel, [shape(1, 3, 256, 256), shape(2, 256, 256)], (mine, theirs),

time: 176 us -> 176 us (level)
  no operation moved by 1% of the time
where the time goes in v7:
time: 176 us
  blocking collectives  146 us (83%)
  Pallas kernels  16.6 us (9%)
  starting transfers between devices  10.8 us (6%)
    all_to_all x10, blocking collectives, spread(): return lax.all_to_all(x, axis, split_axis=0, concat_axis=0, tiled=True)  146 us
    pallas_call x13, Pallas kernels, call(): pl.pallas_call(body, out_shape=shapes, in_specs=in_specs or [VMEM] * len(...  16.6 us
    ppermute x1, starting transfers between devices, local(): theirs = lax.ppermute(mine, 'col', SWAP)  7.54 us
  transfers between devices with their start and end apart: 2, of which 1 were waited for; matrix products, arithmetic and copies ran while one was open for 0% of the time, Pallas kernels for 0%

profile of v7, /device:TPU:1, one launch (start us, length us, event | category | flops | bytes accessed | tf_op | source)
XLA Modules:
  0.0 175.5 jit_solution(871478589474010523)
XLA Ops:
  0.6 4.6 %y0.1 = (bf16[16,16,2048]{2,1,0:T(8,128)(2,1)S(1)}, bf16[10,256,2048]{2,1,0:T(8,128)(2,1)S(1)}, f32[2,256,128]{2,1,0:T(8,128)S(1)}, f32[2,16,256]{2,1,0:T(8,128)...) custom-call(f32[1,3,256,256]{3,2,1,0:T(8,128)} %leaf_rhs.1, f32[2,256,256]{2,1,0:T(8,128)} %anc_rhs.1, ...), custom_call_target="tpu_custom_call" | custom-call | flops 1073741824 | bytes 8388608 | tf_op jit(solution)/shard_map/y0/pallas_call | solution.py:298
  5.3 3.3 %collective-permute-start = (bf16[10,256,2048]{2,1,0:T(8,128)(2,1)S(1)}, bf16[10,256,2048]{2,1,0:T(8,128)(2,1)S(1)}, u32[]{:S(2)}, u32[]{:S(2)}) collective-permute-start(bf16[10,256,2048]{2,1,0:T(8,128)(2,1)S(1)} %get-tuple-element.21.own), channel_id=1, source_target_pairs={{0,1},{1,0},{2,3},{3,2},{4,5},{5,4},{6,7},{7,6},{8,9},{9,8},{10,11... | collective-permute-start | bytes 31457288 | tf_op jit(solution)/shard_map/ppermute | solution.py:336
  8.6 26.2 %all_to_all.50.rest_0_.y0 = bf16[16,16,2048]{2,1,0:T(8,128)(2,1)S(1)} all-to-all(bf16[16,16,2048]{2,1,0:T(8,128)(2,1)S(1)} %hold.1), channel_id=1, replica_groups=mesh['layer'=8,'row'=16,'col'=2] {'row'}, dimensions={0} | all-to-all | bytes 2097152 | tf_op jit(solution)/shard_map/all_to_all | solution.py:315
  34.8 0.9 y1.1
  35.7 14.5 %all_to_all.51.rest_1_.y1 = bf16[16,16,2048]{2,1,0:T(8,128)(2,1)S(1)} all-to-all(bf16[16,16,2048]{2,1,0:T(8,128)(2,1)S(1)} %y1.1), channel_id=1, replica_groups=mesh['layer'=8,'row'=16,'col'=2] {'row'}, dimensions={0} | all-to-all | bytes 2097152 | tf_op jit(solution)/shard_map/all_to_all | solution.py:315
  50.1 1.5 y2.1
  51.6 14.6 %all_to_all.52.rest_2_.y2 = bf16[16,16,2048]{2,1,0:T(8,128)(2,1)S(1)} all-to-all(bf16[16,16,2048]{2,1,0:T(8,128)(2,1)S(1)} %y2.1), channel_id=1, replica_groups=mesh['layer'=8,'row'=16,'col'=2] {'row'}, dimensions={0} | all-to-all | bytes 2097152 | tf_op jit(solution)/shard_map/all_to_all | solution.py:315
  66.2 3.5 %zs.1 = bf16[8,16,512]{2,1,0:T(8,128)(2,1)S(1)} custom-call(bf16[10,256,2048]{2,1,0:T(8,128)(2,1)S(1)} %get-tuple-element.21.own, bf16[10,256,2048]{2,1,0:T(8,128)(2,1)S(1)} %collective-permute-done.oth, bf16[16,16,2048]{2,1,0:T(8,128)(2,1)S(1)} %all_to_all.50.rest_0_.y0, bf16[16,16,2048]{2,1,0:T(8,128)(2,1)S(1)} %all_to_all.51.rest_1_.y1, ...), custom_call_target="tpu_custom_call" | custom-call | flops 1610612736 | bytes 12582912 | tf_op jit(solution)/shard_map/zs/pallas_call | solution.py:298
  69.7 15.9 %all_to_all.53.pieces = bf16[8,16,512]{2,1,0:T(8,128)(2,1)S(1)} all-to-all(bf16[8,16,512]{2,1,0:T(8,128)(2,1)S(1)} %zs.1), channel_id=1, replica_groups=mesh['layer'=8,'row'=16,'col'=2] {'layer'}, dimensions={0} | all-to-all | bytes 262144 | tf_op jit(solution)/shard_map/all_to_all | solution.py:315
  85.8 9.4 %all_to_all.54.values.lower = bf16[16,16,256]{2,1,0:T(8,128)(2,1)S(1)} all-to-all(bf16[16,16,256]{2,1,0:T(8,128)(2,1)S(1)} %get-tuple-element.27), channel_id=1, replica_groups=mesh['layer'=8,'row'=16,'col'=2] {'row'}, dimensions={0} | all-to-all | bytes 262144 | tf_op jit(solution)/shard_map/all_to_all | solution.py:315
  95.2 1.2 z1.1
  96.5 9.6 %all_to_all.55.pieces = bf16[16,16,256]{2,1,0:T(8,128)(2,1)S(1)} all-to-all(bf16[16,16,256]{2,1,0:T(8,128)(2,1)S(1)} %get-tuple-element.29), channel_id=1, replica_groups=mesh['layer'=8,'row'=16,'col'=2] {'row'}, dimensions={0} | all-to-all | bytes 262144 | tf_op jit(solution)/shard_map/all_to_all | solution.py:315
  106.1 0.2 a0.1
  106.3 10.4 %all_to_all.56.anc = bf16[8,16,512]{2,1,0:T(8,128)(2,1)S(1)} all-to-all(bf16[8,16,512]{2,1,0:T(8,128)(2,1)S(1)} %get-tuple-element.31), channel_id=1, replica_groups=mesh['layer'=8,'row'=16,'col'=2] {'layer'}, dimensions={0} | all-to-all | bytes 262144 | tf_op jit(solution)/shard_map/all_to_all | solution.py:315
  116.7 0.7 b2.1
  117.4 15.7 %all_to_all.57.pieces = bf16[16,16,2048]{2,1,0:T(8,128)(2,1)S(1)} all-to-all(bf16[16,16,2048]{2,1,0:T(8,128)(2,1)S(1)} %get-tuple-element.32), channel_id=1, replica_groups=mesh['layer'=8,'row'=16,'col'=2] {'row'}, dimensions={0} | all-to-all | bytes 2097152 | tf_op jit(solution)/shard_map/all_to_all | solution.py:315
  133.1 1.1 b1.1
  134.2 15.1 %all_to_all.58.pieces = bf16[16,16,2048]{2,1,0:T(8,128)(2,1)S(1)} all-to-all(bf16[16,16,2048]{2,1,0:T(8,128)(2,1)S(1)} %get-tuple-element.34), channel_id=1, replica_groups=mesh['layer'=8,'row'=16,'col'=2] {'row'}, dimensions={0} | all-to-all | bytes 2097152 | tf_op jit(solution)/shard_map/all_to_all | solution.py:315
  149.3 1.4 b0.1
  150.8 14.6 %all_to_all.59.pieces = bf16[16,16,2048]{2,1,0:T(8,128)(2,1)S(1)} all-to-all(bf16[16,16,2048]{2,1,0:T(8,128)(2,1)S(1)} %get-tuple-element.36), channel_id=1, replica_groups=mesh['layer'=8,'row'=16,'col'=2] {'row'}, dimensions={0} | all-to-all | bytes 2097152 | tf_op jit(solution)/shard_map/all_to_all | solution.py:315
  165.3 0.3 x0.1.mine
  165.7 7.5 %collective-permute-start.1 = (bf16[5,256,128]{2,1,0:T(8,128)(2,1)S(1)}, bf16[5,256,128]{2,1,0:T(8,128)(2,1)S(1)}, u32[]{:S(2)}, u32[]{:S(2)}) collective-permute-start(bf16[5,256,128]{2,1,0:T(8,128)(2,1)S(1)} %x0.1.mine), channel_id=1, source_target_pairs={{0,1},{1,0},{2,3},{3,2},{4,5},{5,4},{6,7},{7,6},{8,9},{9,8},{10,11... | collective-permute-start | bytes 983048 | tf_op jit(solution)/shard_map/ppermute | solution.py:377
  173.2 1.3 collective-permute-done.1.theirs
  174.4 0.9 join.1
  (3 shorter events, 0.2 us)
Async XLA Ops:
  5.3 29.5 %collective-permute-start = (bf16[10,256,2048]{2,1,0:T(8,128)(2,1)S(1)}, bf16[10,256,2048]{2,1,0:T(8,128)(2,1)S(1)}, u32[]{:S(2)}, u32[]{:S(2)}) collective-permute-start(bf16[10,256,2048]{2,1,0:T(8,128)(2,1)S(1)} %get-tuple-element.21.own), channel_id=1, source_target_pairs={{0,1},{1,0},{2,3},{3,2},{4,5},{5,4},{6,7},{7,6},{8,9},{9,8},{10,11... | collective-permute-start | bytes 31457288 | tf_op jit(solution)/shard_map/ppermute | solution.py:336
  165.7 8.8 %collective-permute-start.1 = (bf16[5,256,128]{2,1,0:T(8,128)(2,1)S(1)}, bf16[5,256,128]{2,1,0:T(8,128)(2,1)S(1)}, u32[]{:S(2)}, u32[]{:S(2)}) collective-permute-start(bf16[5,256,128]{2,1,0:T(8,128)(2,1)S(1)} %x0.1.mine), channel_id=1, source_target_pairs={{0,1},{1,0},{2,3},{3,2},{4,5},{5,4},{6,7},{7,6},{8,9},{9,8},{10,11... | collective-permute-start | bytes 983048 | tf_op jit(solution)/shard_map/ppermute | solution.py:377
